TPU v7x, 512 devices: a whole 4x8x8 slice. The times are simulated.
512 devices in a mesh: ctx: 64 (over z_hi, y, core), exp: 8 (over x, z_lo).
Axes of the slice: x: 4, y: 8, z: 8 (z_hi: 4, z_lo: 2; z = z_hi * 2 + z_lo), core: 2. Of those that a mesh axis runs over, the one named last changes fastest.
Arguments:
- queries: bfloat16 [4096, 16, 128], P(('exp', 'ctx')), may hold values from -6 to 6
- key_heads: bfloat16 [4096, 8, 128], P('ctx', 'exp'), may hold values from -6 to 6
- value_heads: bfloat16 [4096, 8, 128], P('ctx', 'exp'), may hold values from -6 to 6
- expert_ids: int32 [4096, 16], P(('exp', 'ctx')), may hold values from 0 to 63, all different within a row; in each aligned block of 8 rows (0 to 7, 8 to 15, ...) at most 3 rows name the same one
- gate_logits: float32 [4096, 16], P(('exp', 'ctx')), may hold values from -4 to 4
- out_weight: bfloat16 [64, 128, 8192], P('exp', None, 'ctx'), may hold values from -0.5 to 0.5
Outputs:
- mixed_out: bfloat16 [4096, 8192], P('exp', 'ctx')
Inputs may be any that keep to these rules, and one draw needn't show every extreme that they name: `expert_ids`: each token names 16 different experts; among the 8 tokens of an aligned block no expert is named by more than 3 tokens, a bound that some block reaches.
All inputs are finite; a program needn't handle non-finite values.
Results may differ from a plain program's by a relative error of at most 0.018.
Values may be sent and summed in bfloat16 or wider, within the bound.
No kernel may reach another device: no remote copies, remote signals or barrier semaphores. Data moves between devices by JAX's collectives and lax.ppermute only.
A program may use at most 64 MiB of HBM per device.

v0:
```python
import math

import jax
import jax.numpy as jnp
from jax import lax
from jax.experimental import pallas as pl
from jax.experimental.pallas import tpu as pltpu
from jax.sharding import Mesh, PartitionSpec as P


EXPERTS = 64
HD = 128
TOP = 16
MOST = 3
TOK = 8
ROWS = TOK * TOP
GROUPS = 8
PER = EXPERTS // GROUPS
SLOTS = 32
SPAN = 64
CHIPS = 32
KVROWS = 2 * SPAN + 8
NEG_FLOOR = -1e30


f32 = jnp.float32
bf16 = jnp.bfloat16
NT = (((1,), (1,)), ((), ()))


def iota(shape, dim):
    return lax.broadcasted_iota(jnp.int32, shape, dim)


def prep_kernel(q_ref, k_ref, v_ref, ids_ref, logit_ref, qsend_ref, kvsend_ref, back_ref):
    spread = (iota((TOP, ROWS), 1) % TOP == iota((TOP, ROWS), 0)).astype(f32)
    own = iota((TOK, ROWS), 1) // TOP == iota((TOK, ROWS), 0)

    def as_row(table):
        wide = jnp.dot(table, spread, precision=lax.Precision.HIGHEST, preferred_element_type=f32)
        return jnp.sum(jnp.where(own, wide, 0.0), axis=0, keepdims=True)

    id_row = as_row(ids_ref[...].astype(f32))
    gate_exp = jnp.exp(logit_ref[...])
    gate_row = as_row(gate_exp / jnp.sum(gate_exp, axis=1, keepdims=True))
    id_int = id_row.astype(jnp.int32)
    id_col = jnp.broadcast_to(id_row, (ROWS, ROWS)).T
    earlier = (id_col == id_row) & (iota((ROWS, ROWS), 0) < iota((ROWS, ROWS), 1))
    rank = jnp.sum(earlier.astype(f32), axis=0, keepdims=True).astype(jnp.int32)
    slot = (id_int // PER) * SLOTS + (id_int % PER) * MOST + rank
    placed = (iota((GROUPS * SLOTS, ROWS), 0) == slot).astype(bf16)
    rows = jnp.dot(placed, q_ref[...], preferred_element_type=f32)
    tag_at = iota((8, ROWS), 0)
    tags = jnp.where(tag_at == 0, (iota((8, ROWS), 1) // TOP).astype(f32), 0.0)
    tags = jnp.where(tag_at == 1, gate_row, tags).astype(bf16)
    for g in range(GROUPS):
        here = (iota((ROWS, ROWS), 0) == slot - g * SLOTS).astype(bf16)
        info = lax.dot_general(tags, here, NT, preferred_element_type=f32)
        qsend_ref[g] = jnp.concatenate(
            [rows[g * SLOTS : g * SLOTS + PER * MOST], info], axis=0
        ).astype(bf16)
    slot_col = jnp.broadcast_to(slot.astype(f32), (ROWS, ROWS)).T.astype(jnp.int32)
    lane = iota((ROWS, ROWS), 1)
    back_ref[:, :ROWS] = (lane == slot_col).astype(bf16)
    back_ref[:, ROWS:] = (lane + ROWS == slot_col).astype(bf16)
    keys = k_ref[...]
    values = v_ref[...]
    ids = jnp.broadcast_to(id_row, (8, ROWS)).astype(bf16)

    def fill(i, _):
        kvsend_ref[i, 0:SPAN] = keys
        kvsend_ref[i, SPAN : 2 * SPAN] = values
        kvsend_ref[i, 2 * SPAN : KVROWS] = ids
        return 0

    lax.fori_loop(0, CHIPS, fill, 0)


def attend_kernel(at_ref, q_ref, kva_ref, kvb_ref, out_ref, s_ref):
    n = GROUPS * SLOTS
    step = 4
    width = step * SPAN
    steps = CHIPS // step
    queries = q_ref[...].reshape(n, HD)
    ctx = at_ref[0]
    core = at_ref[1]
    tags = jnp.concatenate(
        [q_ref[g, PER * MOST : SLOTS].astype(f32) for g in range(GROUPS)], axis=0
    )
    tags = jnp.concatenate([tags, tags], axis=0).T[0:SLOTS]
    token = jnp.concatenate([tags[:, g * 8 : g * 8 + 1] for g in range(GROUPS)], axis=0)
    gate = jnp.concatenate([tags[:, g * 8 + 1 : g * 8 + 2] for g in range(GROUPS)], axis=0)
    source = iota((n, 1), 0) // SLOTS
    pos = (source * (2 * CHIPS) + ctx) * TOK + token.astype(jnp.int32)
    scale = HD ** (-0.5) * math.log2(math.e)
    lane = iota((1, width), 1)

    def score(i, best, kv_ref, parity, base):
        keys = kv_ref[pl.ds(i * step, step), 0:SPAN, :].reshape(width, HD)
        scores = lax.dot_general(queries, keys, NT, preferred_element_type=f32) * scale
        key_pos = (2 * (i * step + lane // SPAN) + parity) * SPAN + lane % SPAN
        scores = jnp.where(key_pos <= pos, scores, NEG_FLOOR)
        s_ref[base + i] = scores
        return jnp.maximum(best, jnp.maximum(scores[:, :HD], scores[:, HD:]))

    def score_both(i, best):
        best = score(i, best, kva_ref, core, 0)
        return score(i, best, kvb_ref, 1 - core, steps)

    best = lax.fori_loop(0, steps, score_both, jnp.full((n, HD), NEG_FLOOR, f32))
    best = jnp.max(best, axis=1, keepdims=True)

    def weigh(i, carried, kv_ref, base):
        total, acc = carried
        exps = jnp.exp2(s_ref[base + i] - best)
        values = kv_ref[pl.ds(i * step, step), SPAN : 2 * SPAN, :].reshape(width, HD)
        acc = acc + jnp.dot(exps.astype(bf16), values, preferred_element_type=f32)
        return total + exps[:, :HD] + exps[:, HD:], acc

    def weigh_both(i, carried):
        return weigh(i, weigh(i, carried, kva_ref, 0), kvb_ref, steps)

    zero = jnp.zeros((n, HD), f32)
    total, acc = lax.fori_loop(0, steps, weigh_both, (zero, zero))
    total = jnp.sum(total, axis=1, keepdims=True)
    out_ref[...] = (gate * (acc / total)).astype(bf16).reshape(GROUPS, SLOTS, HD)


def compact_kernel(back_ref, got_ref, out_ref):
    rows = jnp.dot(
        back_ref[...], got_ref[...].reshape(GROUPS * SLOTS, HD), preferred_element_type=f32
    ).astype(bf16)

    def fill(i, _):
        out_ref[i] = rows
        return 0

    lax.fori_loop(0, CHIPS, fill, 0)


def project_kernel(at_ref, rows_ref, kv_ref, *refs):
    w_refs = refs[:8]
    mine_ref, other_ref, a_ref = refs[8:]
    x = at_ref[0]
    zl = at_ref[1]
    token = iota((1, ROWS), 1) // TOP
    target_at = iota((EXPERTS * TOK, ROWS), 0)

    def spread(i):
        ids = kv_ref[i, 2 * SPAN : KVROWS, :].astype(f32)[0:1].astype(jnp.int32)
        group = ids // PER
        piece = ((x - group // 2 + 4) % 4) * 2 + (group % 2 + zl) % 2
        target = (piece * PER + ids % PER) * TOK + token
        hot = (target_at == target).astype(bf16)
        got = jnp.dot(hot, rows_ref[i], preferred_element_type=f32)
        return got.reshape(EXPERTS, TOK, HD)

    def fill(i, _):
        both = jnp.concatenate([spread(2 * i), spread(2 * i + 1)], axis=1).astype(bf16)
        at = pl.ds(pl.multiple_of(i * 2 * TOK, 2 * TOK), 2 * TOK)
        for e in range(EXPERTS):
            a_ref[e // PER, at, (e % PER) * HD : (e % PER + 1) * HD] = both[e]
        return 0

    lax.fori_loop(0, CHIPS // 2, fill, 0)

    def product(half):
        total = None
        for piece in range(GROUPS):
            ref = w_refs[4 * half + piece // 2]
            weight = ref[piece % 2 * PER : (piece % 2 + 1) * PER].reshape(PER * HD, HD)
            term = jnp.dot(a_ref[piece], weight, preferred_element_type=f32)
            total = term if total is None else total + term
        return total

    mine_ref[...] = product(0).astype(bf16)
    other_ref[...] = product(1).astype(bf16)


SMEM = pl.BlockSpec(memory_space=pltpu.SMEM)
VMEM = pl.BlockSpec(memory_space=pltpu.VMEM)


def shifted(x, axis, count, by):
    return lax.ppermute(x, axis, [(i, (i + by) % count) for i in range(count)])


def run(queries, key_heads, value_heads, expert_ids, gate_logits, out_weight):
    zh, y, core = lax.axis_index("zh"), lax.axis_index("y"), lax.axis_index("core")
    x, zl = lax.axis_index("x"), lax.axis_index("zl")
    ctx = (zh * 8 + y) * 2 + core
    at = jnp.stack([ctx, core]).astype(jnp.int32)
    at_exp = jnp.stack([x, zl, core]).astype(jnp.int32)
    shape = jax.ShapeDtypeStruct
    qsend, kvsend, back = pl.pallas_call(
        prep_kernel,
        in_specs=[VMEM] * 5,
        out_specs=[VMEM] * 3,
        out_shape=[
            shape((GROUPS, SLOTS, HD), bf16),
            shape((CHIPS, KVROWS, HD), bf16),
            shape((ROWS, GROUPS * SLOTS), bf16),
        ],
        name="prep",
    )(
        queries.reshape(ROWS, HD),
        key_heads.reshape(SPAN, HD),
        value_heads.reshape(SPAN, HD),
        expert_ids,
        gate_logits,
    )
    qgot = lax.all_to_all(qsend, ("x", "zl"), 0, 0, tiled=True)
    kva = lax.all_to_all(kvsend, ("zh", "y"), 0, 0, tiled=True)
    near = shifted(out_weight, "zl", 2, 1)
    pair = jnp.concatenate([out_weight, near], axis=0)
    pieces = [pair]
    for k in range(1, 4):
        pieces.append(shifted(pair, "x", 4, k))
    far = []
    for k in range(4):
        far.append(shifted(pieces[k], "core", 2, 1))
    kvb = shifted(kva, "core", 2, 1)
    attended = pl.pallas_call(
        attend_kernel,
        in_specs=[SMEM, VMEM, VMEM, VMEM],
        out_specs=VMEM,
        out_shape=shape((GROUPS, SLOTS, HD), bf16),
        scratch_shapes=[pltpu.VMEM((16, GROUPS * SLOTS, 4 * SPAN), f32)],
        name="attend",
    )(at, qgot, kva, kvb)
    home = lax.all_to_all(attended, ("x", "zl"), 0, 0, tiled=True)
    rows = pl.pallas_call(
        compact_kernel,
        in_specs=[VMEM, VMEM],
        out_specs=VMEM,
        out_shape=shape((CHIPS, ROWS, HD), bf16),
        name="compact",
    )(back, home)
    rows = lax.all_to_all(rows, ("zh", "y"), 0, 0, tiled=True)
    mine, other = pl.pallas_call(
        project_kernel,
        in_specs=[SMEM] + [VMEM] * 10,
        out_specs=[VMEM, VMEM],
        out_shape=[shape((CHIPS * TOK, HD), bf16)] * 2,
        scratch_shapes=[pltpu.VMEM((GROUPS, CHIPS * TOK, PER * HD), bf16)],
        name="project",
    )(at_exp, rows, kva, *pieces, *far)
    got = shifted(other, "core", 2, 1)
    mine = mine.reshape(CHIPS, 1, TOK, HD)
    got = got.reshape(CHIPS, 1, TOK, HD)
    first = jnp.where(core == 0, mine, got)
    second = jnp.where(core == 0, got, mine)
    return jnp.concatenate([first, second], axis=1).reshape(2 * CHIPS * TOK, HD)


def solution(mesh):
    fine = Mesh(mesh.devices.reshape(4, 8, 2, 4, 2), ("zh", "y", "core", "x", "zl"))
    ctx, exp = ("zh", "y", "core"), ("x", "zl")
    in_specs = (
        P(exp + ctx, None, None),
        P(ctx, exp, None),
        P(ctx, exp, None),
        P(exp + ctx, None),
        P(exp + ctx, None),
        P(exp, None, ctx),
    )
    return jax.shard_map(run, mesh=fine, in_specs=in_specs, out_specs=P(exp, ctx), check_vma=False)
```

profile of v0, /device:TPU:1, one launch (start us, length us, event | category | flops | bytes accessed | tf_op | source)
XLA Modules:
  0.0 173.1 jit_solution(16014741731072428206)
XLA Ops:
  0.0 2.5 %prep.1 = (bf16[8,32,128]{2,1,0:T(8,128)(2,1)}, bf16[32,136,128]{2,1,0:T(8,128)(2,1)}, bf16[128,256]{1,0:T(8,128)(2,1)}) custom-call(bf16[128,128]{1,0:T(8,128)(2,1)} %bitcast.12, bf16[64,128]{1,0:T(8,128)(2,1)} %bitcast.13, bf16[64,128]{1,0:T(8,128)(2,1)} %bitcast.14, s32[8,16]{1,0:T(8,128)} %ids_ref.1, f32[8,16]{1,0:T(8,128)} %logit_ref.1), custom_call_target="tpu_custom_call" | custom-call | tf_op jit(solution)/shard_map/prep/pallas_call | solution.py:195
  2.5 49.5 %all_to_all.20.kva_ref.kv_ref = bf16[32,136,128]{2,1,0:T(8,128)(2,1)S(1)} all-to-all(bf16[32,136,128]{2,1,0:T(8,128)(2,1)} %get-tuple-element.12), channel_id=1, replica_groups=mesh['zh'=4,'y'=8,'core'=2,'x'=4,'zl'=2] {'zh','y'}, dimensions={0} | all-to-all | bytes 2228224 | tf_op jit(solution)/shard_map/all_to_all | solution.py:213
  52.0 4.0 %collective-permute-start = (bf16[32,136,128]{2,1,0:T(8,128)(2,1)S(1)}, bf16[32,136,128]{2,1,0:T(8,128)(2,1)S(1)}, u32[]{:S(2)}, u32[]{:S(2)}) collective-permute-start(bf16[32,136,128]{2,1,0:T(8,128)(2,1)S(1)} %all_to_all.20.kva_ref.kv_ref), channel_id=1, source_target_pairs={{0,8},{8,0},{1,9},{9,1},{2,10},{10,2},{3,11},{11,3},{4,12},{12,4},... | collective-permute-start | bytes 3342344 | tf_op jit(solution)/shard_map/ppermute | solution.py:185
  56.0 4.9 %all-to-all-start = ((bf16[8,32,128]{2,1,0:T(8,128)(2,1)}), bf16[8,32,128]{2,1,0:T(8,128)(2,1)S(1)}, u32[]{:S(2)}, u32[]{:S(2)}) async-start(bf16[8,32,128]{2,1,0:T(8,128)(2,1)} %get-tuple-element.11), calls=%async_computation | async-start | bytes 131072 | tf_op jit(solution)/shard_map/all_to_all | solution.py:212
  60.9 0.7 pad_add_fusion.1.at_ref
  61.6 4.7 %all-to-all-done.q_ref = bf16[8,32,128]{2,1,0:T(8,128)(2,1)S(1)} async-done(((bf16[8,32,128]{2,1,0:T(8,128)(2,1)}), bf16[8,32,128]{2,1,0:T(8,128)(2,1)S(1)}, u32[]{:S(2)}, u32[]{:S(2)}) %all-to-all-start) | async-done | bytes 65568 | tf_op jit(solution)/shard_map/all_to_all | solution.py:212
  66.3 0.6 copy-done.7
  66.9 1.0 copy-done.3
  67.9 6.5 %attend.1 = bf16[8,32,128]{2,1,0:T(8,128)(2,1)} custom-call(s32[2]{0:T(128)} %pad_add_fusion.1.at_ref, bf16[8,32,128]{2,1,0:T(8,128)(2,1)} %copy-done.7, bf16[32,136,128]{2,1,0:T(8,128)(2,1)} %copy-done, bf16[32,136,128]{2,1,0:T(8,128)(2,1)} %copy-done.3), custom_call_target="tpu_custom_call" | custom-call | tf_op jit(solution)/shard_map/attend/pallas_call | solution.py:223
  74.4 9.2 %all_to_all.21.got_ref = bf16[8,32,128]{2,1,0:T(8,128)(2,1)} all-to-all(bf16[8,32,128]{2,1,0:T(8,128)(2,1)} %attend.1), channel_id=1, replica_groups=mesh['zh'=4,'y'=8,'core'=2,'x'=4,'zl'=2] {'x','zl'}, dimensions={0} | all-to-all | bytes 131072 | tf_op jit(solution)/shard_map/all_to_all | solution.py:231
  83.6 2.1 %compact.1 = bf16[32,128,128]{2,1,0:T(8,128)(2,1)} custom-call(bf16[128,256]{1,0:T(8,128)(2,1)} %get-tuple-element.10.back_ref, bf16[8,32,128]{2,1,0:T(8,128)(2,1)} %all_to_all.21.got_ref), custom_call_target="tpu_custom_call" | custom-call | tf_op jit(solution)/shard_map/compact/pallas_call | solution.py:232
  85.7 4.3 %all-to-all-start.3 = ((bf16[32,128,128]{2,1,0:T(8,128)(2,1)}), bf16[32,128,128]{2,1,0:T(8,128)(2,1)S(1)}, u32[]{:S(2)}, u32[]{:S(2)}) async-start(bf16[32,128,128]{2,1,0:T(8,128)(2,1)} %compact.1), calls=%async_computation.3 | async-start | bytes 2097152 | tf_op jit(solution)/shard_map/all_to_all | solution.py:239
  90.0 2.4 %collective-permute-start.1 = (bf16[8,128,128]{2,1,0:T(8,128)(2,1)S(1)}, bf16[8,128,128]{2,1,0:T(8,128)(2,1)S(1)}, u32[]{:S(2)}, u32[]{:S(2)}) collective-permute-start(bf16[8,128,128]{2,1,0:T(8,128)(2,1)S(1)} %copy-done.8), channel_id=1, source_target_pairs={{0,1},{1,0},{2,3},{3,2},{4,5},{5,4},{6,7},{7,6},{8,9},{9,8},{10,11... | collective-permute-start | bytes 786440 | tf_op jit(solution)/shard_map/ppermute | solution.py:185
  92.4 28.5 %collective-permute-done.1 = bf16[8,128,128]{2,1,0:T(8,128)(2,1)S(1)} collective-permute-done((bf16[8,128,128]{2,1,0:T(8,128)(2,1)S(1)}, bf16[8,128,128]{2,1,0:T(8,128)(2,1)S(1)}, u32[]{:S(2)}, u32[]{:S(2)}) %collective-permute-start.1) | collective-permute-done | bytes 262176 | tf_op jit(solution)/shard_map/ppermute | solution.py:185
  121.0 2.2 %collective-permute-start.2 = (bf16[16,128,128]{2,1,0:T(8,128)(2,1)S(1)}, bf16[16,128,128]{2,1,0:T(8,128)(2,1)S(1)}, u32[]{:S(2)}, u32[]{:S(2)}) collective-permute-start(bf16[16,128,128]{2,1,0:T(8,128)(2,1)S(1)} %constant_dynamic-update-slice_fusion.refs_0_), channel_id=1, source_target_pairs={{0,2},{2,4},{4,6},{6,0},{1,3},{3,5},{5,7},{7,1},{8,10},{10,12},{12... | collective-permute-start | bytes 1572872 | tf_op jit(solution)/shard_map/ppermute | solution.py:185
  123.2 3.9 %collective-permute-start.3 = (bf16[16,128,128]{2,1,0:T(8,128)(2,1)S(1)}, bf16[16,128,128]{2,1,0:T(8,128)(2,1)S(1)}, u32[]{:S(2)}, u32[]{:S(2)}) collective-permute-start(bf16[16,128,128]{2,1,0:T(8,128)(2,1)S(1)} %constant_dynamic-update-slice_fusion.refs_0_), channel_id=1, source_target_pairs={{0,4},{2,6},{4,0},{6,2},{1,5},{3,7},{5,1},{7,3},{8,12},{10,14},{12... | collective-permute-start | bytes 1572872 | tf_op jit(solution)/shard_map/ppermute | solution.py:185
  127.2 2.7 %collective-permute-start.4 = (bf16[16,128,128]{2,1,0:T(8,128)(2,1)S(1)}, bf16[16,128,128]{2,1,0:T(8,128)(2,1)S(1)}, u32[]{:S(2)}, u32[]{:S(2)}) collective-permute-start(bf16[16,128,128]{2,1,0:T(8,128)(2,1)S(1)} %constant_dynamic-update-slice_fusion.refs_0_), channel_id=1, source_target_pairs={{0,6},{2,0},{4,2},{6,4},{1,7},{3,1},{5,3},{7,5},{8,14},{10,8},{12,... | collective-permute-start | bytes 1572872 | tf_op jit(solution)/shard_map/ppermute | solution.py:185
  129.9 4.0 %collective-permute-start.5 = (bf16[16,128,128]{2,1,0:T(8,128)(2,1)S(1)}, bf16[16,128,128]{2,1,0:T(8,128)(2,1)}, u32[]{:S(2)}, u32[]{:S(2)}) collective-permute-start(bf16[16,128,128]{2,1,0:T(8,128)(2,1)S(1)} %constant_dynamic-update-slice_fusion.refs_0_), channel_id=1, source_target_pairs={{0,8},{8,0},{1,9},{9,1},{2,10},{10,2},{3,11},{11,3},{4,12},{12,4},... | collective-permute-start | bytes 1572872 | tf_op jit(solution)/shard_map/ppermute | solution.py:185
  133.9 3.0 %collective-permute-done.2.refs_1_ = bf16[16,128,128]{2,1,0:T(8,128)(2,1)S(1)} collective-permute-done((bf16[16,128,128]{2,1,0:T(8,128)(2,1)S(1)}, bf16[16,128,128]{2,1,0:T(8,128)(2,1)S(1)}, u32[]{:S(2)}, u32[]{:S(2)}) %collective-permute-start.2) | collective-permute-done | bytes 524320 | tf_op jit(solution)/shard_map/ppermute | solution.py:185
  136.9 14.7 %collective-permute-start.6 = (bf16[16,128,128]{2,1,0:T(8,128)(2,1)S(1)}, bf16[16,128,128]{2,1,0:T(8,128)(2,1)}, u32[]{:S(2)}, u32[]{:S(2)}) collective-permute-start(bf16[16,128,128]{2,1,0:T(8,128)(2,1)S(1)} %collective-permute-done.2.refs_1_), channel_id=1, source_target_pairs={{0,8},{8,0},{1,9},{9,1},{2,10},{10,2},{3,11},{11,3},{4,12},{12,4},... | collective-permute-start | bytes 1572872 | tf_op jit(solution)/shard_map/ppermute | solution.py:185
  151.6 0.0 collective-permute-done.3.refs_2_
  151.6 1.9 %collective-permute-start.7 = (bf16[16,128,128]{2,1,0:T(8,128)(2,1)S(1)}, bf16[16,128,128]{2,1,0:T(8,128)(2,1)}, u32[]{:S(2)}, u32[]{:S(2)}) collective-permute-start(bf16[16,128,128]{2,1,0:T(8,128)(2,1)S(1)} %collective-permute-done.3.refs_2_), channel_id=1, source_target_pairs={{0,8},{8,0},{1,9},{9,1},{2,10},{10,2},{3,11},{11,3},{4,12},{12,4},... | collective-permute-start | bytes 1572872 | tf_op jit(solution)/shard_map/ppermute | solution.py:185
  153.6 0.0 collective-permute-done.4.refs_3_
  153.6 2.4 %collective-permute-start.8 = (bf16[16,128,128]{2,1,0:T(8,128)(2,1)S(1)}, bf16[16,128,128]{2,1,0:T(8,128)(2,1)}, u32[]{:S(2)}, u32[]{:S(2)}) collective-permute-start(bf16[16,128,128]{2,1,0:T(8,128)(2,1)S(1)} %collective-permute-done.4.refs_3_), channel_id=1, source_target_pairs={{0,8},{8,0},{1,9},{9,1},{2,10},{10,2},{3,11},{11,3},{4,12},{12,4},... | collective-permute-start | bytes 1572872 | tf_op jit(solution)/shard_map/ppermute | solution.py:185
  156.0 0.6 pad_add_fusion.at_ref
  156.6 1.0 collective-permute-done.8.refs_7_
  157.7 0.9 copy-done.1
  158.6 9.5 %project.1 = (bf16[256,128]{1,0:T(8,128)(2,1)}, bf16[256,128]{1,0:T(8,128)(2,1)}) custom-call(s32[3]{0:T(128)} %pad_add_fusion.at_ref, bf16[32,128,128]{2,1,0:T(8,128)(2,1)} %copy-done.1, bf16[32,136,128]{2,1,0:T(8,128)(2,1)} %copy-done, bf16[16,128,128]{2,1,0:T(8,128)(2,1)} %copy-done.2, bf16[16,128,128]{2,1,0:T(8,128)(2,1)} %copy-done.4, ...), custom_call_target="tpu_custom_call" | custom-call | tf_op jit(solution)/shard_map/project/pallas_call | solution.py:240
  168.2 2.3 %collective-permute-start.9 = (bf16[256,128]{1,0:T(8,128)(2,1)}, bf16[256,128]{1,0:T(8,128)(2,1)S(1)}, u32[]{:S(2)}, u32[]{:S(2)}) collective-permute-start(bf16[256,128]{1,0:T(8,128)(2,1)} %get-tuple-element.14), channel_id=1, source_target_pairs={{0,8},{8,0},{1,9},{9,1},{2,10},{10,2},{3,11},{11,3},{4,12},{12,4},... | collective-permute-start | bytes 196616 | tf_op jit(solution)/shard_map/ppermute | solution.py:185
  170.5 1.1 collective-permute-done.9
  171.5 0.9 select_bitcast_fusion.1
  172.4 0.7 copy.7
  (23 shorter events, 0.1 us)
Async XLA Ops:
  52.0 14.3 %copy-start = (bf16[32,136,128]{2,1,0:T(8,128)(2,1)}, bf16[32,136,128]{2,1,0:T(8,128)(2,1)S(1)}, u32[]{:S(2)}) copy-start(bf16[32,136,128]{2,1,0:T(8,128)(2,1)S(1)} %all_to_all.20.kva_ref.kv_ref) | copy-start | bytes 3342340
  52.0 14.3 %collective-permute-start = (bf16[32,136,128]{2,1,0:T(8,128)(2,1)S(1)}, bf16[32,136,128]{2,1,0:T(8,128)(2,1)S(1)}, u32[]{:S(2)}, u32[]{:S(2)}) collective-permute-start(bf16[32,136,128]{2,1,0:T(8,128)(2,1)S(1)} %all_to_all.20.kva_ref.kv_ref), channel_id=1, source_target_pairs={{0,8},{8,0},{1,9},{9,1},{2,10},{10,2},{3,11},{11,3},{4,12},{12,4},... | collective-permute-start | bytes 3342344 | tf_op jit(solution)/shard_map/ppermute | solution.py:185
  56.0 10.3 %all-to-all-start = ((bf16[8,32,128]{2,1,0:T(8,128)(2,1)}), bf16[8,32,128]{2,1,0:T(8,128)(2,1)S(1)}, u32[]{:S(2)}, u32[]{:S(2)}) async-start(bf16[8,32,128]{2,1,0:T(8,128)(2,1)} %get-tuple-element.11), calls=%async_computation | async-start | bytes 131072 | tf_op jit(solution)/shard_map/all_to_all | solution.py:212
  66.3 0.6 copy-start.7
  66.9 1.0 copy-start.3
  85.7 4.3 %copy-start.8 = (bf16[8,128,128]{2,1,0:T(8,128)(2,1)S(1)}, bf16[8,128,128]{2,1,0:T(8,128)(2,1)}, u32[]{:S(2)}) copy-start(bf16[8,128,128]{2,1,0:T(8,128)(2,1)} %param.11) | copy-start | bytes 786436
  85.7 71.9 %all-to-all-start.3 = ((bf16[32,128,128]{2,1,0:T(8,128)(2,1)}), bf16[32,128,128]{2,1,0:T(8,128)(2,1)S(1)}, u32[]{:S(2)}, u32[]{:S(2)}) async-start(bf16[32,128,128]{2,1,0:T(8,128)(2,1)} %compact.1), calls=%async_computation.3 | async-start | bytes 2097152 | tf_op jit(solution)/shard_map/all_to_all | solution.py:239
  90.0 31.0 %collective-permute-start.1 = (bf16[8,128,128]{2,1,0:T(8,128)(2,1)S(1)}, bf16[8,128,128]{2,1,0:T(8,128)(2,1)S(1)}, u32[]{:S(2)}, u32[]{:S(2)}) collective-permute-start(bf16[8,128,128]{2,1,0:T(8,128)(2,1)S(1)} %copy-done.8), channel_id=1, source_target_pairs={{0,1},{1,0},{2,3},{3,2},{4,5},{5,4},{6,7},{7,6},{8,9},{9,8},{10,11... | collective-permute-start | bytes 786440 | tf_op jit(solution)/shard_map/ppermute | solution.py:185
  121.0 36.6 %copy-start.2 = (bf16[16,128,128]{2,1,0:T(8,128)(2,1)}, bf16[16,128,128]{2,1,0:T(8,128)(2,1)S(1)}, u32[]{:S(2)}) copy-start(bf16[16,128,128]{2,1,0:T(8,128)(2,1)S(1)} %constant_dynamic-update-slice_fusion.refs_0_) | copy-start | bytes 1572868
  121.0 15.9 %collective-permute-start.2 = (bf16[16,128,128]{2,1,0:T(8,128)(2,1)S(1)}, bf16[16,128,128]{2,1,0:T(8,128)(2,1)S(1)}, u32[]{:S(2)}, u32[]{:S(2)}) collective-permute-start(bf16[16,128,128]{2,1,0:T(8,128)(2,1)S(1)} %constant_dynamic-update-slice_fusion.refs_0_), channel_id=1, source_target_pairs={{0,2},{2,4},{4,6},{6,0},{1,3},{3,5},{5,7},{7,1},{8,10},{10,12},{12... | collective-permute-start | bytes 1572872 | tf_op jit(solution)/shard_map/ppermute | solution.py:185
  123.2 28.4 %collective-permute-start.3 = (bf16[16,128,128]{2,1,0:T(8,128)(2,1)S(1)}, bf16[16,128,128]{2,1,0:T(8,128)(2,1)S(1)}, u32[]{:S(2)}, u32[]{:S(2)}) collective-permute-start(bf16[16,128,128]{2,1,0:T(8,128)(2,1)S(1)} %constant_dynamic-update-slice_fusion.refs_0_), channel_id=1, source_target_pairs={{0,4},{2,6},{4,0},{6,2},{1,5},{3,7},{5,1},{7,3},{8,12},{10,14},{12... | collective-permute-start | bytes 1572872 | tf_op jit(solution)/shard_map/ppermute | solution.py:185
  127.2 26.4 %collective-permute-start.4 = (bf16[16,128,128]{2,1,0:T(8,128)(2,1)S(1)}, bf16[16,128,128]{2,1,0:T(8,128)(2,1)S(1)}, u32[]{:S(2)}, u32[]{:S(2)}) collective-permute-start(bf16[16,128,128]{2,1,0:T(8,128)(2,1)S(1)} %constant_dynamic-update-slice_fusion.refs_0_), channel_id=1, source_target_pairs={{0,6},{2,0},{4,2},{6,4},{1,7},{3,1},{5,3},{7,5},{8,14},{10,8},{12,... | collective-permute-start | bytes 1572872 | tf_op jit(solution)/shard_map/ppermute | solution.py:185
  129.9 26.7 %collective-permute-start.5 = (bf16[16,128,128]{2,1,0:T(8,128)(2,1)S(1)}, bf16[16,128,128]{2,1,0:T(8,128)(2,1)}, u32[]{:S(2)}, u32[]{:S(2)}) collective-permute-start(bf16[16,128,128]{2,1,0:T(8,128)(2,1)S(1)} %constant_dynamic-update-slice_fusion.refs_0_), channel_id=1, source_target_pairs={{0,8},{8,0},{1,9},{9,1},{2,10},{10,2},{3,11},{11,3},{4,12},{12,4},... | collective-permute-start | bytes 1572872 | tf_op jit(solution)/shard_map/ppermute | solution.py:185
  136.9 20.7 %copy-start.4 = (bf16[16,128,128]{2,1,0:T(8,128)(2,1)}, bf16[16,128,128]{2,1,0:T(8,128)(2,1)S(1)}, u32[]{:S(2)}) copy-start(bf16[16,128,128]{2,1,0:T(8,128)(2,1)S(1)} %collective-permute-done.2.refs_1_) | copy-start | bytes 1572868
  136.9 19.7 %collective-permute-start.6 = (bf16[16,128,128]{2,1,0:T(8,128)(2,1)S(1)}, bf16[16,128,128]{2,1,0:T(8,128)(2,1)}, u32[]{:S(2)}, u32[]{:S(2)}) collective-permute-start(bf16[16,128,128]{2,1,0:T(8,128)(2,1)S(1)} %collective-permute-done.2.refs_1_), channel_id=1, source_target_pairs={{0,8},{8,0},{1,9},{9,1},{2,10},{10,2},{3,11},{11,3},{4,12},{12,4},... | collective-permute-start | bytes 1572872 | tf_op jit(solution)/shard_map/ppermute | solution.py:185
  151.6 6.0 %copy-start.5 = (bf16[16,128,128]{2,1,0:T(8,128)(2,1)}, bf16[16,128,128]{2,1,0:T(8,128)(2,1)S(1)}, u32[]{:S(2)}) copy-start(bf16[16,128,128]{2,1,0:T(8,128)(2,1)S(1)} %collective-permute-done.3.refs_2_) | copy-start | bytes 1572868
  151.6 5.0 %collective-permute-start.7 = (bf16[16,128,128]{2,1,0:T(8,128)(2,1)S(1)}, bf16[16,128,128]{2,1,0:T(8,128)(2,1)}, u32[]{:S(2)}, u32[]{:S(2)}) collective-permute-start(bf16[16,128,128]{2,1,0:T(8,128)(2,1)S(1)} %collective-permute-done.3.refs_2_), channel_id=1, source_target_pairs={{0,8},{8,0},{1,9},{9,1},{2,10},{10,2},{3,11},{11,3},{4,12},{12,4},... | collective-permute-start | bytes 1572872 | tf_op jit(solution)/shard_map/ppermute | solution.py:185
  153.6 4.1 %copy-start.6 = (bf16[16,128,128]{2,1,0:T(8,128)(2,1)}, bf16[16,128,128]{2,1,0:T(8,128)(2,1)S(1)}, u32[]{:S(2)}) copy-start(bf16[16,128,128]{2,1,0:T(8,128)(2,1)S(1)} %collective-permute-done.4.refs_3_) | copy-start | bytes 1572868
  153.6 4.1 %collective-permute-start.8 = (bf16[16,128,128]{2,1,0:T(8,128)(2,1)S(1)}, bf16[16,128,128]{2,1,0:T(8,128)(2,1)}, u32[]{:S(2)}, u32[]{:S(2)}) collective-permute-start(bf16[16,128,128]{2,1,0:T(8,128)(2,1)S(1)} %collective-permute-done.4.refs_3_), channel_id=1, source_target_pairs={{0,8},{8,0},{1,9},{9,1},{2,10},{10,2},{3,11},{11,3},{4,12},{12,4},... | collective-permute-start | bytes 1572872 | tf_op jit(solution)/shard_map/ppermute | solution.py:185
  157.7 1.0 copy-start.1
  168.2 3.4 %collective-permute-start.9 = (bf16[256,128]{1,0:T(8,128)(2,1)}, bf16[256,128]{1,0:T(8,128)(2,1)S(1)}, u32[]{:S(2)}, u32[]{:S(2)}) collective-permute-start(bf16[256,128]{1,0:T(8,128)(2,1)} %get-tuple-element.14), channel_id=1, source_target_pairs={{0,8},{8,0},{1,9},{9,1},{2,10},{10,2},{3,11},{11,3},{4,12},{12,4},... | collective-permute-start | bytes 196616 | tf_op jit(solution)/shard_map/ppermute | solution.py:185
where the time goes:
time: 174 us; the launch traced here: 173 us
  blocking collectives  58.6 us (34%)
  starting transfers between devices  49.7 us (29%)
  waiting for transfers between devices  38.4 us (22%)
  Pallas kernels  20.7 us (12%)
  local copies, waits for them, and re-layouts  3.31 us (2%)
  other arithmetic  2.13 us (1%)
    all_to_all x1, blocking collectives, run(): kva = lax.all_to_all(kvsend, ('zh', 'y'), 0, 0, tiled=True)  49.5 us
    ppermute x10, starting transfers between devices, shifted(): return lax.ppermute(x, axis, [(i, (i + by) % count) for i in range(count)])  40.5 us
    ppermute x10, waiting for transfers between devices, shifted(): return lax.ppermute(x, axis, [(i, (i + by) % count) for i in range(count)])  33.7 us
    pallas_call x1, Pallas kernels, run(): pl.pallas_call(project_kernel, in_specs=[SMEM] + [VMEM] * 10, out_specs=[...  9.54 us
    all_to_all x1, blocking collectives, run(): home = lax.all_to_all(attended, ('x', 'zl'), 0, 0, tiled=True)  9.15 us
    pallas_call x1, Pallas kernels, run(): pl.pallas_call(attend_kernel, in_specs=[SMEM, VMEM, VMEM, VMEM], out_spec...  6.51 us
    all_to_all x1, starting transfers between devices, run(): qgot = lax.all_to_all(qsend, ('x', 'zl'), 0, 0, tiled=True)  4.93 us
    all_to_all x1, waiting for transfers between devices, run(): qgot = lax.all_to_all(qsend, ('x', 'zl'), 0, 0, tiled=True)  4.68 us
  transfers between devices with their start and end apart: 12, of which 5 were waited for; matrix products, arithmetic and copies ran while one was open for 1% of the time, Pallas kernels for 0%

commit v1 on v0

--- a/solution.py
+++ b/solution.py
@@ -32,7 +32,13 @@
     return lax.broadcasted_iota(jnp.int32, shape, dim)
 
 
-def prep_kernel(q_ref, k_ref, v_ref, ids_ref, logit_ref, qsend_ref, kvsend_ref, back_ref):
+def away(group, x, zl):
+    return ((group // 2 - x + 4) % 4) * 2 + (group % 2 + zl) % 2
+
+
+def prep_kernel(q_ref, k_ref, v_ref, ids_ref, logit_ref, kvsend_ref, back_ref, *qsend_refs):
+    x = lax.axis_index("x")
+    zl = lax.axis_index("zl")
     spread = (iota((TOP, ROWS), 1) % TOP == iota((TOP, ROWS), 0)).astype(f32)
     own = iota((TOK, ROWS), 1) // TOP == iota((TOK, ROWS), 0)
 
@@ -47,7 +53,9 @@
     id_col = jnp.broadcast_to(id_row, (ROWS, ROWS)).T
     earlier = (id_col == id_row) & (iota((ROWS, ROWS), 0) < iota((ROWS, ROWS), 1))
     rank = jnp.sum(earlier.astype(f32), axis=0, keepdims=True).astype(jnp.int32)
-    slot = (id_int // PER) * SLOTS + (id_int % PER) * MOST + rank
+    group = id_int // PER
+    within = (id_int % PER) * MOST + rank
+    slot = away(group, x, zl) * SLOTS + within
     placed = (iota((GROUPS * SLOTS, ROWS), 0) == slot).astype(bf16)
     rows = jnp.dot(placed, q_ref[...], preferred_element_type=f32)
     tag_at = iota((8, ROWS), 0)
@@ -56,9 +64,10 @@
     for g in range(GROUPS):
         here = (iota((ROWS, ROWS), 0) == slot - g * SLOTS).astype(bf16)
         info = lax.dot_general(tags, here, NT, preferred_element_type=f32)
-        qsend_ref[g] = jnp.concatenate(
+        qsend_refs[g][...] = jnp.concatenate(
             [rows[g * SLOTS : g * SLOTS + PER * MOST], info], axis=0
         ).astype(bf16)
+    slot = group * SLOTS + within
     slot_col = jnp.broadcast_to(slot.astype(f32), (ROWS, ROWS)).T.astype(jnp.int32)
     lane = iota((ROWS, ROWS), 1)
     back_ref[:, :ROWS] = (lane == slot_col).astype(bf16)
@@ -76,21 +85,25 @@
     lax.fori_loop(0, CHIPS, fill, 0)
 
 
-def attend_kernel(at_ref, q_ref, kva_ref, kvb_ref, out_ref, s_ref):
+def attend_kernel(at_ref, kva_ref, kvb_ref, *refs):
+    q_refs, (out_ref, s_ref) = refs[:GROUPS], refs[GROUPS:]
     n = GROUPS * SLOTS
     step = 4
     width = step * SPAN
     steps = CHIPS // step
-    queries = q_ref[...].reshape(n, HD)
+    queries = jnp.concatenate([q_ref[...] for q_ref in q_refs], axis=0)
     ctx = at_ref[0]
     core = at_ref[1]
     tags = jnp.concatenate(
-        [q_ref[g, PER * MOST : SLOTS].astype(f32) for g in range(GROUPS)], axis=0
+        [q_ref[PER * MOST : SLOTS].astype(f32) for q_ref in q_refs], axis=0
     )
     tags = jnp.concatenate([tags, tags], axis=0).T[0:SLOTS]
     token = jnp.concatenate([tags[:, g * 8 : g * 8 + 1] for g in range(GROUPS)], axis=0)
     gate = jnp.concatenate([tags[:, g * 8 + 1 : g * 8 + 2] for g in range(GROUPS)], axis=0)
-    source = iota((n, 1), 0) // SLOTS
+    sources = [
+        ((at_ref[2] - d // 2 + 4) % 4) * 2 + (at_ref[3] + d % 2) % 2 for d in range(GROUPS)
+    ]
+    source = jnp.concatenate([jnp.full((SLOTS, 1), d, jnp.int32) for d in sources], axis=0)
     pos = (source * (2 * CHIPS) + ctx) * TOK + token.astype(jnp.int32)
     scale = HD ** (-0.5) * math.log2(math.e)
     lane = iota((1, width), 1)
@@ -123,7 +136,9 @@
     zero = jnp.zeros((n, HD), f32)
     total, acc = lax.fori_loop(0, steps, weigh_both, (zero, zero))
     total = jnp.sum(total, axis=1, keepdims=True)
-    out_ref[...] = (gate * (acc / total)).astype(bf16).reshape(GROUPS, SLOTS, HD)
+    result = (gate * (acc / total)).astype(bf16)
+    for d in range(GROUPS):
+        out_ref[sources[d]] = result[d * SLOTS : (d + 1) * SLOTS]
 
 
 def compact_kernel(back_ref, got_ref, out_ref):
@@ -139,8 +154,13 @@
 
 
 def project_kernel(at_ref, rows_ref, kv_ref, *refs):
-    w_refs = refs[:8]
-    mine_ref, other_ref, a_ref = refs[8:]
+    near_refs, far_refs = refs[:4], refs[4:8]
+    mine_ref, other_ref, a_ref, far_ref, sems = refs[8:]
+    copies = [
+        pltpu.make_async_copy(far_refs[k], far_ref.at[k], sems.at[k]) for k in range(4)
+    ]
+    for copy in copies:
+        copy.start()
     x = at_ref[0]
     zl = at_ref[1]
     token = iota((1, ROWS), 1) // TOP
@@ -164,21 +184,22 @@
 
     lax.fori_loop(0, CHIPS // 2, fill, 0)
 
-    def product(half):
-        total = None
-        for piece in range(GROUPS):
-            ref = w_refs[4 * half + piece // 2]
-            weight = ref[piece % 2 * PER : (piece % 2 + 1) * PER].reshape(PER * HD, HD)
-            term = jnp.dot(a_ref[piece], weight, preferred_element_type=f32)
-            total = term if total is None else total + term
-        return total
-
-    mine_ref[...] = product(0).astype(bf16)
-    other_ref[...] = product(1).astype(bf16)
+    for copy in copies:
+        copy.wait()
+    total = jnp.zeros((CHIPS * TOK, 2 * HD), f32)
+    for piece in range(GROUPS):
+        part = slice(piece % 2 * PER, (piece % 2 + 1) * PER)
+        near = near_refs[piece // 2][part].reshape(PER * HD, HD)
+        far = far_ref[piece // 2, part].reshape(PER * HD, HD)
+        weight = jnp.concatenate([near, far], axis=1)
+        total = total + jnp.dot(a_ref[piece], weight, preferred_element_type=f32)
+    mine_ref[...] = total[:, :HD].astype(bf16)
+    other_ref[...] = total[:, HD:].astype(bf16)
 
 
 SMEM = pl.BlockSpec(memory_space=pltpu.SMEM)
 VMEM = pl.BlockSpec(memory_space=pltpu.VMEM)
+ANY = pl.BlockSpec(memory_space=pl.ANY)
 
 
 def shifted(x, axis, count, by):
@@ -189,18 +210,19 @@
     zh, y, core = lax.axis_index("zh"), lax.axis_index("y"), lax.axis_index("core")
     x, zl = lax.axis_index("x"), lax.axis_index("zl")
     ctx = (zh * 8 + y) * 2 + core
-    at = jnp.stack([ctx, core]).astype(jnp.int32)
+    at = jnp.stack([ctx, core, x, zl]).astype(jnp.int32)
     at_exp = jnp.stack([x, zl, core]).astype(jnp.int32)
     shape = jax.ShapeDtypeStruct
-    qsend, kvsend, back = pl.pallas_call(
+    kvsend, back, *qsend = pl.pallas_call(
         prep_kernel,
         in_specs=[VMEM] * 5,
-        out_specs=[VMEM] * 3,
+        out_specs=[VMEM] * 10,
         out_shape=[
-            shape((GROUPS, SLOTS, HD), bf16),
             shape((CHIPS, KVROWS, HD), bf16),
             shape((ROWS, GROUPS * SLOTS), bf16),
-        ],
+        ]
+        + [shape((SLOTS, HD), bf16)] * GROUPS,
+        compiler_params=pltpu.CompilerParams(vmem_limit_bytes=8 << 20),
         name="prep",
     )(
         queries.reshape(ROWS, HD),
@@ -209,7 +231,12 @@
         expert_ids,
         gate_logits,
     )
-    qgot = lax.all_to_all(qsend, ("x", "zl"), 0, 0, tiled=True)
+    qgot = [qsend[0]]
+    for d in range(1, GROUPS):
+        moves = [
+            (i, (i // 2 + d // 2) % 4 * 2 + (i + d) % 2) for i in range(GROUPS)
+        ]
+        qgot.append(lax.ppermute(qsend[d], ("x", "zl"), moves))
     kva = lax.all_to_all(kvsend, ("zh", "y"), 0, 0, tiled=True)
     near = shifted(out_weight, "zl", 2, 1)
     pair = jnp.concatenate([out_weight, near], axis=0)
@@ -222,35 +249,41 @@
     kvb = shifted(kva, "core", 2, 1)
     attended = pl.pallas_call(
         attend_kernel,
-        in_specs=[SMEM, VMEM, VMEM, VMEM],
+        in_specs=[SMEM] + [VMEM] * 10,
         out_specs=VMEM,
         out_shape=shape((GROUPS, SLOTS, HD), bf16),
         scratch_shapes=[pltpu.VMEM((16, GROUPS * SLOTS, 4 * SPAN), f32)],
+        compiler_params=pltpu.CompilerParams(vmem_limit_bytes=14 << 20),
         name="attend",
-    )(at, qgot, kva, kvb)
+    )(at, kva, kvb, *qgot)
     home = lax.all_to_all(attended, ("x", "zl"), 0, 0, tiled=True)
     rows = pl.pallas_call(
         compact_kernel,
         in_specs=[VMEM, VMEM],
         out_specs=VMEM,
         out_shape=shape((CHIPS, ROWS, HD), bf16),
+        compiler_params=pltpu.CompilerParams(vmem_limit_bytes=8 << 20),
         name="compact",
     )(back, home)
     rows = lax.all_to_all(rows, ("zh", "y"), 0, 0, tiled=True)
     mine, other = pl.pallas_call(
         project_kernel,
-        in_specs=[SMEM] + [VMEM] * 10,
+        in_specs=[SMEM] + [VMEM] * 6 + [ANY] * 4,
         out_specs=[VMEM, VMEM],
         out_shape=[shape((CHIPS * TOK, HD), bf16)] * 2,
-        scratch_shapes=[pltpu.VMEM((GROUPS, CHIPS * TOK, PER * HD), bf16)],
+        scratch_shapes=[
+            pltpu.VMEM((GROUPS, CHIPS * TOK, PER * HD), bf16),
+            pltpu.VMEM((4, 2 * PER, HD, HD), bf16),
+            pltpu.SemaphoreType.DMA((4,)),
+        ],
+        compiler_params=pltpu.CompilerParams(vmem_limit_bytes=20 << 20),
         name="project",
     )(at_exp, rows, kva, *pieces, *far)
     got = shifted(other, "core", 2, 1)
+    own = lax.broadcasted_iota(jnp.int32, (CHIPS, 2, TOK, HD), 1) == core
     mine = mine.reshape(CHIPS, 1, TOK, HD)
     got = got.reshape(CHIPS, 1, TOK, HD)
-    first = jnp.where(core == 0, mine, got)
-    second = jnp.where(core == 0, got, mine)
-    return jnp.concatenate([first, second], axis=1).reshape(2 * CHIPS * TOK, HD)
+    return jnp.where(own, mine, got).reshape(2 * CHIPS * TOK, HD)
 
 
 def solution(mesh):

time: 174 us -> 190 us (1.092)
  starting transfers between devices: 49.7 us -> 68.6 us
  local copies, waits for them, and re-layouts: 3.31 us -> 14.8 us
  Pallas kernels: 20.7 us -> 12.6 us
  waiting for transfers between devices: 38.4 us -> 34.6 us
    ppermute x0 -> x7, starting transfers between devices: none -> 22.6 us  [run(): qgot.append(lax.ppermute(qsend[d], ('x', 'zl'), moves))]
    unnamed x19 -> x37, local copies, waits for them, and re-layouts: 2.6 us -> 14.6 us
    pallas_call x3, Pallas kernels: 18.6 us -> 11.3 us  [the longest x1 5.75 us: run(): pl.pallas_call(project_kernel, in_specs=[SMEM] + [VMEM] * 6 + [ANY] * 4,...]
    all_to_all x1 -> x0, starting transfers between devices: 4.93 us -> none  [run(): qgot = lax.all_to_all(qsend, ('x', 'zl'), 0, 0, tiled=True)]
    all_to_all x1 -> x0, waiting for transfers between devices: 4.68 us -> none  [run(): qgot = lax.all_to_all(qsend, ('x', 'zl'), 0, 0, tiled=True)]
    ppermute x0 -> x7, waiting for transfers between devices: none -> 3.04 us  [run(): qgot.append(lax.ppermute(qsend[d], ('x', 'zl'), moves))]
    ppermute x10, waiting for transfers between devices: 33.7 us -> 31.5 us  [shifted(): return lax.ppermute(x, axis, [(i, (i + by) % count) for i in range(count)])]
  transfers between devices with their start and end apart: 12 -> 18, of which waited for: 5 -> 4; matrix products, arithmetic and copies ran while one was open for 1% -> 0% of each run, Pallas kernels for 0% -> 0%
where the time goes in v1:
time: 190 us; the launch traced here: 189 us
  starting transfers between devices  68.6 us (36%)
  blocking collectives  57 us (30%)
  waiting for transfers between devices  34.6 us (18%)
  local copies, waits for them, and re-layouts  14.8 us (8%)
  Pallas kernels  12.6 us (7%)
    all_to_all x1, blocking collectives, run(): kva = lax.all_to_all(kvsend, ('zh', 'y'), 0, 0, tiled=True)  49.3 us
    ppermute x10, starting transfers between devices, shifted(): return lax.ppermute(x, axis, [(i, (i + by) % count) for i in range(count)])  41.5 us
    ppermute x10, waiting for transfers between devices, shifted(): return lax.ppermute(x, axis, [(i, (i + by) % count) for i in range(count)])  31.5 us
    ppermute x7, starting transfers between devices, run(): qgot.append(lax.ppermute(qsend[d], ('x', 'zl'), moves))  22.6 us
    unnamed x37, local copies, waits for them, and re-layouts  14.6 us
    all_to_all x1, blocking collectives, run(): home = lax.all_to_all(attended, ('x', 'zl'), 0, 0, tiled=True)  7.73 us
    pallas_call x1, Pallas kernels, run(): pl.pallas_call(project_kernel, in_specs=[SMEM] + [VMEM] * 6 + [ANY] * 4,...  5.75 us
    pallas_call x1, Pallas kernels, run(): pl.pallas_call(attend_kernel, in_specs=[SMEM] + [VMEM] * 10, out_specs=VM...  4.83 us
  transfers between devices with their start and end apart: 18, of which 4 were waited for; matrix products, arithmetic and copies ran while one was open for 0% of the time, Pallas kernels for 0%

profile of v1, /device:TPU:1, one launch (start us, length us, event | category | flops | bytes accessed | tf_op | source)
XLA Modules:
  0.0 188.9 jit_solution(4844237754331027169)
XLA Ops:
  4.3 49.3 %all_to_all.15.kva_ref.kv_ref = bf16[32,136,128]{2,1,0:T(8,128)(2,1)S(1)} all-to-all(bf16[32,136,128]{2,1,0:T(8,128)(2,1)S(1)} %get-tuple-element.18), channel_id=1, replica_groups=mesh['zh'=4,'y'=8,'core'=2,'x'=4,'zl'=2] {'zh','y'}, dimensions={0} | all-to-all | bytes 2228224 | tf_op jit(solution)/shard_map/all_to_all | solution.py:240
  53.6 4.0 %collective-permute-start = (bf16[32,136,128]{2,1,0:T(8,128)(2,1)S(1)}, bf16[32,136,128]{2,1,0:T(8,128)(2,1)S(1)}, u32[]{:S(2)}, u32[]{:S(2)}) collective-permute-start(bf16[32,136,128]{2,1,0:T(8,128)(2,1)S(1)} %all_to_all.15.kva_ref.kv_ref), channel_id=1, source_target_pairs={{0,8},{8,0},{1,9},{9,1},{2,10},{10,2},{3,11},{11,3},{4,12},{12,4},... | collective-permute-start | bytes 3342344 | tf_op jit(solution)/shard_map/ppermute | solution.py:206
  57.6 3.1 %collective-permute-start.1 = (bf16[32,128]{1,0:T(8,128)(2,1)S(1)}, bf16[32,128]{1,0:T(8,128)(2,1)S(1)}, u32[]{:S(2)}, u32[]{:S(2)}) collective-permute-start(bf16[32,128]{1,0:T(8,128)(2,1)S(1)} %get-tuple-element.20), channel_id=1, source_target_pairs={{0,1},{1,0},{2,3},{3,2},{4,5},{5,4},{6,7},{7,6},{8,9},{9,8},{10,11... | collective-permute-start | bytes 24584 | tf_op jit(solution)/shard_map/ppermute | solution.py:239
  60.7 3.1 %collective-permute-start.2 = (bf16[32,128]{1,0:T(8,128)(2,1)S(1)}, bf16[32,128]{1,0:T(8,128)(2,1)S(1)}, u32[]{:S(2)}, u32[]{:S(2)}) collective-permute-start(bf16[32,128]{1,0:T(8,128)(2,1)S(1)} %get-tuple-element.21), channel_id=1, source_target_pairs={{0,2},{1,3},{2,4},{3,5},{4,6},{5,7},{6,0},{7,1},{8,10},{9,11},{10,... | collective-permute-start | bytes 24584 | tf_op jit(solution)/shard_map/ppermute | solution.py:239
  63.8 3.1 %collective-permute-start.3 = (bf16[32,128]{1,0:T(8,128)(2,1)S(1)}, bf16[32,128]{1,0:T(8,128)(2,1)S(1)}, u32[]{:S(2)}, u32[]{:S(2)}) collective-permute-start(bf16[32,128]{1,0:T(8,128)(2,1)S(1)} %get-tuple-element.22), channel_id=1, source_target_pairs={{0,3},{1,2},{2,5},{3,4},{4,7},{5,6},{6,1},{7,0},{8,11},{9,10},{10,... | collective-permute-start | bytes 24584 | tf_op jit(solution)/shard_map/ppermute | solution.py:239
  66.9 3.3 %collective-permute-start.4 = (bf16[32,128]{1,0:T(8,128)(2,1)S(1)}, bf16[32,128]{1,0:T(8,128)(2,1)S(1)}, u32[]{:S(2)}, u32[]{:S(2)}) collective-permute-start(bf16[32,128]{1,0:T(8,128)(2,1)S(1)} %get-tuple-element.23), channel_id=1, source_target_pairs={{0,4},{1,5},{2,6},{3,7},{4,0},{5,1},{6,2},{7,3},{8,12},{9,13},{10,... | collective-permute-start | bytes 24584 | tf_op jit(solution)/shard_map/ppermute | solution.py:239
  70.3 4.3 %collective-permute-start.5 = (bf16[32,128]{1,0:T(8,128)(2,1)S(1)}, bf16[32,128]{1,0:T(8,128)(2,1)S(1)}, u32[]{:S(2)}, u32[]{:S(2)}) collective-permute-start(bf16[32,128]{1,0:T(8,128)(2,1)S(1)} %get-tuple-element.24), channel_id=1, source_target_pairs={{0,5},{1,4},{2,7},{3,6},{4,1},{5,0},{6,3},{7,2},{8,13},{9,12},{10,... | collective-permute-start | bytes 24584 | tf_op jit(solution)/shard_map/ppermute | solution.py:239
  74.6 3.4 %collective-permute-start.6 = (bf16[32,128]{1,0:T(8,128)(2,1)S(1)}, bf16[32,128]{1,0:T(8,128)(2,1)S(1)}, u32[]{:S(2)}, u32[]{:S(2)}) collective-permute-start(bf16[32,128]{1,0:T(8,128)(2,1)S(1)} %get-tuple-element.25), channel_id=1, source_target_pairs={{0,6},{1,7},{2,0},{3,1},{4,2},{5,3},{6,4},{7,5},{8,14},{9,15},{10,... | collective-permute-start | bytes 24584 | tf_op jit(solution)/shard_map/ppermute | solution.py:239
  78.0 2.2 %collective-permute-start.7 = (bf16[32,128]{1,0:T(8,128)(2,1)S(1)}, bf16[32,128]{1,0:T(8,128)(2,1)S(1)}, u32[]{:S(2)}, u32[]{:S(2)}) collective-permute-start(bf16[32,128]{1,0:T(8,128)(2,1)S(1)} %get-tuple-element.26), channel_id=1, source_target_pairs={{0,7},{1,6},{2,1},{3,0},{4,3},{5,2},{6,5},{7,4},{8,15},{9,14},{10,... | collective-permute-start | bytes 24584 | tf_op jit(solution)/shard_map/ppermute | solution.py:239
  80.3 3.0 %collective-permute-done.7.refs_7_ = bf16[32,128]{1,0:T(8,128)(2,1)S(1)} collective-permute-done((bf16[32,128]{1,0:T(8,128)(2,1)S(1)}, bf16[32,128]{1,0:T(8,128)(2,1)S(1)}, u32[]{:S(2)}, u32[]{:S(2)}) %collective-permute-start.7) | collective-permute-done | bytes 8224 | tf_op jit(solution)/shard_map/ppermute | solution.py:239
  83.3 4.8 %attend.1 = bf16[8,32,128]{2,1,0:T(8,128)(2,1)S(1)} custom-call(s32[4]{0:T(128)S(1)} %pad_add_fusion.1.at_ref, bf16[32,136,128]{2,1,0:T(8,128)(2,1)S(1)} %all_to_all.15.kva_ref.kv_ref, bf16[32,136,128]{2,1,0:T(8,128)(2,1)S(1)} %collective-permute-done.kvb_ref, bf16[32,128]{1,0:T(8,128)(2,1)S(1)} %get-tuple-element.19.refs_0_, ...), custom_call_target="tpu_custom_call" | custom-call | tf_op jit(solution)/shard_map/attend/pallas_call | solution.py:250
  88.2 7.7 %all_to_all.16.got_ref = bf16[8,32,128]{2,1,0:T(8,128)(2,1)S(1)} all-to-all(bf16[8,32,128]{2,1,0:T(8,128)(2,1)S(1)} %attend.1), channel_id=1, replica_groups=mesh['zh'=4,'y'=8,'core'=2,'x'=4,'zl'=2] {'x','zl'}, dimensions={0} | all-to-all | bytes 131072 | tf_op jit(solution)/shard_map/all_to_all | solution.py:259
  95.9 1.3 compact.1
  97.2 4.6 %all-to-all-start.2 = ((bf16[32,128,128]{2,1,0:T(8,128)(2,1)}), bf16[32,128,128]{2,1,0:T(8,128)(2,1)S(1)}, u32[]{:S(2)}, u32[]{:S(2)}) async-start(bf16[32,128,128]{2,1,0:T(8,128)(2,1)} %compact.1), calls=%async_computation.2 | async-start | bytes 2097152 | tf_op jit(solution)/shard_map/all_to_all | solution.py:268
  101.8 2.4 %collective-permute-start.8 = (bf16[8,128,128]{2,1,0:T(8,128)(2,1)S(1)}, bf16[8,128,128]{2,1,0:T(8,128)(2,1)S(1)}, u32[]{:S(2)}, u32[]{:S(2)}) collective-permute-start(bf16[8,128,128]{2,1,0:T(8,128)(2,1)S(1)} %copy-done.17), channel_id=1, source_target_pairs={{0,1},{1,0},{2,3},{3,2},{4,5},{5,4},{6,7},{7,6},{8,9},{9,8},{10,11... | collective-permute-start | bytes 786440 | tf_op jit(solution)/shard_map/ppermute | solution.py:206
  104.2 28.8 %collective-permute-done.8 = bf16[8,128,128]{2,1,0:T(8,128)(2,1)S(1)} collective-permute-done((bf16[8,128,128]{2,1,0:T(8,128)(2,1)S(1)}, bf16[8,128,128]{2,1,0:T(8,128)(2,1)S(1)}, u32[]{:S(2)}, u32[]{:S(2)}) %collective-permute-start.8) | collective-permute-done | bytes 262176 | tf_op jit(solution)/shard_map/ppermute | solution.py:206
  133.1 2.2 %collective-permute-start.9 = (bf16[16,128,128]{2,1,0:T(8,128)(2,1)S(1)}, bf16[16,128,128]{2,1,0:T(8,128)(2,1)S(1)}, u32[]{:S(2)}, u32[]{:S(2)}) collective-permute-start(bf16[16,128,128]{2,1,0:T(8,128)(2,1)S(1)} %constant_dynamic-update-slice_fusion.refs_0_), channel_id=1, source_target_pairs={{0,2},{2,4},{4,6},{6,0},{1,3},{3,5},{5,7},{7,1},{8,10},{10,12},{12... | collective-permute-start | bytes 1572872 | tf_op jit(solution)/shard_map/ppermute | solution.py:206
  135.3 3.7 %collective-permute-start.10 = (bf16[16,128,128]{2,1,0:T(8,128)(2,1)S(1)}, bf16[16,128,128]{2,1,0:T(8,128)(2,1)S(1)}, u32[]{:S(2)}, u32[]{:S(2)}) collective-permute-start(bf16[16,128,128]{2,1,0:T(8,128)(2,1)S(1)} %constant_dynamic-update-slice_fusion.refs_0_), channel_id=1, source_target_pairs={{0,4},{2,6},{4,0},{6,2},{1,5},{3,7},{5,1},{7,3},{8,12},{10,14},{12... | collective-permute-start | bytes 1572872 | tf_op jit(solution)/shard_map/ppermute | solution.py:206
  139.0 2.8 %collective-permute-start.11 = (bf16[16,128,128]{2,1,0:T(8,128)(2,1)S(1)}, bf16[16,128,128]{2,1,0:T(8,128)(2,1)S(1)}, u32[]{:S(2)}, u32[]{:S(2)}) collective-permute-start(bf16[16,128,128]{2,1,0:T(8,128)(2,1)S(1)} %constant_dynamic-update-slice_fusion.refs_0_), channel_id=1, source_target_pairs={{0,6},{2,0},{4,2},{6,4},{1,7},{3,1},{5,3},{7,5},{8,14},{10,8},{12,... | collective-permute-start | bytes 1572872 | tf_op jit(solution)/shard_map/ppermute | solution.py:206
  141.8 4.7 %collective-permute-start.12 = (bf16[16,128,128]{2,1,0:T(8,128)(2,1)S(1)}, bf16[16,128,128]{2,1,0:T(8,128)(2,1)S(1)}, u32[]{:S(2)}, u32[]{:S(2)}) collective-permute-start(bf16[16,128,128]{2,1,0:T(8,128)(2,1)S(1)} %constant_dynamic-update-slice_fusion.refs_0_), channel_id=1, source_target_pairs={{0,8},{8,0},{1,9},{9,1},{2,10},{10,2},{3,11},{11,3},{4,12},{12,4},... | collective-permute-start | bytes 1572872 | tf_op jit(solution)/shard_map/ppermute | solution.py:206
  146.5 1.7 collective-permute-done.9.refs_1_
  148.2 15.5 %collective-permute-start.13 = (bf16[16,128,128]{2,1,0:T(8,128)(2,1)S(1)}, bf16[16,128,128]{2,1,0:T(8,128)(2,1)S(1)}, u32[]{:S(2)}, u32[]{:S(2)}) collective-permute-start(bf16[16,128,128]{2,1,0:T(8,128)(2,1)S(1)} %collective-permute-done.9.refs_1_), channel_id=1, source_target_pairs={{0,8},{8,0},{1,9},{9,1},{2,10},{10,2},{3,11},{11,3},{4,12},{12,4},... | collective-permute-start | bytes 1572872 | tf_op jit(solution)/shard_map/ppermute | solution.py:206
  163.7 1.9 %collective-permute-start.14 = (bf16[16,128,128]{2,1,0:T(8,128)(2,1)S(1)}, bf16[16,128,128]{2,1,0:T(8,128)(2,1)S(1)}, u32[]{:S(2)}, u32[]{:S(2)}) collective-permute-start(bf16[16,128,128]{2,1,0:T(8,128)(2,1)S(1)} %collective-permute-done.10.refs_2_), channel_id=1, source_target_pairs={{0,8},{8,0},{1,9},{9,1},{2,10},{10,2},{3,11},{11,3},{4,12},{12,4},... | collective-permute-start | bytes 1572872 | tf_op jit(solution)/shard_map/ppermute | solution.py:206
  166.4 2.4 %collective-permute-start.15 = (bf16[16,128,128]{2,1,0:T(8,128)(2,1)S(1)}, bf16[16,128,128]{2,1,0:T(8,128)(2,1)S(1)}, u32[]{:S(2)}, u32[]{:S(2)}) collective-permute-start(bf16[16,128,128]{2,1,0:T(8,128)(2,1)S(1)} %collective-permute-done.11.refs_3_), channel_id=1, source_target_pairs={{0,8},{8,0},{1,9},{9,1},{2,10},{10,2},{3,11},{11,3},{4,12},{12,4},... | collective-permute-start | bytes 1572872 | tf_op jit(solution)/shard_map/ppermute | solution.py:206
  172.9 1.0 copy-done.1
  174.0 1.0 copy-done.3
  175.0 1.0 copy-done.5
  176.1 1.0 copy-done.7
  177.1 1.0 copy-done.9
  178.1 1.0 copy-done.11
  179.2 5.8 %project.1 = (bf16[256,128]{1,0:T(8,128)(2,1)S(1)}, bf16[256,128]{1,0:T(8,128)(2,1)S(1)}) custom-call(s32[3]{0:T(128)S(1)} %pad_add_fusion.at_ref, bf16[32,128,128]{2,1,0:T(8,128)(2,1)S(1)} %all-to-all-done.2.rows_ref, bf16[32,136,128]{2,1,0:T(8,128)(2,1)S(1)} %all_to_all.15.kva_ref.kv_ref, ...), custom_call_target="tpu_custom_call" | custom-call | tf_op jit(solution)/shard_map/project/pallas_call | solution.py:269
  184.9 1.9 %collective-permute-start.16 = (bf16[256,128]{1,0:T(8,128)(2,1)S(1)}, bf16[256,128]{1,0:T(8,128)(2,1)S(1)}, u32[]{:S(2)}, u32[]{:S(2)}) collective-permute-start(bf16[256,128]{1,0:T(8,128)(2,1)S(1)} %get-tuple-element.28), channel_id=1, source_target_pairs={{0,8},{8,0},{1,9},{9,1},{2,10},{10,2},{3,11},{11,3},{4,12},{12,4},... | collective-permute-start | bytes 196616 | tf_op jit(solution)/shard_map/ppermute | solution.py:206
  (54 shorter events, 11.3 us)
Async XLA Ops:
  0.0 0.8 copy-start.12
  53.6 29.8 %collective-permute-start = (bf16[32,136,128]{2,1,0:T(8,128)(2,1)S(1)}, bf16[32,136,128]{2,1,0:T(8,128)(2,1)S(1)}, u32[]{:S(2)}, u32[]{:S(2)}) collective-permute-start(bf16[32,136,128]{2,1,0:T(8,128)(2,1)S(1)} %all_to_all.15.kva_ref.kv_ref), channel_id=1, source_target_pairs={{0,8},{8,0},{1,9},{9,1},{2,10},{10,2},{3,11},{11,3},{4,12},{12,4},... | collective-permute-start | bytes 3342344 | tf_op jit(solution)/shard_map/ppermute | solution.py:206
  57.6 12.7 %collective-permute-start.1 = (bf16[32,128]{1,0:T(8,128)(2,1)S(1)}, bf16[32,128]{1,0:T(8,128)(2,1)S(1)}, u32[]{:S(2)}, u32[]{:S(2)}) collective-permute-start(bf16[32,128]{1,0:T(8,128)(2,1)S(1)} %get-tuple-element.20), channel_id=1, source_target_pairs={{0,1},{1,0},{2,3},{3,2},{4,5},{5,4},{6,7},{7,6},{8,9},{9,8},{10,11... | collective-permute-start | bytes 24584 | tf_op jit(solution)/shard_map/ppermute | solution.py:239
  60.7 14.0 %collective-permute-start.2 = (bf16[32,128]{1,0:T(8,128)(2,1)S(1)}, bf16[32,128]{1,0:T(8,128)(2,1)S(1)}, u32[]{:S(2)}, u32[]{:S(2)}) collective-permute-start(bf16[32,128]{1,0:T(8,128)(2,1)S(1)} %get-tuple-element.21), channel_id=1, source_target_pairs={{0,2},{1,3},{2,4},{3,5},{4,6},{5,7},{6,0},{7,1},{8,10},{9,11},{10,... | collective-permute-start | bytes 24584 | tf_op jit(solution)/shard_map/ppermute | solution.py:239
  63.8 14.2 %collective-permute-start.3 = (bf16[32,128]{1,0:T(8,128)(2,1)S(1)}, bf16[32,128]{1,0:T(8,128)(2,1)S(1)}, u32[]{:S(2)}, u32[]{:S(2)}) collective-permute-start(bf16[32,128]{1,0:T(8,128)(2,1)S(1)} %get-tuple-element.22), channel_id=1, source_target_pairs={{0,3},{1,2},{2,5},{3,4},{4,7},{5,6},{6,1},{7,0},{8,11},{9,10},{10,... | collective-permute-start | bytes 24584 | tf_op jit(solution)/shard_map/ppermute | solution.py:239
  66.9 13.4 %collective-permute-start.4 = (bf16[32,128]{1,0:T(8,128)(2,1)S(1)}, bf16[32,128]{1,0:T(8,128)(2,1)S(1)}, u32[]{:S(2)}, u32[]{:S(2)}) collective-permute-start(bf16[32,128]{1,0:T(8,128)(2,1)S(1)} %get-tuple-element.23), channel_id=1, source_target_pairs={{0,4},{1,5},{2,6},{3,7},{4,0},{5,1},{6,2},{7,3},{8,12},{9,13},{10,... | collective-permute-start | bytes 24584 | tf_op jit(solution)/shard_map/ppermute | solution.py:239
  70.3 10.0 %collective-permute-start.5 = (bf16[32,128]{1,0:T(8,128)(2,1)S(1)}, bf16[32,128]{1,0:T(8,128)(2,1)S(1)}, u32[]{:S(2)}, u32[]{:S(2)}) collective-permute-start(bf16[32,128]{1,0:T(8,128)(2,1)S(1)} %get-tuple-element.24), channel_id=1, source_target_pairs={{0,5},{1,4},{2,7},{3,6},{4,1},{5,0},{6,3},{7,2},{8,13},{9,12},{10,... | collective-permute-start | bytes 24584 | tf_op jit(solution)/shard_map/ppermute | solution.py:239
  74.6 5.7 %collective-permute-start.6 = (bf16[32,128]{1,0:T(8,128)(2,1)S(1)}, bf16[32,128]{1,0:T(8,128)(2,1)S(1)}, u32[]{:S(2)}, u32[]{:S(2)}) collective-permute-start(bf16[32,128]{1,0:T(8,128)(2,1)S(1)} %get-tuple-element.25), channel_id=1, source_target_pairs={{0,6},{1,7},{2,0},{3,1},{4,2},{5,3},{6,4},{7,5},{8,14},{9,15},{10,... | collective-permute-start | bytes 24584 | tf_op jit(solution)/shard_map/ppermute | solution.py:239
  78.0 5.3 %collective-permute-start.7 = (bf16[32,128]{1,0:T(8,128)(2,1)S(1)}, bf16[32,128]{1,0:T(8,128)(2,1)S(1)}, u32[]{:S(2)}, u32[]{:S(2)}) collective-permute-start(bf16[32,128]{1,0:T(8,128)(2,1)S(1)} %get-tuple-element.26), channel_id=1, source_target_pairs={{0,7},{1,6},{2,1},{3,0},{4,3},{5,2},{6,5},{7,4},{8,15},{9,14},{10,... | collective-permute-start | bytes 24584 | tf_op jit(solution)/shard_map/ppermute | solution.py:239
  97.2 4.6 %copy-start.17 = (bf16[8,128,128]{2,1,0:T(8,128)(2,1)S(1)}, bf16[8,128,128]{2,1,0:T(8,128)(2,1)}, u32[]{:S(2)}) copy-start(bf16[8,128,128]{2,1,0:T(8,128)(2,1)} %param.11) | copy-start | bytes 786436
  97.2 75.7 %all-to-all-start.2 = ((bf16[32,128,128]{2,1,0:T(8,128)(2,1)}), bf16[32,128,128]{2,1,0:T(8,128)(2,1)S(1)}, u32[]{:S(2)}, u32[]{:S(2)}) async-start(bf16[32,128,128]{2,1,0:T(8,128)(2,1)} %compact.1), calls=%async_computation.2 | async-start | bytes 2097152 | tf_op jit(solution)/shard_map/all_to_all | solution.py:268
  101.8 31.2 %collective-permute-start.8 = (bf16[8,128,128]{2,1,0:T(8,128)(2,1)S(1)}, bf16[8,128,128]{2,1,0:T(8,128)(2,1)S(1)}, u32[]{:S(2)}, u32[]{:S(2)}) collective-permute-start(bf16[8,128,128]{2,1,0:T(8,128)(2,1)S(1)} %copy-done.17), channel_id=1, source_target_pairs={{0,1},{1,0},{2,3},{3,2},{4,5},{5,4},{6,7},{7,6},{8,9},{9,8},{10,11... | collective-permute-start | bytes 786440 | tf_op jit(solution)/shard_map/ppermute | solution.py:206
  133.1 15.1 %collective-permute-start.9 = (bf16[16,128,128]{2,1,0:T(8,128)(2,1)S(1)}, bf16[16,128,128]{2,1,0:T(8,128)(2,1)S(1)}, u32[]{:S(2)}, u32[]{:S(2)}) collective-permute-start(bf16[16,128,128]{2,1,0:T(8,128)(2,1)S(1)} %constant_dynamic-update-slice_fusion.refs_0_), channel_id=1, source_target_pairs={{0,2},{2,4},{4,6},{6,0},{1,3},{3,5},{5,7},{7,1},{8,10},{10,12},{12... | collective-permute-start | bytes 1572872 | tf_op jit(solution)/shard_map/ppermute | solution.py:206
  135.3 28.4 %collective-permute-start.10 = (bf16[16,128,128]{2,1,0:T(8,128)(2,1)S(1)}, bf16[16,128,128]{2,1,0:T(8,128)(2,1)S(1)}, u32[]{:S(2)}, u32[]{:S(2)}) collective-permute-start(bf16[16,128,128]{2,1,0:T(8,128)(2,1)S(1)} %constant_dynamic-update-slice_fusion.refs_0_), channel_id=1, source_target_pairs={{0,4},{2,6},{4,0},{6,2},{1,5},{3,7},{5,1},{7,3},{8,12},{10,14},{12... | collective-permute-start | bytes 1572872 | tf_op jit(solution)/shard_map/ppermute | solution.py:206
  139.0 27.4 %collective-permute-start.11 = (bf16[16,128,128]{2,1,0:T(8,128)(2,1)S(1)}, bf16[16,128,128]{2,1,0:T(8,128)(2,1)S(1)}, u32[]{:S(2)}, u32[]{:S(2)}) collective-permute-start(bf16[16,128,128]{2,1,0:T(8,128)(2,1)S(1)} %constant_dynamic-update-slice_fusion.refs_0_), channel_id=1, source_target_pairs={{0,6},{2,0},{4,2},{6,4},{1,7},{3,1},{5,3},{7,5},{8,14},{10,8},{12,... | collective-permute-start | bytes 1572872 | tf_op jit(solution)/shard_map/ppermute | solution.py:206
  141.8 27.9 %collective-permute-start.12 = (bf16[16,128,128]{2,1,0:T(8,128)(2,1)S(1)}, bf16[16,128,128]{2,1,0:T(8,128)(2,1)S(1)}, u32[]{:S(2)}, u32[]{:S(2)}) collective-permute-start(bf16[16,128,128]{2,1,0:T(8,128)(2,1)S(1)} %constant_dynamic-update-slice_fusion.refs_0_), channel_id=1, source_target_pairs={{0,8},{8,0},{1,9},{9,1},{2,10},{10,2},{3,11},{11,3},{4,12},{12,4},... | collective-permute-start | bytes 1572872 | tf_op jit(solution)/shard_map/ppermute | solution.py:206
  148.2 22.4 %collective-permute-start.13 = (bf16[16,128,128]{2,1,0:T(8,128)(2,1)S(1)}, bf16[16,128,128]{2,1,0:T(8,128)(2,1)S(1)}, u32[]{:S(2)}, u32[]{:S(2)}) collective-permute-start(bf16[16,128,128]{2,1,0:T(8,128)(2,1)S(1)} %collective-permute-done.9.refs_1_), channel_id=1, source_target_pairs={{0,8},{8,0},{1,9},{9,1},{2,10},{10,2},{3,11},{11,3},{4,12},{12,4},... | collective-permute-start | bytes 1572872 | tf_op jit(solution)/shard_map/ppermute | solution.py:206
  163.7 7.6 %collective-permute-start.14 = (bf16[16,128,128]{2,1,0:T(8,128)(2,1)S(1)}, bf16[16,128,128]{2,1,0:T(8,128)(2,1)S(1)}, u32[]{:S(2)}, u32[]{:S(2)}) collective-permute-start(bf16[16,128,128]{2,1,0:T(8,128)(2,1)S(1)} %collective-permute-done.10.refs_2_), channel_id=1, source_target_pairs={{0,8},{8,0},{1,9},{9,1},{2,10},{10,2},{3,11},{11,3},{4,12},{12,4},... | collective-permute-start | bytes 1572872 | tf_op jit(solution)/shard_map/ppermute | solution.py:206
  165.6 0.8 copy-start
  166.4 5.7 %collective-permute-start.15 = (bf16[16,128,128]{2,1,0:T(8,128)(2,1)S(1)}, bf16[16,128,128]{2,1,0:T(8,128)(2,1)S(1)}, u32[]{:S(2)}, u32[]{:S(2)}) collective-permute-start(bf16[16,128,128]{2,1,0:T(8,128)(2,1)S(1)} %collective-permute-done.11.refs_3_), channel_id=1, source_target_pairs={{0,8},{8,0},{1,9},{9,1},{2,10},{10,2},{3,11},{11,3},{4,12},{12,4},... | collective-permute-start | bytes 1572872 | tf_op jit(solution)/shard_map/ppermute | solution.py:206
  168.8 0.8 copy-start.2
  169.7 0.8 copy-start.4
  170.5 0.8 copy-start.6
  171.3 0.8 copy-start.8
  172.1 0.8 copy-start.10
  172.9 1.0 copy-start.1
  174.0 1.0 copy-start.3
  175.0 1.0 copy-start.5
  176.1 1.0 copy-start.7
  177.1 1.0 copy-start.9
  178.1 1.0 copy-start.11
  184.9 3.1 %collective-permute-start.16 = (bf16[256,128]{1,0:T(8,128)(2,1)S(1)}, bf16[256,128]{1,0:T(8,128)(2,1)S(1)}, u32[]{:S(2)}, u32[]{:S(2)}) collective-permute-start(bf16[256,128]{1,0:T(8,128)(2,1)S(1)} %get-tuple-element.28), channel_id=1, source_target_pairs={{0,8},{8,0},{1,9},{9,1},{2,10},{10,2},{3,11},{11,3},{4,12},{12,4},... | collective-permute-start | bytes 196616 | tf_op jit(solution)/shard_map/ppermute | solution.py:206
  (4 other events, 2.8 us)

commit v2 on v1

--- a/solution.py
+++ b/solution.py
@@ -36,7 +36,9 @@
     return ((group // 2 - x + 4) % 4) * 2 + (group % 2 + zl) % 2
 
 
-def prep_kernel(q_ref, k_ref, v_ref, ids_ref, logit_ref, kvsend_ref, back_ref, *qsend_refs):
+def prep_kernel(
+    q_ref, k_ref, v_ref, ids_ref, logit_ref, w_ref, kvsend_ref, back_ref, qnear_ref, cargo_ref
+):
     x = lax.axis_index("x")
     zl = lax.axis_index("zl")
     spread = (iota((TOP, ROWS), 1) % TOP == iota((TOP, ROWS), 0)).astype(f32)
@@ -64,9 +66,14 @@
     for g in range(GROUPS):
         here = (iota((ROWS, ROWS), 0) == slot - g * SLOTS).astype(bf16)
         info = lax.dot_general(tags, here, NT, preferred_element_type=f32)
-        qsend_refs[g][...] = jnp.concatenate(
+        chunk = jnp.concatenate(
             [rows[g * SLOTS : g * SLOTS + PER * MOST], info], axis=0
         ).astype(bf16)
+        if g % 2 == 0:
+            qnear_ref[g // 2] = chunk
+        else:
+            cargo_ref[PER * HD + g // 2 * SLOTS : PER * HD + (g // 2 + 1) * SLOTS] = chunk
+    cargo_ref[0 : PER * HD] = w_ref[...].reshape(PER * HD, HD)
     slot = group * SLOTS + within
     slot_col = jnp.broadcast_to(slot.astype(f32), (ROWS, ROWS)).T.astype(jnp.int32)
     lane = iota((ROWS, ROWS), 1)
@@ -86,16 +93,19 @@
 
 
 def attend_kernel(at_ref, kva_ref, kvb_ref, *refs):
-    q_refs, (out_ref, s_ref) = refs[:GROUPS], refs[GROUPS:]
+    q_refs, (out_ref, s_ref) = refs[:4], refs[4:]
     n = GROUPS * SLOTS
     step = 4
     width = step * SPAN
     steps = CHIPS // step
-    queries = jnp.concatenate([q_ref[...] for q_ref in q_refs], axis=0)
+    chunks = [
+        q_refs[d // 2][d % 2 * SLOTS : (d % 2 + 1) * SLOTS] for d in range(GROUPS)
+    ]
+    queries = jnp.concatenate(chunks, axis=0)
     ctx = at_ref[0]
     core = at_ref[1]
     tags = jnp.concatenate(
-        [q_ref[PER * MOST : SLOTS].astype(f32) for q_ref in q_refs], axis=0
+        [chunk.astype(f32)[PER * MOST :] for chunk in chunks], axis=0
     )
     tags = jnp.concatenate([tags, tags], axis=0).T[0:SLOTS]
     token = jnp.concatenate([tags[:, g * 8 : g * 8 + 1] for g in range(GROUPS)], axis=0)
@@ -154,11 +164,8 @@
 
 
 def project_kernel(at_ref, rows_ref, kv_ref, *refs):
-    near_refs, far_refs = refs[:4], refs[4:8]
-    mine_ref, other_ref, a_ref, far_ref, sems = refs[8:]
-    copies = [
-        pltpu.make_async_copy(far_refs[k], far_ref.at[k], sems.at[k]) for k in range(4)
-    ]
+    mine_ref, other_ref, a_ref, w_ref, sems = refs[8:]
+    copies = [pltpu.make_async_copy(refs[k], w_ref.at[k], sems.at[k]) for k in range(8)]
     for copy in copies:
         copy.start()
     x = at_ref[0]
@@ -189,8 +196,8 @@
     total = jnp.zeros((CHIPS * TOK, 2 * HD), f32)
     for piece in range(GROUPS):
         part = slice(piece % 2 * PER, (piece % 2 + 1) * PER)
-        near = near_refs[piece // 2][part].reshape(PER * HD, HD)
-        far = far_ref[piece // 2, part].reshape(PER * HD, HD)
+        near = w_ref[piece // 2, part].reshape(PER * HD, HD)
+        far = w_ref[4 + piece // 2, part].reshape(PER * HD, HD)
         weight = jnp.concatenate([near, far], axis=1)
         total = total + jnp.dot(a_ref[piece], weight, preferred_element_type=f32)
     mine_ref[...] = total[:, :HD].astype(bf16)
@@ -199,7 +206,7 @@
 
 SMEM = pl.BlockSpec(memory_space=pltpu.SMEM)
 VMEM = pl.BlockSpec(memory_space=pltpu.VMEM)
-ANY = pl.BlockSpec(memory_space=pl.ANY)
+HBM = pl.BlockSpec(memory_space=pltpu.HBM)
 
 
 def shifted(x, axis, count, by):
@@ -213,16 +220,16 @@
     at = jnp.stack([ctx, core, x, zl]).astype(jnp.int32)
     at_exp = jnp.stack([x, zl, core]).astype(jnp.int32)
     shape = jax.ShapeDtypeStruct
-    kvsend, back, *qsend = pl.pallas_call(
+    kvsend, back, qnear, cargo = pl.pallas_call(
         prep_kernel,
-        in_specs=[VMEM] * 5,
-        out_specs=[VMEM] * 10,
+        in_specs=[VMEM] * 6,
+        out_specs=[VMEM] * 4,
         out_shape=[
             shape((CHIPS, KVROWS, HD), bf16),
             shape((ROWS, GROUPS * SLOTS), bf16),
-        ]
-        + [shape((SLOTS, HD), bf16)] * GROUPS,
-        compiler_params=pltpu.CompilerParams(vmem_limit_bytes=8 << 20),
+            shape((4, SLOTS, HD), bf16),
+            shape((PER * HD + 4 * SLOTS, HD), bf16),
+        ],
         name="prep",
     )(
         queries.reshape(ROWS, HD),
@@ -230,16 +237,16 @@
         value_heads.reshape(SPAN, HD),
         expert_ids,
         gate_logits,
+        out_weight,
     )
-    qgot = [qsend[0]]
-    for d in range(1, GROUPS):
-        moves = [
-            (i, (i // 2 + d // 2) % 4 * 2 + (i + d) % 2) for i in range(GROUPS)
-        ]
-        qgot.append(lax.ppermute(qsend[d], ("x", "zl"), moves))
     kva = lax.all_to_all(kvsend, ("zh", "y"), 0, 0, tiled=True)
-    near = shifted(out_weight, "zl", 2, 1)
-    pair = jnp.concatenate([out_weight, near], axis=0)
+    got = shifted(cargo, "zl", 2, 1)
+    crossed = got[PER * HD :].reshape(4, SLOTS, HD)
+    qpair = jnp.concatenate([qnear, crossed], axis=1)
+    qgot = [qpair[k] for k in range(4)]
+    for k in range(1, 4):
+        qgot[k] = shifted(qgot[k], "x", 4, k)
+    pair = jnp.concatenate([out_weight, got[: PER * HD].reshape(PER, HD, HD)], axis=0)
     pieces = [pair]
     for k in range(1, 4):
         pieces.append(shifted(pair, "x", 4, k))
@@ -249,7 +256,7 @@
     kvb = shifted(kva, "core", 2, 1)
     attended = pl.pallas_call(
         attend_kernel,
-        in_specs=[SMEM] + [VMEM] * 10,
+        in_specs=[SMEM] + [VMEM] * 6,
         out_specs=VMEM,
         out_shape=shape((GROUPS, SLOTS, HD), bf16),
         scratch_shapes=[pltpu.VMEM((16, GROUPS * SLOTS, 4 * SPAN), f32)],
@@ -268,15 +275,15 @@
     rows = lax.all_to_all(rows, ("zh", "y"), 0, 0, tiled=True)
     mine, other = pl.pallas_call(
         project_kernel,
-        in_specs=[SMEM] + [VMEM] * 6 + [ANY] * 4,
+        in_specs=[SMEM] + [VMEM] * 2 + [HBM] * 8,
         out_specs=[VMEM, VMEM],
         out_shape=[shape((CHIPS * TOK, HD), bf16)] * 2,
         scratch_shapes=[
             pltpu.VMEM((GROUPS, CHIPS * TOK, PER * HD), bf16),
-            pltpu.VMEM((4, 2 * PER, HD, HD), bf16),
-            pltpu.SemaphoreType.DMA((4,)),
+            pltpu.VMEM((8, 2 * PER, HD, HD), bf16),
+            pltpu.SemaphoreType.DMA((8,)),
         ],
-        compiler_params=pltpu.CompilerParams(vmem_limit_bytes=20 << 20),
+        compiler_params=pltpu.CompilerParams(vmem_limit_bytes=58 << 20),
         name="project",
     )(at_exp, rows, kva, *pieces, *far)
     got = shifted(other, "core", 2, 1)

time: 190 us -> 147 us (0.77)
  waiting for transfers between devices: 34.6 us -> 10.2 us
  starting transfers between devices: 68.6 us -> 54.9 us
  local copies, waits for them, and re-layouts: 14.8 us -> 2.97 us
  Pallas kernels: 12.6 us -> 16.3 us
  blocking collectives: 57 us -> 59.2 us
    ppermute x7 -> x0, starting transfers between devices: 22.6 us -> none  [run(): qgot.append(lax.ppermute(qsend[d], ('x', 'zl'), moves))]
    ppermute x10 -> x13, waiting for transfers between devices: 31.5 us -> 10.2 us  [shifted(): return lax.ppermute(x, axis, [(i, (i + by) % count) for i in range(count)])]
    unnamed x37 -> x26, local copies, waits for them, and re-layouts: 14.6 us -> 2.77 us
    ppermute x10 -> x13, starting transfers between devices: 41.5 us -> 50.7 us  [shifted(): return lax.ppermute(x, axis, [(i, (i + by) % count) for i in range(count)])]
    pallas_call x3, Pallas kernels: 11.3 us -> 15 us  [the longest x1 7.34 us: run(): pl.pallas_call(project_kernel, in_specs=[SMEM] + [VMEM] * 2 + [HBM] * 8,...]
    ppermute x7 -> x0, waiting for transfers between devices: 3.04 us -> none  [run(): qgot.append(lax.ppermute(qsend[d], ('x', 'zl'), moves))]
  transfers between devices with their start and end apart: 18 -> 14, of which waited for: 4 -> 4; matrix products, arithmetic and copies ran while one was open for 0% -> 1% of each run, Pallas kernels for 0% -> 0%
where the time goes in v2:
time: 147 us; the launch traced here: 146 us
  blocking collectives  59.2 us (40%)
  starting transfers between devices  54.9 us (37%)
  Pallas kernels  16.3 us (11%)
  waiting for transfers between devices  10.2 us (7%)
  local copies, waits for them, and re-layouts  2.97 us (2%)
  other arithmetic  2.38 us (2%)
    ppermute x13, starting transfers between devices, shifted(): return lax.ppermute(x, axis, [(i, (i + by) % count) for i in range(count)])  50.7 us
    all_to_all x1, blocking collectives, run(): kva = lax.all_to_all(kvsend, ('zh', 'y'), 0, 0, tiled=True)  49.6 us
    ppermute x13, waiting for transfers between devices, shifted(): return lax.ppermute(x, axis, [(i, (i + by) % count) for i in range(count)])  10.2 us
    all_to_all x1, blocking collectives, run(): home = lax.all_to_all(attended, ('x', 'zl'), 0, 0, tiled=True)  9.55 us
    pallas_call x1, Pallas kernels, run(): pl.pallas_call(project_kernel, in_specs=[SMEM] + [VMEM] * 2 + [HBM] * 8,...  7.34 us
    pallas_call x1, Pallas kernels, run(): pl.pallas_call(attend_kernel, in_specs=[SMEM] + [VMEM] * 6, out_specs=VME...  4.81 us
    all_to_all x1, starting transfers between devices, run(): rows = lax.all_to_all(rows, ('zh', 'y'), 0, 0, tiled=True)  4.26 us
  transfers between devices with their start and end apart: 14, of which 4 were waited for; matrix products, arithmetic and copies ran while one was open for 1% of the time, Pallas kernels for 0%

profile of v2, /device:TPU:1, one launch (start us, length us, event | category | flops | bytes accessed | tf_op | source)
XLA Modules:
  0.0 146.3 jit_solution(11362905684581698368)
XLA Ops:
  0.0 2.9 %prep.1 = (bf16[32,136,128]{2,1,0:T(8,128)(2,1)}, bf16[128,256]{1,0:T(8,128)(2,1)}, bf16[4,32,128]{2,1,0:T(8,128)(2,1)}, bf16[1152,128]{1,0:T(8,128)(2,1)}) custom-call(bf16[128,128]{1,0:T(8,128)(2,1)} %bitcast.27, bf16[64,128]{1,0:T(8,128)(2,1)} %bitcast.28, bf16[64,128]{1,0:T(8,128)(2,1)} %bitcast.29, s32[8,16]{1,0:T(8,128)} %ids_ref.1, ...), custom_call_target="tpu_custom_call" | custom-call | tf_op jit(solution)/shard_map/prep/pallas_call | solution.py:223
  2.9 49.6 %all_to_all.15.kva_ref.kv_ref = bf16[32,136,128]{2,1,0:T(8,128)(2,1)S(1)} all-to-all(bf16[32,136,128]{2,1,0:T(8,128)(2,1)} %get-tuple-element.12), channel_id=1, replica_groups=mesh['zh'=4,'y'=8,'core'=2,'x'=4,'zl'=2] {'zh','y'}, dimensions={0} | all-to-all | bytes 2228224 | tf_op jit(solution)/shard_map/all_to_all | solution.py:242
  52.5 4.0 %collective-permute-start = (bf16[32,136,128]{2,1,0:T(8,128)(2,1)S(1)}, bf16[32,136,128]{2,1,0:T(8,128)(2,1)S(1)}, u32[]{:S(2)}, u32[]{:S(2)}) collective-permute-start(bf16[32,136,128]{2,1,0:T(8,128)(2,1)S(1)} %all_to_all.15.kva_ref.kv_ref), channel_id=1, source_target_pairs={{0,8},{8,0},{1,9},{9,1},{2,10},{10,2},{3,11},{11,3},{4,12},{12,4},... | collective-permute-start | bytes 3342344 | tf_op jit(solution)/shard_map/ppermute | solution.py:213
  56.5 3.1 %collective-permute-start.1 = (bf16[1152,128]{1,0:T(8,128)(2,1)S(1)}, bf16[1152,128]{1,0:T(8,128)(2,1)S(1)}, u32[]{:S(2)}, u32[]{:S(2)}) collective-permute-start(bf16[1152,128]{1,0:T(8,128)(2,1)S(1)} %copy-done.12), channel_id=1, source_target_pairs={{0,1},{1,0},{2,3},{3,2},{4,5},{5,4},{6,7},{7,6},{8,9},{9,8},{10,11... | collective-permute-start | bytes 884744 | tf_op jit(solution)/shard_map/ppermute | solution.py:213
  59.6 7.3 %collective-permute-done.1 = bf16[1152,128]{1,0:T(8,128)(2,1)S(1)} collective-permute-done((bf16[1152,128]{1,0:T(8,128)(2,1)S(1)}, bf16[1152,128]{1,0:T(8,128)(2,1)S(1)}, u32[]{:S(2)}, u32[]{:S(2)}) %collective-permute-start.1) | collective-permute-done | bytes 294944 | tf_op jit(solution)/shard_map/ppermute | solution.py:213
  67.0 3.1 %collective-permute-start.2 = (bf16[64,128]{1,0:T(8,128)(2,1)S(1)}, bf16[64,128]{1,0:T(8,128)(2,1)S(1)}, u32[]{:S(2)}, u32[]{:S(2)}) collective-permute-start(bf16[64,128]{1,0:T(8,128)(2,1)S(1)} %get-tuple-element.19), channel_id=1, source_target_pairs={{0,2},{2,4},{4,6},{6,0},{1,3},{3,5},{5,7},{7,1},{8,10},{10,12},{12... | collective-permute-start | bytes 49160 | tf_op jit(solution)/shard_map/ppermute | solution.py:213
  70.1 4.4 %collective-permute-start.3 = (bf16[64,128]{1,0:T(8,128)(2,1)S(1)}, bf16[64,128]{1,0:T(8,128)(2,1)S(1)}, u32[]{:S(2)}, u32[]{:S(2)}) collective-permute-start(bf16[64,128]{1,0:T(8,128)(2,1)S(1)} %get-tuple-element.20), channel_id=1, source_target_pairs={{0,4},{2,6},{4,0},{6,2},{1,5},{3,7},{5,1},{7,3},{8,12},{10,14},{12... | collective-permute-start | bytes 49160 | tf_op jit(solution)/shard_map/ppermute | solution.py:213
  74.5 3.1 %collective-permute-start.4 = (bf16[64,128]{1,0:T(8,128)(2,1)S(1)}, bf16[64,128]{1,0:T(8,128)(2,1)S(1)}, u32[]{:S(2)}, u32[]{:S(2)}) collective-permute-start(bf16[64,128]{1,0:T(8,128)(2,1)S(1)} %get-tuple-element.17), channel_id=1, source_target_pairs={{0,6},{2,0},{4,2},{6,4},{1,7},{3,1},{5,3},{7,5},{8,14},{10,8},{12,... | collective-permute-start | bytes 49160 | tf_op jit(solution)/shard_map/ppermute | solution.py:213
  77.6 1.3 collective-permute-done.4.refs_3_
  78.9 4.8 %attend.1 = bf16[8,32,128]{2,1,0:T(8,128)(2,1)S(1)} custom-call(s32[4]{0:T(128)S(1)} %pad_add_fusion.1.at_ref, bf16[32,136,128]{2,1,0:T(8,128)(2,1)S(1)} %all_to_all.15.kva_ref.kv_ref, bf16[32,136,128]{2,1,0:T(8,128)(2,1)S(1)} %collective-permute-done.kvb_ref, bf16[64,128]{1,0:T(8,128)(2,1)S(1)} %get-tuple-element.18.refs_0_, ...), custom_call_target="tpu_custom_call" | custom-call | tf_op jit(solution)/shard_map/attend/pallas_call | solution.py:257
  83.8 9.6 %all_to_all.16.got_ref = bf16[8,32,128]{2,1,0:T(8,128)(2,1)S(1)} all-to-all(bf16[8,32,128]{2,1,0:T(8,128)(2,1)S(1)} %attend.1), channel_id=1, replica_groups=mesh['zh'=4,'y'=8,'core'=2,'x'=4,'zl'=2] {'x','zl'}, dimensions={0} | all-to-all | bytes 131072 | tf_op jit(solution)/shard_map/all_to_all | solution.py:266
  93.3 1.3 compact.1
  94.6 4.3 %all-to-all-start.2 = ((bf16[32,128,128]{2,1,0:T(8,128)(2,1)}), bf16[32,128,128]{2,1,0:T(8,128)(2,1)S(1)}, u32[]{:S(2)}, u32[]{:S(2)}) async-start(bf16[32,128,128]{2,1,0:T(8,128)(2,1)} %compact.1), calls=%async_computation.2 | async-start | bytes 2097152 | tf_op jit(solution)/shard_map/all_to_all | solution.py:275
  99.0 2.9 %collective-permute-start.6 = (bf16[16,128,128]{2,1,0:T(8,128)(2,1)S(1)}, bf16[16,128,128]{2,1,0:T(8,128)(2,1)S(1)}, u32[]{:S(2)}, u32[]{:S(2)}) collective-permute-start(bf16[16,128,128]{2,1,0:T(8,128)(2,1)S(1)} %pad_maximum_fusion.refs_0_), channel_id=1, source_target_pairs={{0,4},{2,6},{4,0},{6,2},{1,5},{3,7},{5,1},{7,3},{8,12},{10,14},{12... | collective-permute-start | bytes 1572872 | tf_op jit(solution)/shard_map/ppermute | solution.py:213
  101.9 3.6 %collective-permute-start.7 = (bf16[16,128,128]{2,1,0:T(8,128)(2,1)S(1)}, bf16[16,128,128]{2,1,0:T(8,128)(2,1)S(1)}, u32[]{:S(2)}, u32[]{:S(2)}) collective-permute-start(bf16[16,128,128]{2,1,0:T(8,128)(2,1)S(1)} %pad_maximum_fusion.refs_0_), channel_id=1, source_target_pairs={{0,6},{2,0},{4,2},{6,4},{1,7},{3,1},{5,3},{7,5},{8,14},{10,8},{12,... | collective-permute-start | bytes 1572872 | tf_op jit(solution)/shard_map/ppermute | solution.py:213
  105.5 1.9 %collective-permute-start.5 = (bf16[16,128,128]{2,1,0:T(8,128)(2,1)S(1)}, bf16[16,128,128]{2,1,0:T(8,128)(2,1)S(1)}, u32[]{:S(2)}, u32[]{:S(2)}) collective-permute-start(bf16[16,128,128]{2,1,0:T(8,128)(2,1)S(1)} %pad_maximum_fusion.refs_0_), channel_id=1, source_target_pairs={{0,2},{2,4},{4,6},{6,0},{1,3},{3,5},{5,7},{7,1},{8,10},{10,12},{12... | collective-permute-start | bytes 1572872 | tf_op jit(solution)/shard_map/ppermute | solution.py:213
  107.4 6.8 %collective-permute-start.8 = (bf16[16,128,128]{2,1,0:T(8,128)(2,1)S(1)}, bf16[16,128,128]{2,1,0:T(8,128)(2,1)S(1)}, u32[]{:S(2)}, u32[]{:S(2)}) collective-permute-start(bf16[16,128,128]{2,1,0:T(8,128)(2,1)S(1)} %pad_maximum_fusion.refs_0_), channel_id=1, source_target_pairs={{0,8},{8,0},{1,9},{9,1},{2,10},{10,2},{3,11},{11,3},{4,12},{12,4},... | collective-permute-start | bytes 1572872 | tf_op jit(solution)/shard_map/ppermute | solution.py:213
  114.3 9.1 %collective-permute-start.10 = (bf16[16,128,128]{2,1,0:T(8,128)(2,1)S(1)}, bf16[16,128,128]{2,1,0:T(8,128)(2,1)S(1)}, u32[]{:S(2)}, u32[]{:S(2)}) collective-permute-start(bf16[16,128,128]{2,1,0:T(8,128)(2,1)S(1)} %collective-permute-done.6.refs_2_), channel_id=1, source_target_pairs={{0,8},{8,0},{1,9},{9,1},{2,10},{10,2},{3,11},{11,3},{4,12},{12,4},... | collective-permute-start | bytes 1572872 | tf_op jit(solution)/shard_map/ppermute | solution.py:213
  123.4 0.6 collective-permute-done.7.refs_3_
  124.0 4.4 %collective-permute-start.11 = (bf16[16,128,128]{2,1,0:T(8,128)(2,1)S(1)}, bf16[16,128,128]{2,1,0:T(8,128)(2,1)S(1)}, u32[]{:S(2)}, u32[]{:S(2)}) collective-permute-start(bf16[16,128,128]{2,1,0:T(8,128)(2,1)S(1)} %collective-permute-done.7.refs_3_), channel_id=1, source_target_pairs={{0,8},{8,0},{1,9},{9,1},{2,10},{10,2},{3,11},{11,3},{4,12},{12,4},... | collective-permute-start | bytes 1572872 | tf_op jit(solution)/shard_map/ppermute | solution.py:213
  128.4 1.9 %collective-permute-start.9 = (bf16[16,128,128]{2,1,0:T(8,128)(2,1)S(1)}, bf16[16,128,128]{2,1,0:T(8,128)(2,1)}, u32[]{:S(2)}, u32[]{:S(2)}) collective-permute-start(bf16[16,128,128]{2,1,0:T(8,128)(2,1)S(1)} %collective-permute-done.5.refs_1_), channel_id=1, source_target_pairs={{0,8},{8,0},{1,9},{9,1},{2,10},{10,2},{3,11},{11,3},{4,12},{12,4},... | collective-permute-start | bytes 1572872 | tf_op jit(solution)/shard_map/ppermute | solution.py:213
  130.4 0.6 pad_add_fusion.at_ref
  131.0 0.8 copy-done.8
  131.8 0.2 copy-done.9
  132.0 0.8 copy-done.10
  132.8 1.0 copy-done.2
  133.8 7.3 %project.1 = (bf16[256,128]{1,0:T(8,128)(2,1)}, bf16[256,128]{1,0:T(8,128)(2,1)}) custom-call(s32[3]{0:T(128)} %pad_add_fusion.at_ref, bf16[32,128,128]{2,1,0:T(8,128)(2,1)} %copy-done.2, bf16[32,136,128]{2,1,0:T(8,128)(2,1)} %copy-done, bf16[16,128,128]{2,1,0:T(8,128)(2,1)} %copy-done.3, bf16[16,128,128]{2,1,0:T(8,128)(2,1)} %copy-done.7, ...), custom_call_target="tpu_custom_call" | custom-call | tf_op jit(solution)/shard_map/project/pallas_call | solution.py:276
  141.1 2.4 %collective-permute-start.12 = (bf16[256,128]{1,0:T(8,128)(2,1)}, bf16[256,128]{1,0:T(8,128)(2,1)S(1)}, u32[]{:S(2)}, u32[]{:S(2)}) collective-permute-start(bf16[256,128]{1,0:T(8,128)(2,1)} %get-tuple-element.16), channel_id=1, source_target_pairs={{0,8},{8,0},{1,9},{9,1},{2,10},{10,2},{3,11},{11,3},{4,12},{12,4},... | collective-permute-start | bytes 196616 | tf_op jit(solution)/shard_map/ppermute | solution.py:213
  143.6 0.1 iota.11
  143.6 0.1 iota.12
  143.7 0.9 collective-permute-done.12
  144.6 1.6 %bitcast_select_fusion = bf16[512,128]{1,0:T(8,128)(2,1)} fusion(pred[512]{0:T(512)(128)(4,1)S(1)} %iota.12, bf16[32,8,128]{2,1,0:T(8,128)(2,1)S(1)} %bitcast.26, bf16[32,8,128]{2,1,0:T(8,128)(2,1)} %bitcast.25), kind=kLoop, calls=%fused_computation.1 | loop fusion | flops 65536 | bytes 262656 | tf_op jit(solution)/shard_map/jit(_where)/select_n | solution.py:293
  (38 shorter events, 0.2 us)
Async XLA Ops:
  2.9 53.6 %copy-start.12 = (bf16[1152,128]{1,0:T(8,128)(2,1)S(1)}, bf16[1152,128]{1,0:T(8,128)(2,1)}, u32[]{:S(2)}) copy-start(bf16[1152,128]{1,0:T(8,128)(2,1)} %get-tuple-element.14) | copy-start | bytes 884740
  2.9 64.1 %copy-start.11 = (bf16[4,32,128]{2,1,0:T(8,128)(2,1)S(1)}, bf16[4,32,128]{2,1,0:T(8,128)(2,1)}, u32[]{:S(2)}) copy-start(bf16[4,32,128]{2,1,0:T(8,128)(2,1)} %get-tuple-element.13) | copy-start | bytes 98308
  52.5 31.3 %copy-start = (bf16[32,136,128]{2,1,0:T(8,128)(2,1)}, bf16[32,136,128]{2,1,0:T(8,128)(2,1)S(1)}, u32[]{:S(2)}) copy-start(bf16[32,136,128]{2,1,0:T(8,128)(2,1)S(1)} %all_to_all.15.kva_ref.kv_ref) | copy-start | bytes 3342340
  52.5 26.4 %collective-permute-start = (bf16[32,136,128]{2,1,0:T(8,128)(2,1)S(1)}, bf16[32,136,128]{2,1,0:T(8,128)(2,1)S(1)}, u32[]{:S(2)}, u32[]{:S(2)}) collective-permute-start(bf16[32,136,128]{2,1,0:T(8,128)(2,1)S(1)} %all_to_all.15.kva_ref.kv_ref), channel_id=1, source_target_pairs={{0,8},{8,0},{1,9},{9,1},{2,10},{10,2},{3,11},{11,3},{4,12},{12,4},... | collective-permute-start | bytes 3342344 | tf_op jit(solution)/shard_map/ppermute | solution.py:213
  56.5 10.4 %collective-permute-start.1 = (bf16[1152,128]{1,0:T(8,128)(2,1)S(1)}, bf16[1152,128]{1,0:T(8,128)(2,1)S(1)}, u32[]{:S(2)}, u32[]{:S(2)}) collective-permute-start(bf16[1152,128]{1,0:T(8,128)(2,1)S(1)} %copy-done.12), channel_id=1, source_target_pairs={{0,1},{1,0},{2,3},{3,2},{4,5},{5,4},{6,7},{7,6},{8,9},{9,8},{10,11... | collective-permute-start | bytes 884744 | tf_op jit(solution)/shard_map/ppermute | solution.py:213
  67.0 10.6 %collective-permute-start.2 = (bf16[64,128]{1,0:T(8,128)(2,1)S(1)}, bf16[64,128]{1,0:T(8,128)(2,1)S(1)}, u32[]{:S(2)}, u32[]{:S(2)}) collective-permute-start(bf16[64,128]{1,0:T(8,128)(2,1)S(1)} %get-tuple-element.19), channel_id=1, source_target_pairs={{0,2},{2,4},{4,6},{6,0},{1,3},{3,5},{5,7},{7,1},{8,10},{10,12},{12... | collective-permute-start | bytes 49160 | tf_op jit(solution)/shard_map/ppermute | solution.py:213
  70.1 7.5 %collective-permute-start.3 = (bf16[64,128]{1,0:T(8,128)(2,1)S(1)}, bf16[64,128]{1,0:T(8,128)(2,1)S(1)}, u32[]{:S(2)}, u32[]{:S(2)}) collective-permute-start(bf16[64,128]{1,0:T(8,128)(2,1)S(1)} %get-tuple-element.20), channel_id=1, source_target_pairs={{0,4},{2,6},{4,0},{6,2},{1,5},{3,7},{5,1},{7,3},{8,12},{10,14},{12... | collective-permute-start | bytes 49160 | tf_op jit(solution)/shard_map/ppermute | solution.py:213
  74.5 4.5 %collective-permute-start.4 = (bf16[64,128]{1,0:T(8,128)(2,1)S(1)}, bf16[64,128]{1,0:T(8,128)(2,1)S(1)}, u32[]{:S(2)}, u32[]{:S(2)}) collective-permute-start(bf16[64,128]{1,0:T(8,128)(2,1)S(1)} %get-tuple-element.17), channel_id=1, source_target_pairs={{0,6},{2,0},{4,2},{6,4},{1,7},{3,1},{5,3},{7,5},{8,14},{10,8},{12,... | collective-permute-start | bytes 49160 | tf_op jit(solution)/shard_map/ppermute | solution.py:213
  78.9 14.4 %copy-start.1 = (bf16[128,256]{1,0:T(8,128)(2,1)S(1)}, bf16[128,256]{1,0:T(8,128)(2,1)}, u32[]{:S(2)}) copy-start(bf16[128,256]{1,0:T(8,128)(2,1)} %get-tuple-element.11.back_ref) | copy-start | bytes 196612
  94.6 4.3 %copy-start.4 = (bf16[8,128,128]{2,1,0:T(8,128)(2,1)S(1)}, bf16[8,128,128]{2,1,0:T(8,128)(2,1)}, u32[]{:S(2)}) copy-start(bf16[8,128,128]{2,1,0:T(8,128)(2,1)} %w_ref.1) | copy-start | bytes 786436
  94.6 38.2 %all-to-all-start.2 = ((bf16[32,128,128]{2,1,0:T(8,128)(2,1)}), bf16[32,128,128]{2,1,0:T(8,128)(2,1)S(1)}, u32[]{:S(2)}, u32[]{:S(2)}) async-start(bf16[32,128,128]{2,1,0:T(8,128)(2,1)} %compact.1), calls=%async_computation.2 | async-start | bytes 2097152 | tf_op jit(solution)/shard_map/all_to_all | solution.py:275
  99.0 33.8 %copy-start.3 = (bf16[16,128,128]{2,1,0:T(8,128)(2,1)}, bf16[16,128,128]{2,1,0:T(8,128)(2,1)S(1)}, u32[]{:S(2)}) copy-start(bf16[16,128,128]{2,1,0:T(8,128)(2,1)S(1)} %pad_maximum_fusion.refs_0_) | copy-start | bytes 1572868
  99.0 15.3 %collective-permute-start.6 = (bf16[16,128,128]{2,1,0:T(8,128)(2,1)S(1)}, bf16[16,128,128]{2,1,0:T(8,128)(2,1)S(1)}, u32[]{:S(2)}, u32[]{:S(2)}) collective-permute-start(bf16[16,128,128]{2,1,0:T(8,128)(2,1)S(1)} %pad_maximum_fusion.refs_0_), channel_id=1, source_target_pairs={{0,4},{2,6},{4,0},{6,2},{1,5},{3,7},{5,1},{7,3},{8,12},{10,14},{12... | collective-permute-start | bytes 1572872 | tf_op jit(solution)/shard_map/ppermute | solution.py:213
  101.9 22.1 %collective-permute-start.7 = (bf16[16,128,128]{2,1,0:T(8,128)(2,1)S(1)}, bf16[16,128,128]{2,1,0:T(8,128)(2,1)S(1)}, u32[]{:S(2)}, u32[]{:S(2)}) collective-permute-start(bf16[16,128,128]{2,1,0:T(8,128)(2,1)S(1)} %pad_maximum_fusion.refs_0_), channel_id=1, source_target_pairs={{0,6},{2,0},{4,2},{6,4},{1,7},{3,1},{5,3},{7,5},{8,14},{10,8},{12,... | collective-permute-start | bytes 1572872 | tf_op jit(solution)/shard_map/ppermute | solution.py:213
  105.5 22.9 %collective-permute-start.5 = (bf16[16,128,128]{2,1,0:T(8,128)(2,1)S(1)}, bf16[16,128,128]{2,1,0:T(8,128)(2,1)S(1)}, u32[]{:S(2)}, u32[]{:S(2)}) collective-permute-start(bf16[16,128,128]{2,1,0:T(8,128)(2,1)S(1)} %pad_maximum_fusion.refs_0_), channel_id=1, source_target_pairs={{0,2},{2,4},{4,6},{6,0},{1,3},{3,5},{5,7},{7,1},{8,10},{10,12},{12... | collective-permute-start | bytes 1572872 | tf_op jit(solution)/shard_map/ppermute | solution.py:213
  107.4 23.5 %collective-permute-start.8 = (bf16[16,128,128]{2,1,0:T(8,128)(2,1)S(1)}, bf16[16,128,128]{2,1,0:T(8,128)(2,1)S(1)}, u32[]{:S(2)}, u32[]{:S(2)}) collective-permute-start(bf16[16,128,128]{2,1,0:T(8,128)(2,1)S(1)} %pad_maximum_fusion.refs_0_), channel_id=1, source_target_pairs={{0,8},{8,0},{1,9},{9,1},{2,10},{10,2},{3,11},{11,3},{4,12},{12,4},... | collective-permute-start | bytes 1572872 | tf_op jit(solution)/shard_map/ppermute | solution.py:213
  114.3 18.5 %copy-start.5 = (bf16[16,128,128]{2,1,0:T(8,128)(2,1)}, bf16[16,128,128]{2,1,0:T(8,128)(2,1)S(1)}, u32[]{:S(2)}) copy-start(bf16[16,128,128]{2,1,0:T(8,128)(2,1)S(1)} %collective-permute-done.6.refs_2_) | copy-start | bytes 1572868
  114.3 16.7 %collective-permute-start.10 = (bf16[16,128,128]{2,1,0:T(8,128)(2,1)S(1)}, bf16[16,128,128]{2,1,0:T(8,128)(2,1)S(1)}, u32[]{:S(2)}, u32[]{:S(2)}) collective-permute-start(bf16[16,128,128]{2,1,0:T(8,128)(2,1)S(1)} %collective-permute-done.6.refs_2_), channel_id=1, source_target_pairs={{0,8},{8,0},{1,9},{9,1},{2,10},{10,2},{3,11},{11,3},{4,12},{12,4},... | collective-permute-start | bytes 1572872 | tf_op jit(solution)/shard_map/ppermute | solution.py:213
  124.0 8.8 %copy-start.6 = (bf16[16,128,128]{2,1,0:T(8,128)(2,1)}, bf16[16,128,128]{2,1,0:T(8,128)(2,1)S(1)}, u32[]{:S(2)}) copy-start(bf16[16,128,128]{2,1,0:T(8,128)(2,1)S(1)} %collective-permute-done.7.refs_3_) | copy-start | bytes 1572868
  124.0 7.0 %collective-permute-start.11 = (bf16[16,128,128]{2,1,0:T(8,128)(2,1)S(1)}, bf16[16,128,128]{2,1,0:T(8,128)(2,1)S(1)}, u32[]{:S(2)}, u32[]{:S(2)}) collective-permute-start(bf16[16,128,128]{2,1,0:T(8,128)(2,1)S(1)} %collective-permute-done.7.refs_3_), channel_id=1, source_target_pairs={{0,8},{8,0},{1,9},{9,1},{2,10},{10,2},{3,11},{11,3},{4,12},{12,4},... | collective-permute-start | bytes 1572872 | tf_op jit(solution)/shard_map/ppermute | solution.py:213
  128.4 4.4 %copy-start.7 = (bf16[16,128,128]{2,1,0:T(8,128)(2,1)}, bf16[16,128,128]{2,1,0:T(8,128)(2,1)S(1)}, u32[]{:S(2)}) copy-start(bf16[16,128,128]{2,1,0:T(8,128)(2,1)S(1)} %collective-permute-done.5.refs_1_) | copy-start | bytes 1572868
  128.4 4.3 %collective-permute-start.9 = (bf16[16,128,128]{2,1,0:T(8,128)(2,1)S(1)}, bf16[16,128,128]{2,1,0:T(8,128)(2,1)}, u32[]{:S(2)}, u32[]{:S(2)}) collective-permute-start(bf16[16,128,128]{2,1,0:T(8,128)(2,1)S(1)} %collective-permute-done.5.refs_1_), channel_id=1, source_target_pairs={{0,8},{8,0},{1,9},{9,1},{2,10},{10,2},{3,11},{11,3},{4,12},{12,4},... | collective-permute-start | bytes 1572872 | tf_op jit(solution)/shard_map/ppermute | solution.py:213
  131.0 0.8 copy-start.8
  131.0 1.0 copy-start.9
  132.0 0.8 copy-start.10
  132.8 1.0 copy-start.2
  141.1 3.5 %collective-permute-start.12 = (bf16[256,128]{1,0:T(8,128)(2,1)}, bf16[256,128]{1,0:T(8,128)(2,1)S(1)}, u32[]{:S(2)}, u32[]{:S(2)}) collective-permute-start(bf16[256,128]{1,0:T(8,128)(2,1)} %get-tuple-element.16), channel_id=1, source_target_pairs={{0,8},{8,0},{1,9},{9,1},{2,10},{10,2},{3,11},{11,3},{4,12},{12,4},... | collective-permute-start | bytes 196616 | tf_op jit(solution)/shard_map/ppermute | solution.py:213

commit v3 on v2

--- a/solution.py
+++ b/solution.py
@@ -130,7 +130,9 @@
         best = score(i, best, kva_ref, core, 0)
         return score(i, best, kvb_ref, 1 - core, steps)
 
-    best = lax.fori_loop(0, steps, score_both, jnp.full((n, HD), NEG_FLOOR, f32))
+    best = lax.fori_loop(
+        0, steps, score_both, jnp.full((n, HD), NEG_FLOOR, f32), unroll=4
+    )
     best = jnp.max(best, axis=1, keepdims=True)
 
     def weigh(i, carried, kv_ref, base):
@@ -144,7 +146,7 @@
         return weigh(i, weigh(i, carried, kva_ref, 0), kvb_ref, steps)
 
     zero = jnp.zeros((n, HD), f32)
-    total, acc = lax.fori_loop(0, steps, weigh_both, (zero, zero))
+    total, acc = lax.fori_loop(0, steps, weigh_both, (zero, zero), unroll=4)
     total = jnp.sum(total, axis=1, keepdims=True)
     result = (gate * (acc / total)).astype(bf16)
     for d in range(GROUPS):
@@ -164,8 +166,8 @@
 
 
 def project_kernel(at_ref, rows_ref, kv_ref, *refs):
-    mine_ref, other_ref, a_ref, w_ref, sems = refs[8:]
-    copies = [pltpu.make_async_copy(refs[k], w_ref.at[k], sems.at[k]) for k in range(8)]
+    mine_ref, other_ref, a_ref, w_ref, sems = refs[2:]
+    copies = [pltpu.make_async_copy(refs[k], w_ref.at[k], sems.at[k]) for k in range(2)]
     for copy in copies:
         copy.start()
     x = at_ref[0]
@@ -189,15 +191,15 @@
             a_ref[e // PER, at, (e % PER) * HD : (e % PER + 1) * HD] = both[e]
         return 0
 
-    lax.fori_loop(0, CHIPS // 2, fill, 0)
+    lax.fori_loop(0, CHIPS // 2, fill, 0, unroll=4)
 
     for copy in copies:
         copy.wait()
     total = jnp.zeros((CHIPS * TOK, 2 * HD), f32)
     for piece in range(GROUPS):
-        part = slice(piece % 2 * PER, (piece % 2 + 1) * PER)
-        near = w_ref[piece // 2, part].reshape(PER * HD, HD)
-        far = w_ref[4 + piece // 2, part].reshape(PER * HD, HD)
+        part = slice(piece * PER, (piece + 1) * PER)
+        near = w_ref[0, part].reshape(PER * HD, HD)
+        far = w_ref[1, part].reshape(PER * HD, HD)
         weight = jnp.concatenate([near, far], axis=1)
         total = total + jnp.dot(a_ref[piece], weight, preferred_element_type=f32)
     mine_ref[...] = total[:, :HD].astype(bf16)
@@ -250,9 +252,8 @@
     pieces = [pair]
     for k in range(1, 4):
         pieces.append(shifted(pair, "x", 4, k))
-    far = []
-    for k in range(4):
-        far.append(shifted(pieces[k], "core", 2, 1))
+    near = jnp.concatenate(pieces, axis=0)
+    far = shifted(near, "core", 2, 1)
     kvb = shifted(kva, "core", 2, 1)
     attended = pl.pallas_call(
         attend_kernel,
@@ -275,17 +276,17 @@
     rows = lax.all_to_all(rows, ("zh", "y"), 0, 0, tiled=True)
     mine, other = pl.pallas_call(
         project_kernel,
-        in_specs=[SMEM] + [VMEM] * 2 + [HBM] * 8,
+        in_specs=[SMEM] + [VMEM] * 2 + [HBM] * 2,
         out_specs=[VMEM, VMEM],
         out_shape=[shape((CHIPS * TOK, HD), bf16)] * 2,
         scratch_shapes=[
             pltpu.VMEM((GROUPS, CHIPS * TOK, PER * HD), bf16),
-            pltpu.VMEM((8, 2 * PER, HD, HD), bf16),
-            pltpu.SemaphoreType.DMA((8,)),
+            pltpu.VMEM((2, EXPERTS, HD, HD), bf16),
+            pltpu.SemaphoreType.DMA((2,)),
         ],
-        compiler_params=pltpu.CompilerParams(vmem_limit_bytes=58 << 20),
+        compiler_params=pltpu.CompilerParams(vmem_limit_bytes=50 << 20),
         name="project",
-    )(at_exp, rows, kva, *pieces, *far)
+    )(at_exp, rows, kva, near, far)
     got = shifted(other, "core", 2, 1)
     own = lax.broadcasted_iota(jnp.int32, (CHIPS, 2, TOK, HD), 1) == core
     mine = mine.reshape(CHIPS, 1, TOK, HD)

time: 147 us -> 155 us (1.054)
  blocking collectives: 59.2 us -> 0 us
  waiting for transfers between devices: 10.2 us -> 59.9 us
  starting transfers between devices: 54.9 us -> 71.4 us
  local copies, waits for them, and re-layouts: 2.97 us -> 8.76 us
  Pallas kernels: 16.3 us -> 11.7 us
    all_to_all x2 -> x0, blocking collectives: 59.2 us -> none  [the longest x1 49.6 us: run(): kva = lax.all_to_all(kvsend, ('zh', 'y'), 0, 0, tiled=True)]
    all_to_all x1, waiting for transfers between devices: 0.01 us -> 25.1 us  [run(): rows = lax.all_to_all(rows, ('zh', 'y'), 0, 0, tiled=True)]
    all_to_all x0 -> x2, waiting for transfers between devices: none -> 24.8 us  [the longest x1 24.8 us: run(): kva = lax.all_to_all(kvsend, ('zh', 'y'), 0, 0, tiled=True)]
    all_to_all x0 -> x2, starting transfers between devices: none -> 20 us  [the longest x1 16.6 us: run(): kva = lax.all_to_all(kvsend, ('zh', 'y'), 0, 0, tiled=True)]
    ppermute x13 -> x10, starting transfers between devices: 50.7 us -> 42.9 us  [shifted(): return lax.ppermute(x, axis, [(i, (i + by) % count) for i in range(count)])]
    all_to_all x1, starting transfers between devices: 4.26 us -> 8.52 us  [run(): rows = lax.all_to_all(rows, ('zh', 'y'), 0, 0, tiled=True)]
    pallas_call x1, Pallas kernels: 7.34 us -> 4.03 us  [run(): pl.pallas_call(project_kernel, in_specs=[SMEM] + [VMEM] * 2 + [HBM] * 2,...]
    unnamed x26 -> x14, local copies, waits for them, and re-layouts: 2.77 us -> 5.89 us
  transfers between devices with their start and end apart: 14 -> 13, of which waited for: 4 -> 6; matrix products, arithmetic and copies ran while one was open for 1% -> 5% of each run, Pallas kernels for 0% -> 3%
where the time goes in v3:
time: 155 us; the launch traced here: 153 us
  starting transfers between devices  71.4 us (46%)
  waiting for transfers between devices  59.9 us (39%)
  Pallas kernels  11.7 us (8%)
  local copies, waits for them, and re-layouts  8.76 us (6%)
    ppermute x10, starting transfers between devices, shifted(): return lax.ppermute(x, axis, [(i, (i + by) % count) for i in range(count)])  42.9 us
    all_to_all x1, waiting for transfers between devices, run(): rows = lax.all_to_all(rows, ('zh', 'y'), 0, 0, tiled=True)  25.1 us
    all_to_all x1, waiting for transfers between devices, run(): kva = lax.all_to_all(kvsend, ('zh', 'y'), 0, 0, tiled=True)  24.8 us
    all_to_all x1, starting transfers between devices, run(): kva = lax.all_to_all(kvsend, ('zh', 'y'), 0, 0, tiled=True)  16.6 us
    ppermute x10, waiting for transfers between devices, shifted(): return lax.ppermute(x, axis, [(i, (i + by) % count) for i in range(count)])  10 us
    all_to_all x1, starting transfers between devices, run(): rows = lax.all_to_all(rows, ('zh', 'y'), 0, 0, tiled=True)  8.52 us
    unnamed x14, local copies, waits for them, and re-layouts  5.89 us
    pallas_call x1, Pallas kernels, run(): pl.pallas_call(project_kernel, in_specs=[SMEM] + [VMEM] * 2 + [HBM] * 2,...  4.03 us
  transfers between devices with their start and end apart: 13, of which 6 were waited for; matrix products, arithmetic and copies ran while one was open for 5% of the time, Pallas kernels for 3%

profile of v3, /device:TPU:1, one launch (start us, length us, event | category | flops | bytes accessed | tf_op | source)
XLA Modules:
  0.0 153.0 jit_solution(13926185623453134661)
XLA Ops:
  0.0 2.9 %prep.1 = (bf16[32,136,128]{2,1,0:T(8,128)(2,1)}, bf16[128,256]{1,0:T(8,128)(2,1)}, bf16[4,32,128]{2,1,0:T(8,128)(2,1)}, bf16[1152,128]{1,0:T(8,128)(2,1)}) custom-call(bf16[128,128]{1,0:T(8,128)(2,1)} %bitcast.28, bf16[64,128]{1,0:T(8,128)(2,1)} %bitcast.29, bf16[64,128]{1,0:T(8,128)(2,1)} %bitcast.30, s32[8,16]{1,0:T(8,128)} %ids_ref.1, ...), custom_call_target="tpu_custom_call" | custom-call | tf_op jit(solution)/shard_map/prep/pallas_call | solution.py:225
  2.9 16.6 %all-to-all-start = ((bf16[32,136,128]{2,1,0:T(8,128)(2,1)}), bf16[32,136,128]{2,1,0:T(8,128)(2,1)S(1)}, u32[]{:S(2)}, u32[]{:S(2)}) async-start(bf16[32,136,128]{2,1,0:T(8,128)(2,1)} %get-tuple-element.12), calls=%async_computation | async-start | bytes 2228224 | tf_op jit(solution)/shard_map/all_to_all | solution.py:244
  19.6 3.1 %collective-permute-start.1 = (bf16[1152,128]{1,0:T(8,128)(2,1)S(1)}, bf16[1152,128]{1,0:T(8,128)(2,1)S(1)}, u32[]{:S(2)}, u32[]{:S(2)}) collective-permute-start(bf16[1152,128]{1,0:T(8,128)(2,1)S(1)} %copy-done.4), channel_id=1, source_target_pairs={{0,1},{1,0},{2,3},{3,2},{4,5},{5,4},{6,7},{7,6},{8,9},{9,8},{10,11... | collective-permute-start | bytes 884744 | tf_op jit(solution)/shard_map/ppermute | solution.py:215
  22.7 24.8 %all-to-all-done.kva_ref.kv_ref = bf16[32,136,128]{2,1,0:T(8,128)(2,1)S(1)} async-done(((bf16[32,136,128]{2,1,0:T(8,128)(2,1)}), bf16[32,136,128]{2,1,0:T(8,128)(2,1)S(1)}, u32[]{:S(2)}, u32[]{:S(2)}) %all-to-all-start) | async-done | bytes 1114144 | tf_op jit(solution)/shard_map/all_to_all | solution.py:244
  47.5 6.0 %collective-permute-start = (bf16[32,136,128]{2,1,0:T(8,128)(2,1)S(1)}, bf16[32,136,128]{2,1,0:T(8,128)(2,1)S(1)}, u32[]{:S(2)}, u32[]{:S(2)}) collective-permute-start(bf16[32,136,128]{2,1,0:T(8,128)(2,1)S(1)} %all-to-all-done.kva_ref.kv_ref), channel_id=1, source_target_pairs={{0,8},{8,0},{1,9},{9,1},{2,10},{10,2},{3,11},{11,3},{4,12},{12,4},... | collective-permute-start | bytes 3342344 | tf_op jit(solution)/shard_map/ppermute | solution.py:215
  53.5 0.7 copy-done.2
  54.2 3.1 %collective-permute-start.5 = (bf16[16,128,128]{2,1,0:T(8,128)(2,1)S(1)}, bf16[16,128,128]{2,1,0:T(8,128)(2,1)}, u32[]{:S(2)}, u32[]{:S(2)}) collective-permute-start(bf16[16,128,128]{2,1,0:T(8,128)(2,1)S(1)} %pad_maximum_fusion), channel_id=1, source_target_pairs={{0,2},{2,4},{4,6},{6,0},{1,3},{3,5},{5,7},{7,1},{8,10},{10,12},{12... | collective-permute-start | bytes 1572872 | tf_op jit(solution)/shard_map/ppermute | solution.py:215
  57.3 4.4 %collective-permute-start.6 = (bf16[16,128,128]{2,1,0:T(8,128)(2,1)S(1)}, bf16[16,128,128]{2,1,0:T(8,128)(2,1)}, u32[]{:S(2)}, u32[]{:S(2)}) collective-permute-start(bf16[16,128,128]{2,1,0:T(8,128)(2,1)S(1)} %pad_maximum_fusion), channel_id=1, source_target_pairs={{0,4},{2,6},{4,0},{6,2},{1,5},{3,7},{5,1},{7,3},{8,12},{10,14},{12... | collective-permute-start | bytes 1572872 | tf_op jit(solution)/shard_map/ppermute | solution.py:215
  61.7 0.7 constant_dynamic-update-slice_fusion.4
  62.4 3.1 %collective-permute-start.7 = (bf16[16,128,128]{2,1,0:T(8,128)(2,1)S(1)}, bf16[16,128,128]{2,1,0:T(8,128)(2,1)}, u32[]{:S(2)}, u32[]{:S(2)}) collective-permute-start(bf16[16,128,128]{2,1,0:T(8,128)(2,1)S(1)} %pad_maximum_fusion), channel_id=1, source_target_pairs={{0,6},{2,0},{4,2},{6,4},{1,7},{3,1},{5,3},{7,5},{8,14},{10,8},{12,... | collective-permute-start | bytes 1572872 | tf_op jit(solution)/shard_map/ppermute | solution.py:215
  65.6 0.8 slice.24
  66.3 2.2 %collective-permute-start.2 = (bf16[64,128]{1,0:T(8,128)(2,1)S(1)}, bf16[64,128]{1,0:T(8,128)(2,1)S(1)}, u32[]{:S(2)}, u32[]{:S(2)}) collective-permute-start(bf16[64,128]{1,0:T(8,128)(2,1)S(1)} %get-tuple-element.19), channel_id=1, source_target_pairs={{0,2},{2,4},{4,6},{6,0},{1,3},{3,5},{5,7},{7,1},{8,10},{10,12},{12... | collective-permute-start | bytes 49160 | tf_op jit(solution)/shard_map/ppermute | solution.py:215
  68.6 0.7 constant_dynamic-update-slice_fusion.3
  69.3 1.6 %collective-permute-done.5 = bf16[16,128,128]{2,1,0:T(8,128)(2,1)} collective-permute-done((bf16[16,128,128]{2,1,0:T(8,128)(2,1)S(1)}, bf16[16,128,128]{2,1,0:T(8,128)(2,1)}, u32[]{:S(2)}, u32[]{:S(2)}) %collective-permute-start.5) | collective-permute-done | bytes 524320 | tf_op jit(solution)/shard_map/ppermute | solution.py:215
  70.9 3.5 %collective-permute-start.3 = (bf16[64,128]{1,0:T(8,128)(2,1)S(1)}, bf16[64,128]{1,0:T(8,128)(2,1)S(1)}, u32[]{:S(2)}, u32[]{:S(2)}) collective-permute-start(bf16[64,128]{1,0:T(8,128)(2,1)S(1)} %get-tuple-element.20), channel_id=1, source_target_pairs={{0,4},{2,6},{4,0},{6,2},{1,5},{3,7},{5,1},{7,3},{8,12},{10,14},{12... | collective-permute-start | bytes 49160 | tf_op jit(solution)/shard_map/ppermute | solution.py:215
  74.3 1.9 %constant_dynamic-update-slice_fusion.2 = bf16[64,128,128]{2,1,0:T(8,128)(2,1)} fusion(bf16[64,128,128]{2,1,0:T(8,128)(2,1)} %constant_dynamic-update-slice_fusion.3, bf16[16,128,128]{2,1,0:T(8,128)(2,1)} %collective-permute-done.5), kind=kLoop, calls=%fused_computation.18 | loop fusion | bytes 1048576
  76.2 6.9 %collective-permute-done.6 = bf16[16,128,128]{2,1,0:T(8,128)(2,1)} collective-permute-done((bf16[16,128,128]{2,1,0:T(8,128)(2,1)S(1)}, bf16[16,128,128]{2,1,0:T(8,128)(2,1)}, u32[]{:S(2)}, u32[]{:S(2)}) %collective-permute-start.6) | collective-permute-done | bytes 524320 | tf_op jit(solution)/shard_map/ppermute | solution.py:215
  83.2 2.0 %collective-permute-start.4 = (bf16[64,128]{1,0:T(8,128)(2,1)S(1)}, bf16[64,128]{1,0:T(8,128)(2,1)S(1)}, u32[]{:S(2)}, u32[]{:S(2)}) collective-permute-start(bf16[64,128]{1,0:T(8,128)(2,1)S(1)} %get-tuple-element.17), channel_id=1, source_target_pairs={{0,6},{2,0},{4,2},{6,4},{1,7},{3,1},{5,3},{7,5},{8,14},{10,8},{12,... | collective-permute-start | bytes 49160 | tf_op jit(solution)/shard_map/ppermute | solution.py:215
  85.2 1.9 %constant_dynamic-update-slice_fusion.1 = bf16[64,128,128]{2,1,0:T(8,128)(2,1)} fusion(bf16[64,128,128]{2,1,0:T(8,128)(2,1)} %constant_dynamic-update-slice_fusion.2, bf16[16,128,128]{2,1,0:T(8,128)(2,1)} %collective-permute-done.6), kind=kLoop, calls=%fused_computation.17 | loop fusion | bytes 1048576
  87.1 0.8 collective-permute-done.4.refs_3_
  87.9 3.5 %attend.1 = bf16[8,32,128]{2,1,0:T(8,128)(2,1)} custom-call(s32[4]{0:T(128)S(1)} %pad_add_fusion.1.at_ref, bf16[32,136,128]{2,1,0:T(8,128)(2,1)S(1)} %all-to-all-done.kva_ref.kv_ref, bf16[32,136,128]{2,1,0:T(8,128)(2,1)S(1)} %collective-permute-done.kvb_ref, bf16[64,128]{1,0:T(8,128)(2,1)S(1)} %get-tuple-element.18.refs_0_, ...), custom_call_target="tpu_custom_call" | custom-call | tf_op jit(solution)/shard_map/attend/pallas_call | solution.py:258
  91.4 3.3 %all-to-all-start.1 = ((bf16[8,32,128]{2,1,0:T(8,128)(2,1)}), bf16[8,32,128]{2,1,0:T(8,128)(2,1)S(1)}, u32[]{:S(2)}, u32[]{:S(2)}) async-start(bf16[8,32,128]{2,1,0:T(8,128)(2,1)} %attend.1), calls=%async_computation.1 | async-start | bytes 131072 | tf_op jit(solution)/shard_map/all_to_all | solution.py:267
  94.7 1.9 %constant_dynamic-update-slice_fusion.refs_0_ = bf16[64,128,128]{2,1,0:T(8,128)(2,1)} fusion(bf16[64,128,128]{2,1,0:T(8,128)(2,1)} %constant_dynamic-update-slice_fusion.1, bf16[16,128,128]{2,1,0:T(8,128)(2,1)} %collective-permute-done.7), kind=kLoop, calls=%fused_computation.16 | loop fusion | bytes 1048576 | tf_op jit(solution)/shard_map/concatenate | solution.py:255
  96.6 8.3 %collective-permute-start.8 = (bf16[64,128,128]{2,1,0:T(8,128)(2,1)}, bf16[64,128,128]{2,1,0:T(8,128)(2,1)}, u32[]{:S(2)}, u32[]{:S(2)}) collective-permute-start(bf16[64,128,128]{2,1,0:T(8,128)(2,1)} %constant_dynamic-update-slice_fusion.refs_0_), channel_id=1, source_target_pairs={{0,8},{8,0},{1,9},{9,1},{2,10},{10,2},{3,11},{11,3},{4,12},{12,4},... | collective-permute-start | bytes 6291464 | tf_op jit(solution)/shard_map/ppermute | solution.py:215
  105.0 1.3 compact.1
  106.3 8.5 %all-to-all-start.2 = ((bf16[32,128,128]{2,1,0:T(8,128)(2,1)}), bf16[32,128,128]{2,1,0:T(8,128)(2,1)S(1)}, u32[]{:S(2)}, u32[]{:S(2)}) async-start(bf16[32,128,128]{2,1,0:T(8,128)(2,1)} %compact.1), calls=%async_computation.2 | async-start | bytes 2097152 | tf_op jit(solution)/shard_map/all_to_all | solution.py:276
  114.9 25.1 %all-to-all-done.2.rows_ref = bf16[32,128,128]{2,1,0:T(8,128)(2,1)S(1)} async-done(((bf16[32,128,128]{2,1,0:T(8,128)(2,1)}), bf16[32,128,128]{2,1,0:T(8,128)(2,1)S(1)}, u32[]{:S(2)}, u32[]{:S(2)}) %all-to-all-start.2) | async-done | bytes 1048608 | tf_op jit(solution)/shard_map/all_to_all | solution.py:276
  140.0 4.0 %project.1 = (bf16[256,128]{1,0:T(8,128)(2,1)S(1)}, bf16[256,128]{1,0:T(8,128)(2,1)S(1)}) custom-call(s32[3]{0:T(128)S(1)} %pad_add_fusion.at_ref, bf16[32,128,128]{2,1,0:T(8,128)(2,1)S(1)} %all-to-all-done.2.rows_ref, bf16[32,136,128]{2,1,0:T(8,128)(2,1)S(1)} %all-to-all-done.kva_ref.kv_ref, ...), custom_call_target="tpu_custom_call" | custom-call | tf_op jit(solution)/shard_map/project/pallas_call | solution.py:277
  144.0 7.3 %collective-permute-start.9 = (bf16[256,128]{1,0:T(8,128)(2,1)S(1)}, bf16[256,128]{1,0:T(8,128)(2,1)S(1)}, u32[]{:S(2)}, u32[]{:S(2)}) collective-permute-start(bf16[256,128]{1,0:T(8,128)(2,1)S(1)} %get-tuple-element.16), channel_id=1, source_target_pairs={{0,8},{8,0},{1,9},{9,1},{2,10},{10,2},{3,11},{11,3},{4,12},{12,4},... | collective-permute-start | bytes 196616 | tf_op jit(solution)/shard_map/ppermute | solution.py:215
  151.4 0.1 iota.12
  151.5 0.7 collective-permute-done.9
  152.2 0.8 bitcast_select_fusion
  (23 shorter events, 0.4 us)
Async XLA Ops:
  0.0 54.2 %copy-start.1 = (bf16[8,128,128]{2,1,0:T(8,128)(2,1)S(1)}, bf16[8,128,128]{2,1,0:T(8,128)(2,1)}, u32[]{:S(2)}) copy-start(bf16[8,128,128]{2,1,0:T(8,128)(2,1)} %w_ref.1) | copy-start | bytes 786436
  2.9 16.6 %copy-start.4 = (bf16[1152,128]{1,0:T(8,128)(2,1)S(1)}, bf16[1152,128]{1,0:T(8,128)(2,1)}, u32[]{:S(2)}) copy-start(bf16[1152,128]{1,0:T(8,128)(2,1)} %get-tuple-element.14) | copy-start | bytes 884740
  2.9 63.4 %copy-start.3 = (bf16[4,32,128]{2,1,0:T(8,128)(2,1)S(1)}, bf16[4,32,128]{2,1,0:T(8,128)(2,1)}, u32[]{:S(2)}) copy-start(bf16[4,32,128]{2,1,0:T(8,128)(2,1)} %get-tuple-element.13) | copy-start | bytes 98308
  2.9 44.5 %all-to-all-start = ((bf16[32,136,128]{2,1,0:T(8,128)(2,1)}), bf16[32,136,128]{2,1,0:T(8,128)(2,1)S(1)}, u32[]{:S(2)}, u32[]{:S(2)}) async-start(bf16[32,136,128]{2,1,0:T(8,128)(2,1)} %get-tuple-element.12), calls=%async_computation | async-start | bytes 2228224 | tf_op jit(solution)/shard_map/all_to_all | solution.py:244
  19.6 33.9 %collective-permute-start.1 = (bf16[1152,128]{1,0:T(8,128)(2,1)S(1)}, bf16[1152,128]{1,0:T(8,128)(2,1)S(1)}, u32[]{:S(2)}, u32[]{:S(2)}) collective-permute-start(bf16[1152,128]{1,0:T(8,128)(2,1)S(1)} %copy-done.4), channel_id=1, source_target_pairs={{0,1},{1,0},{2,3},{3,2},{4,5},{5,4},{6,7},{7,6},{8,9},{9,8},{10,11... | collective-permute-start | bytes 884744 | tf_op jit(solution)/shard_map/ppermute | solution.py:215
  47.5 40.4 %collective-permute-start = (bf16[32,136,128]{2,1,0:T(8,128)(2,1)S(1)}, bf16[32,136,128]{2,1,0:T(8,128)(2,1)S(1)}, u32[]{:S(2)}, u32[]{:S(2)}) collective-permute-start(bf16[32,136,128]{2,1,0:T(8,128)(2,1)S(1)} %all-to-all-done.kva_ref.kv_ref), channel_id=1, source_target_pairs={{0,8},{8,0},{1,9},{9,1},{2,10},{10,2},{3,11},{11,3},{4,12},{12,4},... | collective-permute-start | bytes 3342344 | tf_op jit(solution)/shard_map/ppermute | solution.py:215
  53.5 0.7 copy-start.2
  54.2 16.7 %collective-permute-start.5 = (bf16[16,128,128]{2,1,0:T(8,128)(2,1)S(1)}, bf16[16,128,128]{2,1,0:T(8,128)(2,1)}, u32[]{:S(2)}, u32[]{:S(2)}) collective-permute-start(bf16[16,128,128]{2,1,0:T(8,128)(2,1)S(1)} %pad_maximum_fusion), channel_id=1, source_target_pairs={{0,2},{2,4},{4,6},{6,0},{1,3},{3,5},{5,7},{7,1},{8,10},{10,12},{12... | collective-permute-start | bytes 1572872 | tf_op jit(solution)/shard_map/ppermute | solution.py:215
  57.3 25.8 %collective-permute-start.6 = (bf16[16,128,128]{2,1,0:T(8,128)(2,1)S(1)}, bf16[16,128,128]{2,1,0:T(8,128)(2,1)}, u32[]{:S(2)}, u32[]{:S(2)}) collective-permute-start(bf16[16,128,128]{2,1,0:T(8,128)(2,1)S(1)} %pad_maximum_fusion), channel_id=1, source_target_pairs={{0,4},{2,6},{4,0},{6,2},{1,5},{3,7},{5,1},{7,3},{8,12},{10,14},{12... | collective-permute-start | bytes 1572872 | tf_op jit(solution)/shard_map/ppermute | solution.py:215
  62.4 32.3 %collective-permute-start.7 = (bf16[16,128,128]{2,1,0:T(8,128)(2,1)S(1)}, bf16[16,128,128]{2,1,0:T(8,128)(2,1)}, u32[]{:S(2)}, u32[]{:S(2)}) collective-permute-start(bf16[16,128,128]{2,1,0:T(8,128)(2,1)S(1)} %pad_maximum_fusion), channel_id=1, source_target_pairs={{0,6},{2,0},{4,2},{6,4},{1,7},{3,1},{5,3},{7,5},{8,14},{10,8},{12,... | collective-permute-start | bytes 1572872 | tf_op jit(solution)/shard_map/ppermute | solution.py:215
  66.3 20.8 %collective-permute-start.2 = (bf16[64,128]{1,0:T(8,128)(2,1)S(1)}, bf16[64,128]{1,0:T(8,128)(2,1)S(1)}, u32[]{:S(2)}, u32[]{:S(2)}) collective-permute-start(bf16[64,128]{1,0:T(8,128)(2,1)S(1)} %get-tuple-element.19), channel_id=1, source_target_pairs={{0,2},{2,4},{4,6},{6,0},{1,3},{3,5},{5,7},{7,1},{8,10},{10,12},{12... | collective-permute-start | bytes 49160 | tf_op jit(solution)/shard_map/ppermute | solution.py:215
  70.9 16.2 %collective-permute-start.3 = (bf16[64,128]{1,0:T(8,128)(2,1)S(1)}, bf16[64,128]{1,0:T(8,128)(2,1)S(1)}, u32[]{:S(2)}, u32[]{:S(2)}) collective-permute-start(bf16[64,128]{1,0:T(8,128)(2,1)S(1)} %get-tuple-element.20), channel_id=1, source_target_pairs={{0,4},{2,6},{4,0},{6,2},{1,5},{3,7},{5,1},{7,3},{8,12},{10,14},{12... | collective-permute-start | bytes 49160 | tf_op jit(solution)/shard_map/ppermute | solution.py:215
  83.2 21.8 %copy-start = (bf16[128,256]{1,0:T(8,128)(2,1)S(1)}, bf16[128,256]{1,0:T(8,128)(2,1)}, u32[]{:S(2)}) copy-start(bf16[128,256]{1,0:T(8,128)(2,1)} %get-tuple-element.11.back_ref) | copy-start | bytes 196612
  83.2 4.7 %collective-permute-start.4 = (bf16[64,128]{1,0:T(8,128)(2,1)S(1)}, bf16[64,128]{1,0:T(8,128)(2,1)S(1)}, u32[]{:S(2)}, u32[]{:S(2)}) collective-permute-start(bf16[64,128]{1,0:T(8,128)(2,1)S(1)} %get-tuple-element.17), channel_id=1, source_target_pairs={{0,6},{2,0},{4,2},{6,4},{1,7},{3,1},{5,3},{7,5},{8,14},{10,8},{12,... | collective-permute-start | bytes 49160 | tf_op jit(solution)/shard_map/ppermute | solution.py:215
  91.4 13.6 %all-to-all-start.1 = ((bf16[8,32,128]{2,1,0:T(8,128)(2,1)}), bf16[8,32,128]{2,1,0:T(8,128)(2,1)S(1)}, u32[]{:S(2)}, u32[]{:S(2)}) async-start(bf16[8,32,128]{2,1,0:T(8,128)(2,1)} %attend.1), calls=%async_computation.1 | async-start | bytes 131072 | tf_op jit(solution)/shard_map/all_to_all | solution.py:267
  96.6 18.3 %collective-permute-start.8 = (bf16[64,128,128]{2,1,0:T(8,128)(2,1)}, bf16[64,128,128]{2,1,0:T(8,128)(2,1)}, u32[]{:S(2)}, u32[]{:S(2)}) collective-permute-start(bf16[64,128,128]{2,1,0:T(8,128)(2,1)} %constant_dynamic-update-slice_fusion.refs_0_), channel_id=1, source_target_pairs={{0,8},{8,0},{1,9},{9,1},{2,10},{10,2},{3,11},{11,3},{4,12},{12,4},... | collective-permute-start | bytes 6291464 | tf_op jit(solution)/shard_map/ppermute | solution.py:215
  106.3 33.7 %all-to-all-start.2 = ((bf16[32,128,128]{2,1,0:T(8,128)(2,1)}), bf16[32,128,128]{2,1,0:T(8,128)(2,1)S(1)}, u32[]{:S(2)}, u32[]{:S(2)}) async-start(bf16[32,128,128]{2,1,0:T(8,128)(2,1)} %compact.1), calls=%async_computation.2 | async-start | bytes 2097152 | tf_op jit(solution)/shard_map/all_to_all | solution.py:276
  144.0 8.1 %collective-permute-start.9 = (bf16[256,128]{1,0:T(8,128)(2,1)S(1)}, bf16[256,128]{1,0:T(8,128)(2,1)S(1)}, u32[]{:S(2)}, u32[]{:S(2)}) collective-permute-start(bf16[256,128]{1,0:T(8,128)(2,1)S(1)} %get-tuple-element.16), channel_id=1, source_target_pairs={{0,8},{8,0},{1,9},{9,1},{2,10},{10,2},{3,11},{11,3},{4,12},{12,4},... | collective-permute-start | bytes 196616 | tf_op jit(solution)/shard_map/ppermute | solution.py:215

commit v4 on v3

--- a/solution.py
+++ b/solution.py
@@ -41,11 +41,11 @@
 ):
     x = lax.axis_index("x")
     zl = lax.axis_index("zl")
-    spread = (iota((TOP, ROWS), 1) % TOP == iota((TOP, ROWS), 0)).astype(f32)
+    spread = (iota((TOP, ROWS), 1) % TOP == iota((TOP, ROWS), 0)).astype(bf16)
     own = iota((TOK, ROWS), 1) // TOP == iota((TOK, ROWS), 0)
 
     def as_row(table):
-        wide = jnp.dot(table, spread, precision=lax.Precision.HIGHEST, preferred_element_type=f32)
+        wide = jnp.dot(table.astype(bf16), spread, preferred_element_type=f32)
         return jnp.sum(jnp.where(own, wide, 0.0), axis=0, keepdims=True)
 
     id_row = as_row(ids_ref[...].astype(f32))
@@ -92,8 +92,7 @@
     lax.fori_loop(0, CHIPS, fill, 0)
 
 
-def attend_kernel(at_ref, kva_ref, kvb_ref, *refs):
-    q_refs, (out_ref, s_ref) = refs[:4], refs[4:]
+def attend_half(at_ref, kv_ref, q_refs, s_ref, parity, best):
     n = GROUPS * SLOTS
     step = 4
     width = step * SPAN
@@ -103,10 +102,7 @@
     ]
     queries = jnp.concatenate(chunks, axis=0)
     ctx = at_ref[0]
-    core = at_ref[1]
-    tags = jnp.concatenate(
-        [chunk.astype(f32)[PER * MOST :] for chunk in chunks], axis=0
-    )
+    tags = jnp.concatenate([chunk.astype(f32)[PER * MOST :] for chunk in chunks], axis=0)
     tags = jnp.concatenate([tags, tags], axis=0).T[0:SLOTS]
     token = jnp.concatenate([tags[:, g * 8 : g * 8 + 1] for g in range(GROUPS)], axis=0)
     gate = jnp.concatenate([tags[:, g * 8 + 1 : g * 8 + 2] for g in range(GROUPS)], axis=0)
@@ -118,36 +114,48 @@
     scale = HD ** (-0.5) * math.log2(math.e)
     lane = iota((1, width), 1)
 
-    def score(i, best, kv_ref, parity, base):
+    def score(i, top):
         keys = kv_ref[pl.ds(i * step, step), 0:SPAN, :].reshape(width, HD)
         scores = lax.dot_general(queries, keys, NT, preferred_element_type=f32) * scale
         key_pos = (2 * (i * step + lane // SPAN) + parity) * SPAN + lane % SPAN
         scores = jnp.where(key_pos <= pos, scores, NEG_FLOOR)
-        s_ref[base + i] = scores
-        return jnp.maximum(best, jnp.maximum(scores[:, :HD], scores[:, HD:]))
-
-    def score_both(i, best):
-        best = score(i, best, kva_ref, core, 0)
-        return score(i, best, kvb_ref, 1 - core, steps)
-
-    best = lax.fori_loop(
-        0, steps, score_both, jnp.full((n, HD), NEG_FLOOR, f32), unroll=4
-    )
+        s_ref[i] = scores
+        return jnp.maximum(top, jnp.maximum(scores[:, :HD], scores[:, HD:]))
+
+    best = lax.fori_loop(0, steps, score, best, unroll=8)
     best = jnp.max(best, axis=1, keepdims=True)
 
-    def weigh(i, carried, kv_ref, base):
+    def weigh(i, carried):
         total, acc = carried
-        exps = jnp.exp2(s_ref[base + i] - best)
+        scores = s_ref[i]
+        exps = jnp.where(scores > 0.5 * NEG_FLOOR, jnp.exp2(scores - best), 0.0)
         values = kv_ref[pl.ds(i * step, step), SPAN : 2 * SPAN, :].reshape(width, HD)
         acc = acc + jnp.dot(exps.astype(bf16), values, preferred_element_type=f32)
         return total + exps[:, :HD] + exps[:, HD:], acc
 
-    def weigh_both(i, carried):
-        return weigh(i, weigh(i, carried, kva_ref, 0), kvb_ref, steps)
-
     zero = jnp.zeros((n, HD), f32)
-    total, acc = lax.fori_loop(0, steps, weigh_both, (zero, zero), unroll=4)
-    total = jnp.sum(total, axis=1, keepdims=True)
+    total, acc = lax.fori_loop(0, steps, weigh, (zero, zero), unroll=8)
+    return best, total, acc, gate, sources
+
+
+def attend_own_kernel(at_ref, kv_ref, *refs):
+    q_refs, (best_ref, total_ref, acc_ref, s_ref) = refs[:4], refs[4:]
+    best = jnp.full((GROUPS * SLOTS, HD), NEG_FLOOR, f32)
+    best, total, acc, _, _ = attend_half(at_ref, kv_ref, q_refs, s_ref, at_ref[1], best)
+    best_ref[...] = jnp.broadcast_to(best, acc.shape)
+    total_ref[...] = total
+    acc_ref[...] = acc
+
+
+def attend_kernel(at_ref, kv_ref, *refs):
+    q_refs, (best_ref, total_ref, acc_ref, out_ref, s_ref) = refs[:4], refs[4:]
+    before = best_ref[...]
+    best, total, acc, gate, sources = attend_half(
+        at_ref, kv_ref, q_refs, s_ref, 1 - at_ref[1], before
+    )
+    fade = jnp.exp2(before - best)
+    total = jnp.sum(total + total_ref[...] * fade, axis=1, keepdims=True)
+    acc = acc + acc_ref[...] * fade
     result = (gate * (acc / total)).astype(bf16)
     for d in range(GROUPS):
         out_ref[sources[d]] = result[d * SLOTS : (d + 1) * SLOTS]
@@ -163,6 +171,18 @@
         return 0
 
     lax.fori_loop(0, CHIPS, fill, 0)
+
+
+def join_kernel(*refs):
+    out_ref, sems = refs[4:]
+    copies = [
+        pltpu.make_async_copy(refs[k], out_ref.at[pl.ds(k * 2 * PER, 2 * PER)], sems.at[k])
+        for k in range(4)
+    ]
+    for copy in copies:
+        copy.start()
+    for copy in copies:
+        copy.wait()
 
 
 def project_kernel(at_ref, rows_ref, kv_ref, *refs):
@@ -208,6 +228,7 @@
 
 SMEM = pl.BlockSpec(memory_space=pltpu.SMEM)
 VMEM = pl.BlockSpec(memory_space=pltpu.VMEM)
+ANY = pl.BlockSpec(memory_space=pl.ANY)
 HBM = pl.BlockSpec(memory_space=pltpu.HBM)
 
 
@@ -252,18 +273,37 @@
     pieces = [pair]
     for k in range(1, 4):
         pieces.append(shifted(pair, "x", 4, k))
-    near = jnp.concatenate(pieces, axis=0)
+    near = pl.pallas_call(
+        join_kernel,
+        in_specs=[ANY] * 4,
+        out_specs=ANY,
+        out_shape=shape((EXPERTS, HD, HD), bf16),
+        scratch_shapes=[pltpu.SemaphoreType.DMA((4,))],
+        compiler_params=pltpu.CompilerParams(vmem_limit_bytes=4 << 20),
+        name="join",
+    )(*pieces)
     far = shifted(near, "core", 2, 1)
     kvb = shifted(kva, "core", 2, 1)
+    state = shape((GROUPS * SLOTS, HD), f32)
+    scratch = [pltpu.VMEM((8, GROUPS * SLOTS, 4 * SPAN), f32)]
+    running = pl.pallas_call(
+        attend_own_kernel,
+        in_specs=[SMEM] + [VMEM] * 5,
+        out_specs=[VMEM] * 3,
+        out_shape=[state] * 3,
+        scratch_shapes=scratch,
+        compiler_params=pltpu.CompilerParams(vmem_limit_bytes=14 << 20),
+        name="attend_own",
+    )(at, kva, *qgot)
     attended = pl.pallas_call(
         attend_kernel,
-        in_specs=[SMEM] + [VMEM] * 6,
+        in_specs=[SMEM] + [VMEM] * 8,
         out_specs=VMEM,
         out_shape=shape((GROUPS, SLOTS, HD), bf16),
-        scratch_shapes=[pltpu.VMEM((16, GROUPS * SLOTS, 4 * SPAN), f32)],
+        scratch_shapes=scratch,
         compiler_params=pltpu.CompilerParams(vmem_limit_bytes=14 << 20),
         name="attend",
-    )(at, kva, kvb, *qgot)
+    )(at, kvb, *qgot, *running)
     home = lax.all_to_all(attended, ("x", "zl"), 0, 0, tiled=True)
     rows = pl.pallas_call(
         compact_kernel,
@@ -284,7 +324,7 @@
             pltpu.VMEM((2, EXPERTS, HD, HD), bf16),
             pltpu.SemaphoreType.DMA((2,)),
         ],
-        compiler_params=pltpu.CompilerParams(vmem_limit_bytes=50 << 20),
+        compiler_params=pltpu.CompilerParams(vmem_limit_bytes=48 << 20),
         name="project",
     )(at_exp, rows, kva, near, far)
     got = shifted(other, "core", 2, 1)

time: 155 us -> 171 us (1.10)
  blocking collectives: 0 us -> 49.6 us
  starting transfers between devices: 71.4 us -> 43.2 us
  local copies, waits for them, and re-layouts: 8.76 us -> 4.04 us
  waiting for transfers between devices: 59.9 us -> 57.4 us
    all_to_all x0 -> x1, blocking collectives: none -> 49.6 us  [run(): kva = lax.all_to_all(kvsend, ('zh', 'y'), 0, 0, tiled=True)]
    all_to_all x1 -> x0, waiting for transfers between devices: 24.8 us -> none  [run(): kva = lax.all_to_all(kvsend, ('zh', 'y'), 0, 0, tiled=True)]
    ppermute x10, waiting for transfers between devices: 10 us -> 29.2 us  [shifted(): return lax.ppermute(x, axis, [(i, (i + by) % count) for i in range(count)])]
    all_to_all x1 -> x0, starting transfers between devices: 16.6 us -> none  [run(): kva = lax.all_to_all(kvsend, ('zh', 'y'), 0, 0, tiled=True)]
    ppermute x10, starting transfers between devices: 42.9 us -> 35.1 us  [shifted(): return lax.ppermute(x, axis, [(i, (i + by) % count) for i in range(count)])]
    all_to_all x1, starting transfers between devices: 8.52 us -> 4.68 us  [run(): rows = lax.all_to_all(rows, ('zh', 'y'), 0, 0, tiled=True)]
    all_to_all x1, waiting for transfers between devices: 25.1 us -> 28.1 us  [run(): rows = lax.all_to_all(rows, ('zh', 'y'), 0, 0, tiled=True)]
    pallas_call x1 -> x3, Pallas kernels: 3.48 us -> 5.56 us  [the longest x1 2.56 us: run(): pl.pallas_call(attend_kernel, in_specs=[SMEM] + [VMEM] * 8, out_specs=VME...]
  transfers between devices with their start and end apart: 13 -> 12, of which waited for: 6 -> 6; matrix products, arithmetic and copies ran while one was open for 5% -> 0% of each run, Pallas kernels for 3% -> 3%
where the time goes in v4:
time: 171 us; the launch traced here: 169 us
  waiting for transfers between devices  57.4 us (34%)
  blocking collectives  49.6 us (29%)
  starting transfers between devices  43.2 us (25%)
  Pallas kernels  13.2 us (8%)
  local copies, waits for them, and re-layouts  4.04 us (2%)
    all_to_all x1, blocking collectives, run(): kva = lax.all_to_all(kvsend, ('zh', 'y'), 0, 0, tiled=True)  49.6 us
    ppermute x10, starting transfers between devices, shifted(): return lax.ppermute(x, axis, [(i, (i + by) % count) for i in range(count)])  35.1 us
    ppermute x10, waiting for transfers between devices, shifted(): return lax.ppermute(x, axis, [(i, (i + by) % count) for i in range(count)])  29.2 us
    all_to_all x1, waiting for transfers between devices, run(): rows = lax.all_to_all(rows, ('zh', 'y'), 0, 0, tiled=True)  28.1 us
    all_to_all x1, starting transfers between devices, run(): rows = lax.all_to_all(rows, ('zh', 'y'), 0, 0, tiled=True)  4.68 us
    pallas_call x1, Pallas kernels, run(): pl.pallas_call(project_kernel, in_specs=[SMEM] + [VMEM] * 2 + [HBM] * 2,...  4.47 us
    unnamed x18, local copies, waits for them, and re-layouts  3.84 us
    all_to_all x1, starting transfers between devices, run(): home = lax.all_to_all(attended, ('x', 'zl'), 0, 0, tiled=True)  3.48 us
  transfers between devices with their start and end apart: 12, of which 6 were waited for; matrix products, arithmetic and copies ran while one was open for 0% of the time, Pallas kernels for 3%

profile of v4, /device:TPU:1, one launch (start us, length us, event | category | flops | bytes accessed | tf_op | source)
XLA Modules:
  0.0 168.8 jit_solution(9537977338050067849)
XLA Ops:
  0.0 2.9 %prep.1 = (bf16[32,136,128]{2,1,0:T(8,128)(2,1)}, bf16[128,256]{1,0:T(8,128)(2,1)}, bf16[4,32,128]{2,1,0:T(8,128)(2,1)}, bf16[1152,128]{1,0:T(8,128)(2,1)}) custom-call(bf16[128,128]{1,0:T(8,128)(2,1)} %bitcast.27, bf16[64,128]{1,0:T(8,128)(2,1)} %bitcast.28, bf16[64,128]{1,0:T(8,128)(2,1)} %bitcast.29, s32[8,16]{1,0:T(8,128)} %ids_ref.1, ...), custom_call_target="tpu_custom_call" | custom-call | tf_op jit(solution)/shard_map/prep/pallas_call | solution.py:246
  2.9 49.6 %all_to_all.15.kv_ref = bf16[32,136,128]{2,1,0:T(8,128)(2,1)S(1)} all-to-all(bf16[32,136,128]{2,1,0:T(8,128)(2,1)} %get-tuple-element.15), channel_id=1, replica_groups=mesh['zh'=4,'y'=8,'core'=2,'x'=4,'zl'=2] {'zh','y'}, dimensions={0} | all-to-all | bytes 2228224 | tf_op jit(solution)/shard_map/all_to_all | solution.py:265
  52.5 4.1 %collective-permute-start = (bf16[32,136,128]{2,1,0:T(8,128)(2,1)S(1)}, bf16[32,136,128]{2,1,0:T(8,128)(2,1)S(1)}, u32[]{:S(2)}, u32[]{:S(2)}) collective-permute-start(bf16[32,136,128]{2,1,0:T(8,128)(2,1)S(1)} %all_to_all.15.kv_ref), channel_id=1, source_target_pairs={{0,8},{8,0},{1,9},{9,1},{2,10},{10,2},{3,11},{11,3},{4,12},{12,4},... | collective-permute-start | bytes 3342344 | tf_op jit(solution)/shard_map/ppermute | solution.py:236
  56.6 3.1 %collective-permute-start.1 = (bf16[1152,128]{1,0:T(8,128)(2,1)S(1)}, bf16[1152,128]{1,0:T(8,128)(2,1)S(1)}, u32[]{:S(2)}, u32[]{:S(2)}) collective-permute-start(bf16[1152,128]{1,0:T(8,128)(2,1)S(1)} %copy-done.8), channel_id=1, source_target_pairs={{0,1},{1,0},{2,3},{3,2},{4,5},{5,4},{6,7},{7,6},{8,9},{9,8},{10,11... | collective-permute-start | bytes 884744 | tf_op jit(solution)/shard_map/ppermute | solution.py:236
  59.7 7.3 %collective-permute-done.1 = bf16[1152,128]{1,0:T(8,128)(2,1)S(1)} collective-permute-done((bf16[1152,128]{1,0:T(8,128)(2,1)S(1)}, bf16[1152,128]{1,0:T(8,128)(2,1)S(1)}, u32[]{:S(2)}, u32[]{:S(2)}) %collective-permute-start.1) | collective-permute-done | bytes 294944 | tf_op jit(solution)/shard_map/ppermute | solution.py:236
  67.2 4.4 %collective-permute-start.7 = (bf16[16,128,128]{2,1,0:T(8,128)(2,1)S(1)}, bf16[16,128,128]{2,1,0:T(8,128)(2,1)S(1)}, u32[]{:S(2)}, u32[]{:S(2)}) collective-permute-start(bf16[16,128,128]{2,1,0:T(8,128)(2,1)S(1)} %pad_maximum_fusion.refs_0_), channel_id=1, source_target_pairs={{0,6},{2,0},{4,2},{6,4},{1,7},{3,1},{5,3},{7,5},{8,14},{10,8},{12,... | collective-permute-start | bytes 1572872 | tf_op jit(solution)/shard_map/ppermute | solution.py:236
  71.6 2.4 %collective-permute-start.6 = (bf16[16,128,128]{2,1,0:T(8,128)(2,1)S(1)}, bf16[16,128,128]{2,1,0:T(8,128)(2,1)}, u32[]{:S(2)}, u32[]{:S(2)}) collective-permute-start(bf16[16,128,128]{2,1,0:T(8,128)(2,1)S(1)} %pad_maximum_fusion.refs_0_), channel_id=1, source_target_pairs={{0,4},{2,6},{4,0},{6,2},{1,5},{3,7},{5,1},{7,3},{8,12},{10,14},{12... | collective-permute-start | bytes 1572872 | tf_op jit(solution)/shard_map/ppermute | solution.py:236
  74.0 2.5 %collective-permute-start.5 = (bf16[16,128,128]{2,1,0:T(8,128)(2,1)S(1)}, bf16[16,128,128]{2,1,0:T(8,128)(2,1)}, u32[]{:S(2)}, u32[]{:S(2)}) collective-permute-start(bf16[16,128,128]{2,1,0:T(8,128)(2,1)S(1)} %pad_maximum_fusion.refs_0_), channel_id=1, source_target_pairs={{0,2},{2,4},{4,6},{6,0},{1,3},{3,5},{5,7},{7,1},{8,10},{10,12},{12... | collective-permute-start | bytes 1572872 | tf_op jit(solution)/shard_map/ppermute | solution.py:236
  76.6 4.0 %collective-permute-start.4 = (bf16[64,128]{1,0:T(8,128)(2,1)S(1)}, bf16[64,128]{1,0:T(8,128)(2,1)S(1)}, u32[]{:S(2)}, u32[]{:S(2)}) collective-permute-start(bf16[64,128]{1,0:T(8,128)(2,1)S(1)} %get-tuple-element.23), channel_id=1, source_target_pairs={{0,6},{2,0},{4,2},{6,4},{1,7},{3,1},{5,3},{7,5},{8,14},{10,8},{12,... | collective-permute-start | bytes 49160 | tf_op jit(solution)/shard_map/ppermute | solution.py:236
  80.5 12.9 %collective-permute-done.4.refs_3_ = bf16[64,128]{1,0:T(8,128)(2,1)S(1)} collective-permute-done((bf16[64,128]{1,0:T(8,128)(2,1)S(1)}, bf16[64,128]{1,0:T(8,128)(2,1)S(1)}, u32[]{:S(2)}, u32[]{:S(2)}) %collective-permute-start.4) | collective-permute-done | bytes 16416 | tf_op jit(solution)/shard_map/ppermute | solution.py:236
  93.4 1.9 %collective-permute-start.2 = (bf16[64,128]{1,0:T(8,128)(2,1)S(1)}, bf16[64,128]{1,0:T(8,128)(2,1)S(1)}, u32[]{:S(2)}, u32[]{:S(2)}) collective-permute-start(bf16[64,128]{1,0:T(8,128)(2,1)S(1)} %get-tuple-element.25), channel_id=1, source_target_pairs={{0,2},{2,4},{4,6},{6,0},{1,3},{3,5},{5,7},{7,1},{8,10},{10,12},{12... | collective-permute-start | bytes 49160 | tf_op jit(solution)/shard_map/ppermute | solution.py:236
  95.3 5.0 %collective-permute-done.2.refs_1_ = bf16[64,128]{1,0:T(8,128)(2,1)S(1)} collective-permute-done((bf16[64,128]{1,0:T(8,128)(2,1)S(1)}, bf16[64,128]{1,0:T(8,128)(2,1)S(1)}, u32[]{:S(2)}, u32[]{:S(2)}) %collective-permute-start.2) | collective-permute-done | bytes 16416 | tf_op jit(solution)/shard_map/ppermute | solution.py:236
  100.3 2.5 %collective-permute-start.3 = (bf16[64,128]{1,0:T(8,128)(2,1)S(1)}, bf16[64,128]{1,0:T(8,128)(2,1)S(1)}, u32[]{:S(2)}, u32[]{:S(2)}) collective-permute-start(bf16[64,128]{1,0:T(8,128)(2,1)S(1)} %get-tuple-element.26), channel_id=1, source_target_pairs={{0,4},{2,6},{4,0},{6,2},{1,5},{3,7},{5,1},{7,3},{8,12},{10,14},{12... | collective-permute-start | bytes 49160 | tf_op jit(solution)/shard_map/ppermute | solution.py:236
  102.9 3.4 %collective-permute-done.3.refs_2_ = bf16[64,128]{1,0:T(8,128)(2,1)S(1)} collective-permute-done((bf16[64,128]{1,0:T(8,128)(2,1)S(1)}, bf16[64,128]{1,0:T(8,128)(2,1)S(1)}, u32[]{:S(2)}, u32[]{:S(2)}) %collective-permute-start.3) | collective-permute-done | bytes 16416 | tf_op jit(solution)/shard_map/ppermute | solution.py:236
  106.3 1.7 %attend_own.1 = (f32[256,128]{1,0:T(8,128)S(1)}, f32[256,128]{1,0:T(8,128)S(1)}, f32[256,128]{1,0:T(8,128)S(1)}) custom-call(s32[4]{0:T(128)S(1)} %pad_add_fusion.1.at_ref, bf16[32,136,128]{2,1,0:T(8,128)(2,1)S(1)} %all_to_all.15.kv_ref, bf16[64,128]{1,0:T(8,128)(2,1)S(1)} %get-tuple-element.24.refs_0_, bf16[64,128]{1,0:T(8,128)(2,1)S(1)} %collective-permute-done.2.refs_1_, ...), custom_call_target="tpu_custom_call" | custom-call | tf_op jit(solution)/shard_map/attend_own/pallas_call | solution.py:289
  108.0 2.6 %attend.1 = bf16[8,32,128]{2,1,0:T(8,128)(2,1)} custom-call(s32[4]{0:T(128)S(1)} %pad_add_fusion.1.at_ref, bf16[32,136,128]{2,1,0:T(8,128)(2,1)S(1)} %collective-permute-done.kv_ref, bf16[64,128]{1,0:T(8,128)(2,1)S(1)} %get-tuple-element.24.refs_0_, bf16[64,128]{1,0:T(8,128)(2,1)S(1)} %collective-permute-done.2.refs_1_, ...), custom_call_target="tpu_custom_call" | custom-call | tf_op jit(solution)/shard_map/attend/pallas_call | solution.py:298
  110.6 3.5 %all-to-all-start.1 = ((bf16[8,32,128]{2,1,0:T(8,128)(2,1)}), bf16[8,32,128]{2,1,0:T(8,128)(2,1)S(1)}, u32[]{:S(2)}, u32[]{:S(2)}) async-start(bf16[8,32,128]{2,1,0:T(8,128)(2,1)} %attend.1), calls=%async_computation.1 | async-start | bytes 131072 | tf_op jit(solution)/shard_map/all_to_all | solution.py:307
  114.1 0.8 copy-done.3
  114.9 1.0 copy-done.2
  115.9 1.0 copy-done.4
  117.0 1.3 join.1.refs_0_
  118.2 6.2 %collective-permute-start.8 = (bf16[64,128,128]{2,1,0:T(8,128)(2,1)S(1)}, bf16[64,128,128]{2,1,0:T(8,128)(2,1)}, u32[]{:S(2)}, u32[]{:S(2)}) collective-permute-start(bf16[64,128,128]{2,1,0:T(8,128)(2,1)S(1)} %join.1.refs_0_), channel_id=1, source_target_pairs={{0,8},{8,0},{1,9},{9,1},{2,10},{10,2},{3,11},{11,3},{4,12},{12,4},... | collective-permute-start | bytes 6291464 | tf_op jit(solution)/shard_map/ppermute | solution.py:236
  124.4 0.3 compact.1
  124.8 0.9 copy-done
  125.7 4.7 %all-to-all-start.2 = ((bf16[32,128,128]{2,1,0:T(8,128)(2,1)}), bf16[32,128,128]{2,1,0:T(8,128)(2,1)}, u32[]{:S(2)}, u32[]{:S(2)}) async-start(bf16[32,128,128]{2,1,0:T(8,128)(2,1)} %copy-done), calls=%async_computation.2 | async-start | bytes 2097152 | tf_op jit(solution)/shard_map/all_to_all | solution.py:316
  130.5 28.1 %all-to-all-done.2.rows_ref = bf16[32,128,128]{2,1,0:T(8,128)(2,1)} async-done(((bf16[32,128,128]{2,1,0:T(8,128)(2,1)}), bf16[32,128,128]{2,1,0:T(8,128)(2,1)}, u32[]{:S(2)}, u32[]{:S(2)}) %all-to-all-start.2) | async-done | bytes 1048608 | tf_op jit(solution)/shard_map/all_to_all | solution.py:316
  158.6 4.5 %project.1 = (bf16[256,128]{1,0:T(8,128)(2,1)S(1)}, bf16[256,128]{1,0:T(8,128)(2,1)S(1)}) custom-call(s32[3]{0:T(128)S(1)} %pad_add_fusion.at_ref, bf16[32,128,128]{2,1,0:T(8,128)(2,1)} %all-to-all-done.2.rows_ref, bf16[32,136,128]{2,1,0:T(8,128)(2,1)S(1)} %all_to_all.15.kv_ref, bf16[64,128,128]{2,1,0:T(8,128)(2,1)S(1)} %join.1.refs_0_, ...), custom_call_target="tpu_custom_call" | custom-call | tf_op jit(solution)/shard_map/project/pallas_call | solution.py:317
  163.1 4.0 %collective-permute-start.9 = (bf16[256,128]{1,0:T(8,128)(2,1)S(1)}, bf16[256,128]{1,0:T(8,128)(2,1)S(1)}, u32[]{:S(2)}, u32[]{:S(2)}) collective-permute-start(bf16[256,128]{1,0:T(8,128)(2,1)S(1)} %get-tuple-element.22), channel_id=1, source_target_pairs={{0,8},{8,0},{1,9},{9,1},{2,10},{10,2},{3,11},{11,3},{4,12},{12,4},... | collective-permute-start | bytes 196616 | tf_op jit(solution)/shard_map/ppermute | solution.py:236
  167.1 0.1 iota.11
  167.2 0.1 iota.12
  167.3 0.7 collective-permute-done.9
  168.0 0.8 bitcast_select_fusion
  (27 shorter events, 0.3 us)
Async XLA Ops:
  2.9 53.7 %copy-start.8 = (bf16[1152,128]{1,0:T(8,128)(2,1)S(1)}, bf16[1152,128]{1,0:T(8,128)(2,1)}, u32[]{:S(2)}) copy-start(bf16[1152,128]{1,0:T(8,128)(2,1)} %get-tuple-element.17) | copy-start | bytes 884740
  2.9 64.2 %copy-start.6 = (bf16[8,128,128]{2,1,0:T(8,128)(2,1)S(1)}, bf16[8,128,128]{2,1,0:T(8,128)(2,1)}, u32[]{:S(2)}) copy-start(bf16[8,128,128]{2,1,0:T(8,128)(2,1)} %w_ref.1) | copy-start | bytes 786436
  52.5 24.1 %copy-start.7 = (bf16[4,32,128]{2,1,0:T(8,128)(2,1)S(1)}, bf16[4,32,128]{2,1,0:T(8,128)(2,1)}, u32[]{:S(2)}) copy-start(bf16[4,32,128]{2,1,0:T(8,128)(2,1)} %get-tuple-element.16) | copy-start | bytes 98308
  52.5 55.5 %collective-permute-start = (bf16[32,136,128]{2,1,0:T(8,128)(2,1)S(1)}, bf16[32,136,128]{2,1,0:T(8,128)(2,1)S(1)}, u32[]{:S(2)}, u32[]{:S(2)}) collective-permute-start(bf16[32,136,128]{2,1,0:T(8,128)(2,1)S(1)} %all_to_all.15.kv_ref), channel_id=1, source_target_pairs={{0,8},{8,0},{1,9},{9,1},{2,10},{10,2},{3,11},{11,3},{4,12},{12,4},... | collective-permute-start | bytes 3342344 | tf_op jit(solution)/shard_map/ppermute | solution.py:236
  56.6 10.4 %collective-permute-start.1 = (bf16[1152,128]{1,0:T(8,128)(2,1)S(1)}, bf16[1152,128]{1,0:T(8,128)(2,1)S(1)}, u32[]{:S(2)}, u32[]{:S(2)}) collective-permute-start(bf16[1152,128]{1,0:T(8,128)(2,1)S(1)} %copy-done.8), channel_id=1, source_target_pairs={{0,1},{1,0},{2,3},{3,2},{4,5},{5,4},{6,7},{7,6},{8,9},{9,8},{10,11... | collective-permute-start | bytes 884744 | tf_op jit(solution)/shard_map/ppermute | solution.py:236
  67.2 43.4 %copy-start.1 = (bf16[16,128,128]{2,1,0:T(8,128)(2,1)}, bf16[16,128,128]{2,1,0:T(8,128)(2,1)S(1)}, u32[]{:S(2)}) copy-start(bf16[16,128,128]{2,1,0:T(8,128)(2,1)S(1)} %pad_maximum_fusion.refs_0_) | copy-start | bytes 1572868
  67.2 46.9 %collective-permute-start.7 = (bf16[16,128,128]{2,1,0:T(8,128)(2,1)S(1)}, bf16[16,128,128]{2,1,0:T(8,128)(2,1)S(1)}, u32[]{:S(2)}, u32[]{:S(2)}) collective-permute-start(bf16[16,128,128]{2,1,0:T(8,128)(2,1)S(1)} %pad_maximum_fusion.refs_0_), channel_id=1, source_target_pairs={{0,6},{2,0},{4,2},{6,4},{1,7},{3,1},{5,3},{7,5},{8,14},{10,8},{12,... | collective-permute-start | bytes 1572872 | tf_op jit(solution)/shard_map/ppermute | solution.py:236
  71.6 43.3 %collective-permute-start.6 = (bf16[16,128,128]{2,1,0:T(8,128)(2,1)S(1)}, bf16[16,128,128]{2,1,0:T(8,128)(2,1)}, u32[]{:S(2)}, u32[]{:S(2)}) collective-permute-start(bf16[16,128,128]{2,1,0:T(8,128)(2,1)S(1)} %pad_maximum_fusion.refs_0_), channel_id=1, source_target_pairs={{0,4},{2,6},{4,0},{6,2},{1,5},{3,7},{5,1},{7,3},{8,12},{10,14},{12... | collective-permute-start | bytes 1572872 | tf_op jit(solution)/shard_map/ppermute | solution.py:236
  74.0 40.9 %collective-permute-start.5 = (bf16[16,128,128]{2,1,0:T(8,128)(2,1)S(1)}, bf16[16,128,128]{2,1,0:T(8,128)(2,1)}, u32[]{:S(2)}, u32[]{:S(2)}) collective-permute-start(bf16[16,128,128]{2,1,0:T(8,128)(2,1)S(1)} %pad_maximum_fusion.refs_0_), channel_id=1, source_target_pairs={{0,2},{2,4},{4,6},{6,0},{1,3},{3,5},{5,7},{7,1},{8,10},{10,12},{12... | collective-permute-start | bytes 1572872 | tf_op jit(solution)/shard_map/ppermute | solution.py:236
  76.6 16.8 %collective-permute-start.4 = (bf16[64,128]{1,0:T(8,128)(2,1)S(1)}, bf16[64,128]{1,0:T(8,128)(2,1)S(1)}, u32[]{:S(2)}, u32[]{:S(2)}) collective-permute-start(bf16[64,128]{1,0:T(8,128)(2,1)S(1)} %get-tuple-element.23), channel_id=1, source_target_pairs={{0,6},{2,0},{4,2},{6,4},{1,7},{3,1},{5,3},{7,5},{8,14},{10,8},{12,... | collective-permute-start | bytes 49160 | tf_op jit(solution)/shard_map/ppermute | solution.py:236
  93.4 6.9 %collective-permute-start.2 = (bf16[64,128]{1,0:T(8,128)(2,1)S(1)}, bf16[64,128]{1,0:T(8,128)(2,1)S(1)}, u32[]{:S(2)}, u32[]{:S(2)}) collective-permute-start(bf16[64,128]{1,0:T(8,128)(2,1)S(1)} %get-tuple-element.25), channel_id=1, source_target_pairs={{0,2},{2,4},{4,6},{6,0},{1,3},{3,5},{5,7},{7,1},{8,10},{10,12},{12... | collective-permute-start | bytes 49160 | tf_op jit(solution)/shard_map/ppermute | solution.py:236
  100.3 6.0 %collective-permute-start.3 = (bf16[64,128]{1,0:T(8,128)(2,1)S(1)}, bf16[64,128]{1,0:T(8,128)(2,1)S(1)}, u32[]{:S(2)}, u32[]{:S(2)}) collective-permute-start(bf16[64,128]{1,0:T(8,128)(2,1)S(1)} %get-tuple-element.26), channel_id=1, source_target_pairs={{0,4},{2,6},{4,0},{6,2},{1,5},{3,7},{5,1},{7,3},{8,12},{10,14},{12... | collective-permute-start | bytes 49160 | tf_op jit(solution)/shard_map/ppermute | solution.py:236
  110.6 13.8 %copy-start.5 = (bf16[128,256]{1,0:T(8,128)(2,1)S(1)}, bf16[128,256]{1,0:T(8,128)(2,1)}, u32[]{:S(2)}) copy-start(bf16[128,256]{1,0:T(8,128)(2,1)} %get-tuple-element.14.back_ref) | copy-start | bytes 196612
  110.6 13.8 %all-to-all-start.1 = ((bf16[8,32,128]{2,1,0:T(8,128)(2,1)}), bf16[8,32,128]{2,1,0:T(8,128)(2,1)S(1)}, u32[]{:S(2)}, u32[]{:S(2)}) async-start(bf16[8,32,128]{2,1,0:T(8,128)(2,1)} %attend.1), calls=%async_computation.1 | async-start | bytes 131072 | tf_op jit(solution)/shard_map/all_to_all | solution.py:307
  114.1 0.8 copy-start.3
  114.9 1.0 copy-start.2
  115.9 1.0 copy-start.4
  118.2 12.2 %collective-permute-start.8 = (bf16[64,128,128]{2,1,0:T(8,128)(2,1)S(1)}, bf16[64,128,128]{2,1,0:T(8,128)(2,1)}, u32[]{:S(2)}, u32[]{:S(2)}) collective-permute-start(bf16[64,128,128]{2,1,0:T(8,128)(2,1)S(1)} %join.1.refs_0_), channel_id=1, source_target_pairs={{0,8},{8,0},{1,9},{9,1},{2,10},{10,2},{3,11},{11,3},{4,12},{12,4},... | collective-permute-start | bytes 6291464 | tf_op jit(solution)/shard_map/ppermute | solution.py:236
  124.7 1.0 copy-start
  125.7 32.9 %all-to-all-start.2 = ((bf16[32,128,128]{2,1,0:T(8,128)(2,1)}), bf16[32,128,128]{2,1,0:T(8,128)(2,1)}, u32[]{:S(2)}, u32[]{:S(2)}) async-start(bf16[32,128,128]{2,1,0:T(8,128)(2,1)} %copy-done), calls=%async_computation.2 | async-start | bytes 2097152 | tf_op jit(solution)/shard_map/all_to_all | solution.py:316
  163.1 4.9 %collective-permute-start.9 = (bf16[256,128]{1,0:T(8,128)(2,1)S(1)}, bf16[256,128]{1,0:T(8,128)(2,1)S(1)}, u32[]{:S(2)}, u32[]{:S(2)}) collective-permute-start(bf16[256,128]{1,0:T(8,128)(2,1)S(1)} %get-tuple-element.22), channel_id=1, source_target_pairs={{0,8},{8,0},{1,9},{9,1},{2,10},{10,2},{3,11},{11,3},{4,12},{12,4},... | collective-permute-start | bytes 196616 | tf_op jit(solution)/shard_map/ppermute | solution.py:236

commit v5 on v4

--- a/solution.py
+++ b/solution.py
@@ -36,18 +36,35 @@
     return ((group // 2 - x + 4) % 4) * 2 + (group % 2 + zl) % 2
 
 
-def prep_kernel(
-    q_ref, k_ref, v_ref, ids_ref, logit_ref, w_ref, kvsend_ref, back_ref, qnear_ref, cargo_ref
-):
+def spread_tables():
+    wide = (iota((TOP, ROWS), 1) % TOP == iota((TOP, ROWS), 0)).astype(bf16)
+    own = iota((TOK, ROWS), 1) // TOP == iota((TOK, ROWS), 0)
+
+    def as_row(table):
+        every = jnp.dot(table.astype(bf16), wide, preferred_element_type=f32)
+        return jnp.sum(jnp.where(own, every, 0.0), axis=0, keepdims=True)
+
+    return as_row
+
+
+def prep_kv_kernel(k_ref, v_ref, ids_ref, kvsend_ref, chunk_ref, sems):
+    id_row = spread_tables()(ids_ref[...].astype(f32))
+    chunk_ref[0:SPAN] = k_ref[...]
+    chunk_ref[SPAN : 2 * SPAN] = v_ref[...]
+    chunk_ref[2 * SPAN : KVROWS] = jnp.broadcast_to(id_row, (8, ROWS)).astype(bf16)
+    copies = [
+        pltpu.make_async_copy(chunk_ref, kvsend_ref.at[i], sems.at[i]) for i in range(CHIPS)
+    ]
+    for copy in copies:
+        copy.start()
+    for copy in copies:
+        copy.wait()
+
+
+def prep_q_kernel(q_ref, ids_ref, logit_ref, back_ref, qsend_ref):
     x = lax.axis_index("x")
     zl = lax.axis_index("zl")
-    spread = (iota((TOP, ROWS), 1) % TOP == iota((TOP, ROWS), 0)).astype(bf16)
-    own = iota((TOK, ROWS), 1) // TOP == iota((TOK, ROWS), 0)
-
-    def as_row(table):
-        wide = jnp.dot(table.astype(bf16), spread, preferred_element_type=f32)
-        return jnp.sum(jnp.where(own, wide, 0.0), axis=0, keepdims=True)
-
+    as_row = spread_tables()
     id_row = as_row(ids_ref[...].astype(f32))
     gate_exp = jnp.exp(logit_ref[...])
     gate_row = as_row(gate_exp / jnp.sum(gate_exp, axis=1, keepdims=True))
@@ -66,30 +83,14 @@
     for g in range(GROUPS):
         here = (iota((ROWS, ROWS), 0) == slot - g * SLOTS).astype(bf16)
         info = lax.dot_general(tags, here, NT, preferred_element_type=f32)
-        chunk = jnp.concatenate(
+        qsend_ref[g // 2, g % 2 * SLOTS : (g % 2 + 1) * SLOTS] = jnp.concatenate(
             [rows[g * SLOTS : g * SLOTS + PER * MOST], info], axis=0
         ).astype(bf16)
-        if g % 2 == 0:
-            qnear_ref[g // 2] = chunk
-        else:
-            cargo_ref[PER * HD + g // 2 * SLOTS : PER * HD + (g // 2 + 1) * SLOTS] = chunk
-    cargo_ref[0 : PER * HD] = w_ref[...].reshape(PER * HD, HD)
     slot = group * SLOTS + within
     slot_col = jnp.broadcast_to(slot.astype(f32), (ROWS, ROWS)).T.astype(jnp.int32)
     lane = iota((ROWS, ROWS), 1)
     back_ref[:, :ROWS] = (lane == slot_col).astype(bf16)
     back_ref[:, ROWS:] = (lane + ROWS == slot_col).astype(bf16)
-    keys = k_ref[...]
-    values = v_ref[...]
-    ids = jnp.broadcast_to(id_row, (8, ROWS)).astype(bf16)
-
-    def fill(i, _):
-        kvsend_ref[i, 0:SPAN] = keys
-        kvsend_ref[i, SPAN : 2 * SPAN] = values
-        kvsend_ref[i, 2 * SPAN : KVROWS] = ids
-        return 0
-
-    lax.fori_loop(0, CHIPS, fill, 0)
 
 
 def attend_half(at_ref, kv_ref, q_refs, s_ref, parity, best):
@@ -98,7 +99,7 @@
     width = step * SPAN
     steps = CHIPS // step
     chunks = [
-        q_refs[d // 2][d % 2 * SLOTS : (d % 2 + 1) * SLOTS] for d in range(GROUPS)
+        q_refs[4][d // 2] if d % 2 else q_refs[d // 2][0:SLOTS] for d in range(GROUPS)
     ]
     queries = jnp.concatenate(chunks, axis=0)
     ctx = at_ref[0]
@@ -139,7 +140,7 @@
 
 
 def attend_own_kernel(at_ref, kv_ref, *refs):
-    q_refs, (best_ref, total_ref, acc_ref, s_ref) = refs[:4], refs[4:]
+    q_refs, (best_ref, total_ref, acc_ref, s_ref) = refs[:5], refs[5:]
     best = jnp.full((GROUPS * SLOTS, HD), NEG_FLOOR, f32)
     best, total, acc, _, _ = attend_half(at_ref, kv_ref, q_refs, s_ref, at_ref[1], best)
     best_ref[...] = jnp.broadcast_to(best, acc.shape)
@@ -148,7 +149,7 @@
 
 
 def attend_kernel(at_ref, kv_ref, *refs):
-    q_refs, (best_ref, total_ref, acc_ref, out_ref, s_ref) = refs[:4], refs[4:]
+    q_refs, (best_ref, total_ref, acc_ref, out_ref, s_ref) = refs[:5], refs[5:]
     before = best_ref[...]
     best, total, acc, gate, sources = attend_half(
         at_ref, kv_ref, q_refs, s_ref, 1 - at_ref[1], before
@@ -243,33 +244,32 @@
     at = jnp.stack([ctx, core, x, zl]).astype(jnp.int32)
     at_exp = jnp.stack([x, zl, core]).astype(jnp.int32)
     shape = jax.ShapeDtypeStruct
-    kvsend, back, qnear, cargo = pl.pallas_call(
-        prep_kernel,
-        in_specs=[VMEM] * 6,
-        out_specs=[VMEM] * 4,
+    near = shifted(out_weight, "zl", 2, 1)
+    kvsend = pl.pallas_call(
+        prep_kv_kernel,
+        in_specs=[VMEM] * 3,
+        out_specs=HBM,
+        out_shape=shape((CHIPS, KVROWS, HD), bf16),
+        scratch_shapes=[pltpu.VMEM((KVROWS, HD), bf16), pltpu.SemaphoreType.DMA((CHIPS,))],
+        name="prep_kv",
+    )(key_heads.reshape(SPAN, HD), value_heads.reshape(SPAN, HD), expert_ids)
+    kva = lax.all_to_all(kvsend, ("zh", "y"), 0, 0, tiled=True)
+    back, qsend = pl.pallas_call(
+        prep_q_kernel,
+        in_specs=[VMEM] * 3,
+        out_specs=[VMEM] * 2,
         out_shape=[
-            shape((CHIPS, KVROWS, HD), bf16),
             shape((ROWS, GROUPS * SLOTS), bf16),
-            shape((4, SLOTS, HD), bf16),
-            shape((PER * HD + 4 * SLOTS, HD), bf16),
+            shape((4, 2 * SLOTS, HD), bf16),
         ],
-        name="prep",
-    )(
-        queries.reshape(ROWS, HD),
-        key_heads.reshape(SPAN, HD),
-        value_heads.reshape(SPAN, HD),
-        expert_ids,
-        gate_logits,
-        out_weight,
-    )
-    kva = lax.all_to_all(kvsend, ("zh", "y"), 0, 0, tiled=True)
-    got = shifted(cargo, "zl", 2, 1)
-    crossed = got[PER * HD :].reshape(4, SLOTS, HD)
-    qpair = jnp.concatenate([qnear, crossed], axis=1)
-    qgot = [qpair[k] for k in range(4)]
+        name="prep_q",
+    )(queries.reshape(ROWS, HD), expert_ids, gate_logits)
+    qgot = [qsend[k] for k in range(4)]
     for k in range(1, 4):
         qgot[k] = shifted(qgot[k], "x", 4, k)
-    pair = jnp.concatenate([out_weight, got[: PER * HD].reshape(PER, HD, HD)], axis=0)
+    crossing = jnp.stack([part[SLOTS:] for part in qgot])
+    qgot.append(shifted(crossing, "zl", 2, 1))
+    pair = jnp.concatenate([out_weight, near], axis=0)
     pieces = [pair]
     for k in range(1, 4):
         pieces.append(shifted(pair, "x", 4, k))
@@ -288,7 +288,7 @@
     scratch = [pltpu.VMEM((8, GROUPS * SLOTS, 4 * SPAN), f32)]
     running = pl.pallas_call(
         attend_own_kernel,
-        in_specs=[SMEM] + [VMEM] * 5,
+        in_specs=[SMEM] + [VMEM] * 6,
         out_specs=[VMEM] * 3,
         out_shape=[state] * 3,
         scratch_shapes=scratch,
@@ -297,7 +297,7 @@
     )(at, kva, *qgot)
     attended = pl.pallas_call(
         attend_kernel,
-        in_specs=[SMEM] + [VMEM] * 8,
+        in_specs=[SMEM] + [VMEM] * 9,
         out_specs=VMEM,
         out_shape=shape((GROUPS, SLOTS, HD), bf16),
         scratch_shapes=scratch,

time: 171 us -> 144 us (0.84)
  blocking collectives: 49.6 us -> 0 us
  starting transfers between devices: 43.2 us -> 68.1 us
  waiting for transfers between devices: 57.4 us -> 53.1 us
    all_to_all x1 -> x0, blocking collectives: 49.6 us -> none  [run(): kva = lax.all_to_all(kvsend, ('zh', 'y'), 0, 0, tiled=True)]
    ppermute x10 -> x11, waiting for transfers between devices: 29.2 us -> 12.1 us  [shifted(): return lax.ppermute(x, axis, [(i, (i + by) % count) for i in range(count)])]
    all_to_all x0 -> x1, starting transfers between devices: none -> 16.6 us  [run(): kva = lax.all_to_all(kvsend, ('zh', 'y'), 0, 0, tiled=True)]
    all_to_all x0 -> x1, waiting for transfers between devices: none -> 12.8 us  [run(): kva = lax.all_to_all(kvsend, ('zh', 'y'), 0, 0, tiled=True)]
    all_to_all x1, starting transfers between devices: 4.68 us -> 10 us  [run(): rows = lax.all_to_all(rows, ('zh', 'y'), 0, 0, tiled=True)]
    ppermute x10 -> x11, starting transfers between devices: 35.1 us -> 37.1 us  [shifted(): return lax.ppermute(x, axis, [(i, (i + by) % count) for i in range(count)])]
    pallas_call x3 -> x4, Pallas kernels: 7.16 us -> 8.34 us  [the longest x1 2.55 us: run(): pl.pallas_call(attend_kernel, in_specs=[SMEM] + [VMEM] * 9, out_specs=VME...]
    unnamed x18 -> x15, local copies, waits for them, and re-layouts: 3.84 us -> 3.85 us
  transfers between devices with their start and end apart: 12 -> 14, of which waited for: 6 -> 6; matrix products, arithmetic and copies ran while one was open for 0% -> 1% of each run, Pallas kernels for 3% -> 5%
where the time goes in v5:
time: 144 us; the launch traced here: 142 us
  starting transfers between devices  68.1 us (47%)
  waiting for transfers between devices  53.1 us (37%)
  Pallas kernels  14.4 us (10%)
  local copies, waits for them, and re-layouts  5.55 us (4%)
    ppermute x11, starting transfers between devices, shifted(): return lax.ppermute(x, axis, [(i, (i + by) % count) for i in range(count)])  37.1 us
    all_to_all x1, waiting for transfers between devices, run(): rows = lax.all_to_all(rows, ('zh', 'y'), 0, 0, tiled=True)  28.3 us
    all_to_all x1, starting transfers between devices, run(): kva = lax.all_to_all(kvsend, ('zh', 'y'), 0, 0, tiled=True)  16.6 us
    all_to_all x1, waiting for transfers between devices, run(): kva = lax.all_to_all(kvsend, ('zh', 'y'), 0, 0, tiled=True)  12.8 us
    ppermute x11, waiting for transfers between devices, shifted(): return lax.ppermute(x, axis, [(i, (i + by) % count) for i in range(count)])  12.1 us
    all_to_all x1, starting transfers between devices, run(): rows = lax.all_to_all(rows, ('zh', 'y'), 0, 0, tiled=True)  10 us
    pallas_call x1, Pallas kernels, run(): pl.pallas_call(project_kernel, in_specs=[SMEM] + [VMEM] * 2 + [HBM] * 2,...  4.47 us
    all_to_all x1, starting transfers between devices, run(): home = lax.all_to_all(attended, ('x', 'zl'), 0, 0, tiled=True)  4.3 us
  transfers between devices with their start and end apart: 14, of which 6 were waited for; matrix products, arithmetic and copies ran while one was open for 1% of the time, Pallas kernels for 5%

profile of v5, /device:TPU:1, one launch (start us, length us, event | category | flops | bytes accessed | tf_op | source)
XLA Modules:
  0.0 142.4 jit_solution(2504810793948391464)
XLA Ops:
  0.0 2.2 %prep_kv.1 = bf16[32,136,128]{2,1,0:T(8,128)(2,1)} custom-call(bf16[64,128]{1,0:T(8,128)(2,1)} %bitcast.30, bf16[64,128]{1,0:T(8,128)(2,1)} %bitcast.31, s32[8,16]{1,0:T(8,128)} %ids_ref.3), custom_call_target="tpu_custom_call" | custom-call | tf_op jit(solution)/shard_map/prep_kv/pallas_call | solution.py:248
  2.2 16.6 %all-to-all-start = ((bf16[32,136,128]{2,1,0:T(8,128)(2,1)}), bf16[32,136,128]{2,1,0:T(8,128)(2,1)S(1)}, u32[]{:S(2)}, u32[]{:S(2)}) async-start(bf16[32,136,128]{2,1,0:T(8,128)(2,1)} %prep_kv.1), calls=%async_computation | async-start | bytes 2228224 | tf_op jit(solution)/shard_map/all_to_all | solution.py:256
  18.8 1.9 %prep_q.1 = (bf16[128,256]{1,0:T(8,128)(2,1)}, bf16[4,64,128]{2,1,0:T(8,128)(2,1)}) custom-call(bf16[128,128]{1,0:T(8,128)(2,1)} %bitcast.29, s32[8,16]{1,0:T(8,128)} %ids_ref.3, f32[8,16]{1,0:T(8,128)} %logit_ref.1), custom_call_target="tpu_custom_call" | custom-call | tf_op jit(solution)/shard_map/prep_q/pallas_call | solution.py:257
  20.7 0.8 slice_bitcast_fusion
  21.5 4.4 %collective-permute-start.3 = (bf16[64,128]{1,0:T(8,128)(2,1)S(1)}, bf16[64,128]{1,0:T(8,128)(2,1)S(1)}, u32[]{:S(2)}, u32[]{:S(2)}) collective-permute-start(bf16[64,128]{1,0:T(8,128)(2,1)S(1)} %get-tuple-element.19), channel_id=1, source_target_pairs={{0,6},{2,0},{4,2},{6,4},{1,7},{3,1},{5,3},{7,5},{8,14},{10,8},{12,... | collective-permute-start | bytes 49160 | tf_op jit(solution)/shard_map/ppermute | solution.py:237
  25.9 2.4 %collective-permute-start.2 = (bf16[64,128]{1,0:T(8,128)(2,1)S(1)}, bf16[64,128]{1,0:T(8,128)(2,1)S(1)}, u32[]{:S(2)}, u32[]{:S(2)}) collective-permute-start(bf16[64,128]{1,0:T(8,128)(2,1)S(1)} %get-tuple-element.20), channel_id=1, source_target_pairs={{0,4},{2,6},{4,0},{6,2},{1,5},{3,7},{5,1},{7,3},{8,12},{10,14},{12... | collective-permute-start | bytes 49160 | tf_op jit(solution)/shard_map/ppermute | solution.py:237
  28.3 2.5 %collective-permute-start.1 = (bf16[64,128]{1,0:T(8,128)(2,1)S(1)}, bf16[64,128]{1,0:T(8,128)(2,1)S(1)}, u32[]{:S(2)}, u32[]{:S(2)}) collective-permute-start(bf16[64,128]{1,0:T(8,128)(2,1)S(1)} %get-tuple-element.21), channel_id=1, source_target_pairs={{0,2},{2,4},{4,6},{6,0},{1,3},{3,5},{5,7},{7,1},{8,10},{10,12},{12... | collective-permute-start | bytes 49160 | tf_op jit(solution)/shard_map/ppermute | solution.py:237
  30.8 3.1 %collective-permute-start.5 = (bf16[8,128,128]{2,1,0:T(8,128)(2,1)S(1)}, bf16[8,128,128]{2,1,0:T(8,128)(2,1)S(1)}, u32[]{:S(2)}, u32[]{:S(2)}) collective-permute-start(bf16[8,128,128]{2,1,0:T(8,128)(2,1)S(1)} %copy-done.6), channel_id=1, source_target_pairs={{0,1},{1,0},{2,3},{3,2},{4,5},{5,4},{6,7},{7,6},{8,9},{9,8},{10,11... | collective-permute-start | bytes 786440 | tf_op jit(solution)/shard_map/ppermute | solution.py:237
  34.0 12.8 %all-to-all-done.kv_ref = bf16[32,136,128]{2,1,0:T(8,128)(2,1)S(1)} async-done(((bf16[32,136,128]{2,1,0:T(8,128)(2,1)}), bf16[32,136,128]{2,1,0:T(8,128)(2,1)S(1)}, u32[]{:S(2)}, u32[]{:S(2)}) %all-to-all-start) | async-done | bytes 1114144 | tf_op jit(solution)/shard_map/all_to_all | solution.py:256
  46.7 6.0 %collective-permute-start = (bf16[32,136,128]{2,1,0:T(8,128)(2,1)S(1)}, bf16[32,136,128]{2,1,0:T(8,128)(2,1)S(1)}, u32[]{:S(2)}, u32[]{:S(2)}) collective-permute-start(bf16[32,136,128]{2,1,0:T(8,128)(2,1)S(1)} %all-to-all-done.kv_ref), channel_id=1, source_target_pairs={{0,8},{8,0},{1,9},{9,1},{2,10},{10,2},{3,11},{11,3},{4,12},{12,4},... | collective-permute-start | bytes 3342344 | tf_op jit(solution)/shard_map/ppermute | solution.py:237
  52.7 0.7 slice.30
  53.5 4.4 %collective-permute-start.8 = (bf16[16,128,128]{2,1,0:T(8,128)(2,1)S(1)}, bf16[16,128,128]{2,1,0:T(8,128)(2,1)S(1)}, u32[]{:S(2)}, u32[]{:S(2)}) collective-permute-start(bf16[16,128,128]{2,1,0:T(8,128)(2,1)S(1)} %constant_dynamic-update-slice_fusion.refs_0_), channel_id=1, source_target_pairs={{0,6},{2,0},{4,2},{6,4},{1,7},{3,1},{5,3},{7,5},{8,14},{10,8},{12,... | collective-permute-start | bytes 1572872 | tf_op jit(solution)/shard_map/ppermute | solution.py:237
  57.9 2.4 %collective-permute-start.7 = (bf16[16,128,128]{2,1,0:T(8,128)(2,1)S(1)}, bf16[16,128,128]{2,1,0:T(8,128)(2,1)}, u32[]{:S(2)}, u32[]{:S(2)}) collective-permute-start(bf16[16,128,128]{2,1,0:T(8,128)(2,1)S(1)} %constant_dynamic-update-slice_fusion.refs_0_), channel_id=1, source_target_pairs={{0,4},{2,6},{4,0},{6,2},{1,5},{3,7},{5,1},{7,3},{8,12},{10,14},{12... | collective-permute-start | bytes 1572872 | tf_op jit(solution)/shard_map/ppermute | solution.py:237
  60.3 2.5 %collective-permute-start.6 = (bf16[16,128,128]{2,1,0:T(8,128)(2,1)S(1)}, bf16[16,128,128]{2,1,0:T(8,128)(2,1)}, u32[]{:S(2)}, u32[]{:S(2)}) collective-permute-start(bf16[16,128,128]{2,1,0:T(8,128)(2,1)S(1)} %constant_dynamic-update-slice_fusion.refs_0_), channel_id=1, source_target_pairs={{0,2},{2,4},{4,6},{6,0},{1,3},{3,5},{5,7},{7,1},{8,10},{10,12},{12... | collective-permute-start | bytes 1572872 | tf_op jit(solution)/shard_map/ppermute | solution.py:237
  62.9 3.1 %collective-permute-start.4 = (bf16[4,32,128]{2,1,0:T(8,128)(2,1)S(1)}, bf16[4,32,128]{2,1,0:T(8,128)(2,1)S(1)}, u32[]{:S(2)}, u32[]{:S(2)}) collective-permute-start(bf16[4,32,128]{2,1,0:T(8,128)(2,1)S(1)} %pad_maximum_fusion), channel_id=1, source_target_pairs={{0,1},{1,0},{2,3},{3,2},{4,5},{5,4},{6,7},{7,6},{8,9},{9,8},{10,11... | collective-permute-start | bytes 98312 | tf_op jit(solution)/shard_map/ppermute | solution.py:237
  66.1 1.8 %collective-permute-done.4.refs_4_ = bf16[4,32,128]{2,1,0:T(8,128)(2,1)S(1)} collective-permute-done((bf16[4,32,128]{2,1,0:T(8,128)(2,1)S(1)}, bf16[4,32,128]{2,1,0:T(8,128)(2,1)S(1)}, u32[]{:S(2)}, u32[]{:S(2)}) %collective-permute-start.4) | collective-permute-done | bytes 32800 | tf_op jit(solution)/shard_map/ppermute | solution.py:237
  68.0 1.7 %attend_own.1 = (f32[256,128]{1,0:T(8,128)S(1)}, f32[256,128]{1,0:T(8,128)S(1)}, f32[256,128]{1,0:T(8,128)S(1)}) custom-call(s32[4]{0:T(128)S(1)} %pad_add_fusion.1.at_ref, bf16[32,136,128]{2,1,0:T(8,128)(2,1)S(1)} %all-to-all-done.kv_ref, bf16[64,128]{1,0:T(8,128)(2,1)S(1)} %get-tuple-element.22.refs_0_, ...), custom_call_target="tpu_custom_call" | custom-call | tf_op jit(solution)/shard_map/attend_own/pallas_call | solution.py:289
  69.7 2.5 %attend.1 = bf16[8,32,128]{2,1,0:T(8,128)(2,1)} custom-call(s32[4]{0:T(128)S(1)} %pad_add_fusion.1.at_ref, bf16[32,136,128]{2,1,0:T(8,128)(2,1)S(1)} %collective-permute-done.kv_ref, bf16[64,128]{1,0:T(8,128)(2,1)S(1)} %get-tuple-element.22.refs_0_, bf16[64,128]{1,0:T(8,128)(2,1)S(1)} %collective-permute-done.1.refs_1_, ...), custom_call_target="tpu_custom_call" | custom-call | tf_op jit(solution)/shard_map/attend/pallas_call | solution.py:298
  72.3 4.3 %all-to-all-start.1 = ((bf16[8,32,128]{2,1,0:T(8,128)(2,1)}), bf16[8,32,128]{2,1,0:T(8,128)(2,1)S(1)}, u32[]{:S(2)}, u32[]{:S(2)}) async-start(bf16[8,32,128]{2,1,0:T(8,128)(2,1)} %attend.1), calls=%async_computation.1 | async-start | bytes 131072 | tf_op jit(solution)/shard_map/all_to_all | solution.py:307
  76.6 3.9 %collective-permute-done.8.refs_3_ = bf16[16,128,128]{2,1,0:T(8,128)(2,1)S(1)} collective-permute-done((bf16[16,128,128]{2,1,0:T(8,128)(2,1)S(1)}, bf16[16,128,128]{2,1,0:T(8,128)(2,1)S(1)}, u32[]{:S(2)}, u32[]{:S(2)}) %collective-permute-start.8) | collective-permute-done | bytes 524320 | tf_op jit(solution)/shard_map/ppermute | solution.py:237
  80.5 0.8 copy-done.3
  81.3 5.6 %collective-permute-done.6.refs_1_ = bf16[16,128,128]{2,1,0:T(8,128)(2,1)} collective-permute-done((bf16[16,128,128]{2,1,0:T(8,128)(2,1)S(1)}, bf16[16,128,128]{2,1,0:T(8,128)(2,1)}, u32[]{:S(2)}, u32[]{:S(2)}) %collective-permute-start.6) | collective-permute-done | bytes 524320 | tf_op jit(solution)/shard_map/ppermute | solution.py:237
  86.9 1.0 copy-done.2
  88.0 1.0 copy-done.4
  89.0 1.3 join.1.refs_0_
  90.3 2.5 %collective-permute-start.9 = (bf16[64,128,128]{2,1,0:T(8,128)(2,1)S(1)}, bf16[64,128,128]{2,1,0:T(8,128)(2,1)}, u32[]{:S(2)}, u32[]{:S(2)}) collective-permute-start(bf16[64,128,128]{2,1,0:T(8,128)(2,1)S(1)} %join.1.refs_0_), channel_id=1, source_target_pairs={{0,8},{8,0},{1,9},{9,1},{2,10},{10,2},{3,11},{11,3},{4,12},{12,4},... | collective-permute-start | bytes 6291464 | tf_op jit(solution)/shard_map/ppermute | solution.py:237
  93.1 0.9 copy-done
  94.1 10.0 %all-to-all-start.2 = ((bf16[32,128,128]{2,1,0:T(8,128)(2,1)}), bf16[32,128,128]{2,1,0:T(8,128)(2,1)}, u32[]{:S(2)}, u32[]{:S(2)}) async-start(bf16[32,128,128]{2,1,0:T(8,128)(2,1)} %copy-done), calls=%async_computation.2 | async-start | bytes 2097152 | tf_op jit(solution)/shard_map/all_to_all | solution.py:316
  104.2 28.3 %all-to-all-done.2.rows_ref = bf16[32,128,128]{2,1,0:T(8,128)(2,1)} async-done(((bf16[32,128,128]{2,1,0:T(8,128)(2,1)}), bf16[32,128,128]{2,1,0:T(8,128)(2,1)}, u32[]{:S(2)}, u32[]{:S(2)}) %all-to-all-start.2) | async-done | bytes 1048608 | tf_op jit(solution)/shard_map/all_to_all | solution.py:316
  132.5 4.5 %project.1 = (bf16[256,128]{1,0:T(8,128)(2,1)S(1)}, bf16[256,128]{1,0:T(8,128)(2,1)S(1)}) custom-call(s32[3]{0:T(128)S(1)} %pad_add_fusion.at_ref, bf16[32,128,128]{2,1,0:T(8,128)(2,1)} %all-to-all-done.2.rows_ref, bf16[32,136,128]{2,1,0:T(8,128)(2,1)S(1)} %all-to-all-done.kv_ref, bf16[64,128,128]{2,1,0:T(8,128)(2,1)S(1)} %join.1.refs_0_, ...), custom_call_target="tpu_custom_call" | custom-call | tf_op jit(solution)/shard_map/project/pallas_call | solution.py:317
  137.0 3.7 %collective-permute-start.10 = (bf16[256,128]{1,0:T(8,128)(2,1)S(1)}, bf16[256,128]{1,0:T(8,128)(2,1)S(1)}, u32[]{:S(2)}, u32[]{:S(2)}) collective-permute-start(bf16[256,128]{1,0:T(8,128)(2,1)S(1)} %get-tuple-element.18), channel_id=1, source_target_pairs={{0,8},{8,0},{1,9},{9,1},{2,10},{10,2},{3,11},{11,3},{4,12},{12,4},... | collective-permute-start | bytes 196616 | tf_op jit(solution)/shard_map/ppermute | solution.py:237
  141.6 0.8 bitcast_select_fusion
  (31 shorter events, 1.5 us)
Async XLA Ops:
  2.2 28.7 %copy-start.6 = (bf16[8,128,128]{2,1,0:T(8,128)(2,1)S(1)}, bf16[8,128,128]{2,1,0:T(8,128)(2,1)}, u32[]{:S(2)}) copy-start(bf16[8,128,128]{2,1,0:T(8,128)(2,1)} %param.11) | copy-start | bytes 786436
  2.2 44.5 %all-to-all-start = ((bf16[32,136,128]{2,1,0:T(8,128)(2,1)}), bf16[32,136,128]{2,1,0:T(8,128)(2,1)S(1)}, u32[]{:S(2)}, u32[]{:S(2)}) async-start(bf16[32,136,128]{2,1,0:T(8,128)(2,1)} %prep_kv.1), calls=%async_computation | async-start | bytes 2228224 | tf_op jit(solution)/shard_map/all_to_all | solution.py:256
  21.5 31.9 %collective-permute-start.3 = (bf16[64,128]{1,0:T(8,128)(2,1)S(1)}, bf16[64,128]{1,0:T(8,128)(2,1)S(1)}, u32[]{:S(2)}, u32[]{:S(2)}) collective-permute-start(bf16[64,128]{1,0:T(8,128)(2,1)S(1)} %get-tuple-element.19), channel_id=1, source_target_pairs={{0,6},{2,0},{4,2},{6,4},{1,7},{3,1},{5,3},{7,5},{8,14},{10,8},{12,... | collective-permute-start | bytes 49160 | tf_op jit(solution)/shard_map/ppermute | solution.py:237
  25.9 34.5 %collective-permute-start.2 = (bf16[64,128]{1,0:T(8,128)(2,1)S(1)}, bf16[64,128]{1,0:T(8,128)(2,1)S(1)}, u32[]{:S(2)}, u32[]{:S(2)}) collective-permute-start(bf16[64,128]{1,0:T(8,128)(2,1)S(1)} %get-tuple-element.20), channel_id=1, source_target_pairs={{0,4},{2,6},{4,0},{6,2},{1,5},{3,7},{5,1},{7,3},{8,12},{10,14},{12... | collective-permute-start | bytes 49160 | tf_op jit(solution)/shard_map/ppermute | solution.py:237
  28.3 34.6 %collective-permute-start.1 = (bf16[64,128]{1,0:T(8,128)(2,1)S(1)}, bf16[64,128]{1,0:T(8,128)(2,1)S(1)}, u32[]{:S(2)}, u32[]{:S(2)}) collective-permute-start(bf16[64,128]{1,0:T(8,128)(2,1)S(1)} %get-tuple-element.21), channel_id=1, source_target_pairs={{0,2},{2,4},{4,6},{6,0},{1,3},{3,5},{5,7},{7,1},{8,10},{10,12},{12... | collective-permute-start | bytes 49160 | tf_op jit(solution)/shard_map/ppermute | solution.py:237
  30.8 22.6 %collective-permute-start.5 = (bf16[8,128,128]{2,1,0:T(8,128)(2,1)S(1)}, bf16[8,128,128]{2,1,0:T(8,128)(2,1)S(1)}, u32[]{:S(2)}, u32[]{:S(2)}) collective-permute-start(bf16[8,128,128]{2,1,0:T(8,128)(2,1)S(1)} %copy-done.6), channel_id=1, source_target_pairs={{0,1},{1,0},{2,3},{3,2},{4,5},{5,4},{6,7},{7,6},{8,9},{9,8},{10,11... | collective-permute-start | bytes 786440 | tf_op jit(solution)/shard_map/ppermute | solution.py:237
  46.7 23.0 %collective-permute-start = (bf16[32,136,128]{2,1,0:T(8,128)(2,1)S(1)}, bf16[32,136,128]{2,1,0:T(8,128)(2,1)S(1)}, u32[]{:S(2)}, u32[]{:S(2)}) collective-permute-start(bf16[32,136,128]{2,1,0:T(8,128)(2,1)S(1)} %all-to-all-done.kv_ref), channel_id=1, source_target_pairs={{0,8},{8,0},{1,9},{9,1},{2,10},{10,2},{3,11},{11,3},{4,12},{12,4},... | collective-permute-start | bytes 3342344 | tf_op jit(solution)/shard_map/ppermute | solution.py:237
  53.5 18.8 %copy-start.1 = (bf16[16,128,128]{2,1,0:T(8,128)(2,1)}, bf16[16,128,128]{2,1,0:T(8,128)(2,1)S(1)}, u32[]{:S(2)}) copy-start(bf16[16,128,128]{2,1,0:T(8,128)(2,1)S(1)} %constant_dynamic-update-slice_fusion.refs_0_) | copy-start | bytes 1572868
  53.5 27.0 %collective-permute-start.8 = (bf16[16,128,128]{2,1,0:T(8,128)(2,1)S(1)}, bf16[16,128,128]{2,1,0:T(8,128)(2,1)S(1)}, u32[]{:S(2)}, u32[]{:S(2)}) collective-permute-start(bf16[16,128,128]{2,1,0:T(8,128)(2,1)S(1)} %constant_dynamic-update-slice_fusion.refs_0_), channel_id=1, source_target_pairs={{0,6},{2,0},{4,2},{6,4},{1,7},{3,1},{5,3},{7,5},{8,14},{10,8},{12,... | collective-permute-start | bytes 1572872 | tf_op jit(solution)/shard_map/ppermute | solution.py:237
  57.9 23.4 %collective-permute-start.7 = (bf16[16,128,128]{2,1,0:T(8,128)(2,1)S(1)}, bf16[16,128,128]{2,1,0:T(8,128)(2,1)}, u32[]{:S(2)}, u32[]{:S(2)}) collective-permute-start(bf16[16,128,128]{2,1,0:T(8,128)(2,1)S(1)} %constant_dynamic-update-slice_fusion.refs_0_), channel_id=1, source_target_pairs={{0,4},{2,6},{4,0},{6,2},{1,5},{3,7},{5,1},{7,3},{8,12},{10,14},{12... | collective-permute-start | bytes 1572872 | tf_op jit(solution)/shard_map/ppermute | solution.py:237
  60.3 26.6 %collective-permute-start.6 = (bf16[16,128,128]{2,1,0:T(8,128)(2,1)S(1)}, bf16[16,128,128]{2,1,0:T(8,128)(2,1)}, u32[]{:S(2)}, u32[]{:S(2)}) collective-permute-start(bf16[16,128,128]{2,1,0:T(8,128)(2,1)S(1)} %constant_dynamic-update-slice_fusion.refs_0_), channel_id=1, source_target_pairs={{0,2},{2,4},{4,6},{6,0},{1,3},{3,5},{5,7},{7,1},{8,10},{10,12},{12... | collective-permute-start | bytes 1572872 | tf_op jit(solution)/shard_map/ppermute | solution.py:237
  62.9 5.1 %collective-permute-start.4 = (bf16[4,32,128]{2,1,0:T(8,128)(2,1)S(1)}, bf16[4,32,128]{2,1,0:T(8,128)(2,1)S(1)}, u32[]{:S(2)}, u32[]{:S(2)}) collective-permute-start(bf16[4,32,128]{2,1,0:T(8,128)(2,1)S(1)} %pad_maximum_fusion), channel_id=1, source_target_pairs={{0,1},{1,0},{2,3},{3,2},{4,5},{5,4},{6,7},{7,6},{8,9},{9,8},{10,11... | collective-permute-start | bytes 98312 | tf_op jit(solution)/shard_map/ppermute | solution.py:237
  72.3 20.5 %copy-start.5 = (bf16[128,256]{1,0:T(8,128)(2,1)S(1)}, bf16[128,256]{1,0:T(8,128)(2,1)}, u32[]{:S(2)}) copy-start(bf16[128,256]{1,0:T(8,128)(2,1)} %get-tuple-element.12.back_ref) | copy-start | bytes 196612
  72.3 20.5 %all-to-all-start.1 = ((bf16[8,32,128]{2,1,0:T(8,128)(2,1)}), bf16[8,32,128]{2,1,0:T(8,128)(2,1)S(1)}, u32[]{:S(2)}, u32[]{:S(2)}) async-start(bf16[8,32,128]{2,1,0:T(8,128)(2,1)} %attend.1), calls=%async_computation.1 | async-start | bytes 131072 | tf_op jit(solution)/shard_map/all_to_all | solution.py:307
  80.5 0.8 copy-start.3
  86.9 1.0 copy-start.2
  88.0 1.0 copy-start.4
  90.3 13.9 %collective-permute-start.9 = (bf16[64,128,128]{2,1,0:T(8,128)(2,1)S(1)}, bf16[64,128,128]{2,1,0:T(8,128)(2,1)}, u32[]{:S(2)}, u32[]{:S(2)}) collective-permute-start(bf16[64,128,128]{2,1,0:T(8,128)(2,1)S(1)} %join.1.refs_0_), channel_id=1, source_target_pairs={{0,8},{8,0},{1,9},{9,1},{2,10},{10,2},{3,11},{11,3},{4,12},{12,4},... | collective-permute-start | bytes 6291464 | tf_op jit(solution)/shard_map/ppermute | solution.py:237
  93.1 1.0 copy-start
  94.1 38.4 %all-to-all-start.2 = ((bf16[32,128,128]{2,1,0:T(8,128)(2,1)}), bf16[32,128,128]{2,1,0:T(8,128)(2,1)}, u32[]{:S(2)}, u32[]{:S(2)}) async-start(bf16[32,128,128]{2,1,0:T(8,128)(2,1)} %copy-done), calls=%async_computation.2 | async-start | bytes 2097152 | tf_op jit(solution)/shard_map/all_to_all | solution.py:316
  137.0 4.6 %collective-permute-start.10 = (bf16[256,128]{1,0:T(8,128)(2,1)S(1)}, bf16[256,128]{1,0:T(8,128)(2,1)S(1)}, u32[]{:S(2)}, u32[]{:S(2)}) collective-permute-start(bf16[256,128]{1,0:T(8,128)(2,1)S(1)} %get-tuple-element.18), channel_id=1, source_target_pairs={{0,8},{8,0},{1,9},{9,1},{2,10},{10,2},{3,11},{11,3},{4,12},{12,4},... | collective-permute-start | bytes 196616 | tf_op jit(solution)/shard_map/ppermute | solution.py:237

commit v6 on v4

--- a/solution.py
+++ b/solution.py
@@ -37,7 +37,8 @@
 
 
 def prep_kernel(
-    q_ref, k_ref, v_ref, ids_ref, logit_ref, w_ref, kvsend_ref, back_ref, qnear_ref, cargo_ref
+    q_ref, k_ref, v_ref, ids_ref, logit_ref, w_ref,
+    kvsend_ref, back_ref, qnear_ref, cargo_ref, chunk_ref, sems,
 ):
     x = lax.axis_index("x")
     zl = lax.axis_index("zl")
@@ -49,6 +50,14 @@
         return jnp.sum(jnp.where(own, wide, 0.0), axis=0, keepdims=True)
 
     id_row = as_row(ids_ref[...].astype(f32))
+    chunk_ref[0:SPAN] = k_ref[...]
+    chunk_ref[SPAN : 2 * SPAN] = v_ref[...]
+    chunk_ref[2 * SPAN : KVROWS] = jnp.broadcast_to(id_row, (8, ROWS)).astype(bf16)
+    copies = [
+        pltpu.make_async_copy(chunk_ref, kvsend_ref.at[i], sems.at[i]) for i in range(CHIPS)
+    ]
+    for copy in copies:
+        copy.start()
     gate_exp = jnp.exp(logit_ref[...])
     gate_row = as_row(gate_exp / jnp.sum(gate_exp, axis=1, keepdims=True))
     id_int = id_row.astype(jnp.int32)
@@ -79,17 +88,8 @@
     lane = iota((ROWS, ROWS), 1)
     back_ref[:, :ROWS] = (lane == slot_col).astype(bf16)
     back_ref[:, ROWS:] = (lane + ROWS == slot_col).astype(bf16)
-    keys = k_ref[...]
-    values = v_ref[...]
-    ids = jnp.broadcast_to(id_row, (8, ROWS)).astype(bf16)
-
-    def fill(i, _):
-        kvsend_ref[i, 0:SPAN] = keys
-        kvsend_ref[i, SPAN : 2 * SPAN] = values
-        kvsend_ref[i, 2 * SPAN : KVROWS] = ids
-        return 0
-
-    lax.fori_loop(0, CHIPS, fill, 0)
+    for copy in copies:
+        copy.wait()
 
 
 def attend_half(at_ref, kv_ref, q_refs, s_ref, parity, best):
@@ -161,16 +161,15 @@
         out_ref[sources[d]] = result[d * SLOTS : (d + 1) * SLOTS]
 
 
-def compact_kernel(back_ref, got_ref, out_ref):
-    rows = jnp.dot(
+def compact_kernel(back_ref, got_ref, out_ref, rows_ref, sems):
+    rows_ref[...] = jnp.dot(
         back_ref[...], got_ref[...].reshape(GROUPS * SLOTS, HD), preferred_element_type=f32
     ).astype(bf16)
-
-    def fill(i, _):
-        out_ref[i] = rows
-        return 0
-
-    lax.fori_loop(0, CHIPS, fill, 0)
+    copies = [pltpu.make_async_copy(rows_ref, out_ref.at[i], sems.at[i]) for i in range(CHIPS)]
+    for copy in copies:
+        copy.start()
+    for copy in copies:
+        copy.wait()
 
 
 def join_kernel(*refs):
@@ -246,7 +245,8 @@
     kvsend, back, qnear, cargo = pl.pallas_call(
         prep_kernel,
         in_specs=[VMEM] * 6,
-        out_specs=[VMEM] * 4,
+        out_specs=[HBM] + [VMEM] * 3,
+        scratch_shapes=[pltpu.VMEM((KVROWS, HD), bf16), pltpu.SemaphoreType.DMA((CHIPS,))],
         out_shape=[
             shape((CHIPS, KVROWS, HD), bf16),
             shape((ROWS, GROUPS * SLOTS), bf16),
@@ -308,8 +308,9 @@
     rows = pl.pallas_call(
         compact_kernel,
         in_specs=[VMEM, VMEM],
-        out_specs=VMEM,
+        out_specs=HBM,
         out_shape=shape((CHIPS, ROWS, HD), bf16),
+        scratch_shapes=[pltpu.VMEM((ROWS, HD), bf16), pltpu.SemaphoreType.DMA((CHIPS,))],
         compiler_params=pltpu.CompilerParams(vmem_limit_bytes=8 << 20),
         name="compact",
     )(back, home)

time: 171 us -> 174 us (1.018)
  Pallas kernels: 13.2 us -> 15.3 us
    pallas_call x2, Pallas kernels: 3.19 us -> 5.31 us  [the longest x1 3.46 us: run(): pl.pallas_call(prep_kernel, in_specs=[VMEM] * 6, out_specs=[HBM] + [VMEM]...]
  transfers between devices with their start and end apart: 12 -> 12, of which waited for: 6 -> 6; matrix products, arithmetic and copies ran while one was open for 0% -> 0% of each run, Pallas kernels for 3% -> 4%
where the time goes in v6:
time: 174 us; the launch traced here: 171 us
  waiting for transfers between devices  57.5 us (33%)
  blocking collectives  49.6 us (29%)
  starting transfers between devices  43.2 us (25%)
  Pallas kernels  15.3 us (9%)
  local copies, waits for them, and re-layouts  4.04 us (2%)
    all_to_all x1, blocking collectives, run(): kva = lax.all_to_all(kvsend, ('zh', 'y'), 0, 0, tiled=True)  49.6 us
    ppermute x10, starting transfers between devices, shifted(): return lax.ppermute(x, axis, [(i, (i + by) % count) for i in range(count)])  35 us
    ppermute x10, waiting for transfers between devices, shifted(): return lax.ppermute(x, axis, [(i, (i + by) % count) for i in range(count)])  29.2 us
    all_to_all x1, waiting for transfers between devices, run(): rows = lax.all_to_all(rows, ('zh', 'y'), 0, 0, tiled=True)  28.2 us
    all_to_all x1, starting transfers between devices, run(): rows = lax.all_to_all(rows, ('zh', 'y'), 0, 0, tiled=True)  4.68 us
    pallas_call x1, Pallas kernels, run(): pl.pallas_call(project_kernel, in_specs=[SMEM] + [VMEM] * 2 + [HBM] * 2,...  4.47 us
    unnamed x18, local copies, waits for them, and re-layouts  3.84 us
    all_to_all x1, starting transfers between devices, run(): home = lax.all_to_all(attended, ('x', 'zl'), 0, 0, tiled=True)  3.48 us
  transfers between devices with their start and end apart: 12, of which 6 were waited for; matrix products, arithmetic and copies ran while one was open for 0% of the time, Pallas kernels for 4%

profile of v6, /device:TPU:1, one launch (start us, length us, event | category | flops | bytes accessed | tf_op | source)
XLA Modules:
  0.0 170.9 jit_solution(9499003640586262138)
XLA Ops:
  0.0 3.5 %prep.1 = (bf16[32,136,128]{2,1,0:T(8,128)(2,1)}, bf16[128,256]{1,0:T(8,128)(2,1)}, bf16[4,32,128]{2,1,0:T(8,128)(2,1)}, bf16[1152,128]{1,0:T(8,128)(2,1)}) custom-call(bf16[128,128]{1,0:T(8,128)(2,1)} %bitcast.27, bf16[64,128]{1,0:T(8,128)(2,1)} %bitcast.28, bf16[64,128]{1,0:T(8,128)(2,1)} %bitcast.29, s32[8,16]{1,0:T(8,128)} %ids_ref.1, ...), custom_call_target="tpu_custom_call" | custom-call | tf_op jit(solution)/shard_map/prep/pallas_call | solution.py:245
  3.5 49.6 %all_to_all.15.kv_ref = bf16[32,136,128]{2,1,0:T(8,128)(2,1)S(1)} all-to-all(bf16[32,136,128]{2,1,0:T(8,128)(2,1)} %get-tuple-element.15), channel_id=1, replica_groups=mesh['zh'=4,'y'=8,'core'=2,'x'=4,'zl'=2] {'zh','y'}, dimensions={0} | all-to-all | bytes 2228224 | tf_op jit(solution)/shard_map/all_to_all | solution.py:265
  53.1 4.1 %collective-permute-start = (bf16[32,136,128]{2,1,0:T(8,128)(2,1)S(1)}, bf16[32,136,128]{2,1,0:T(8,128)(2,1)S(1)}, u32[]{:S(2)}, u32[]{:S(2)}) collective-permute-start(bf16[32,136,128]{2,1,0:T(8,128)(2,1)S(1)} %all_to_all.15.kv_ref), channel_id=1, source_target_pairs={{0,8},{8,0},{1,9},{9,1},{2,10},{10,2},{3,11},{11,3},{4,12},{12,4},... | collective-permute-start | bytes 3342344 | tf_op jit(solution)/shard_map/ppermute | solution.py:235
  57.2 3.1 %collective-permute-start.1 = (bf16[1152,128]{1,0:T(8,128)(2,1)S(1)}, bf16[1152,128]{1,0:T(8,128)(2,1)S(1)}, u32[]{:S(2)}, u32[]{:S(2)}) collective-permute-start(bf16[1152,128]{1,0:T(8,128)(2,1)S(1)} %copy-done.8), channel_id=1, source_target_pairs={{0,1},{1,0},{2,3},{3,2},{4,5},{5,4},{6,7},{7,6},{8,9},{9,8},{10,11... | collective-permute-start | bytes 884744 | tf_op jit(solution)/shard_map/ppermute | solution.py:235
  60.3 7.3 %collective-permute-done.1 = bf16[1152,128]{1,0:T(8,128)(2,1)S(1)} collective-permute-done((bf16[1152,128]{1,0:T(8,128)(2,1)S(1)}, bf16[1152,128]{1,0:T(8,128)(2,1)S(1)}, u32[]{:S(2)}, u32[]{:S(2)}) %collective-permute-start.1) | collective-permute-done | bytes 294944 | tf_op jit(solution)/shard_map/ppermute | solution.py:235
  67.8 4.4 %collective-permute-start.7 = (bf16[16,128,128]{2,1,0:T(8,128)(2,1)S(1)}, bf16[16,128,128]{2,1,0:T(8,128)(2,1)S(1)}, u32[]{:S(2)}, u32[]{:S(2)}) collective-permute-start(bf16[16,128,128]{2,1,0:T(8,128)(2,1)S(1)} %pad_maximum_fusion.refs_0_), channel_id=1, source_target_pairs={{0,6},{2,0},{4,2},{6,4},{1,7},{3,1},{5,3},{7,5},{8,14},{10,8},{12,... | collective-permute-start | bytes 1572872 | tf_op jit(solution)/shard_map/ppermute | solution.py:235
  72.2 2.4 %collective-permute-start.6 = (bf16[16,128,128]{2,1,0:T(8,128)(2,1)S(1)}, bf16[16,128,128]{2,1,0:T(8,128)(2,1)}, u32[]{:S(2)}, u32[]{:S(2)}) collective-permute-start(bf16[16,128,128]{2,1,0:T(8,128)(2,1)S(1)} %pad_maximum_fusion.refs_0_), channel_id=1, source_target_pairs={{0,4},{2,6},{4,0},{6,2},{1,5},{3,7},{5,1},{7,3},{8,12},{10,14},{12... | collective-permute-start | bytes 1572872 | tf_op jit(solution)/shard_map/ppermute | solution.py:235
  74.6 2.5 %collective-permute-start.5 = (bf16[16,128,128]{2,1,0:T(8,128)(2,1)S(1)}, bf16[16,128,128]{2,1,0:T(8,128)(2,1)}, u32[]{:S(2)}, u32[]{:S(2)}) collective-permute-start(bf16[16,128,128]{2,1,0:T(8,128)(2,1)S(1)} %pad_maximum_fusion.refs_0_), channel_id=1, source_target_pairs={{0,2},{2,4},{4,6},{6,0},{1,3},{3,5},{5,7},{7,1},{8,10},{10,12},{12... | collective-permute-start | bytes 1572872 | tf_op jit(solution)/shard_map/ppermute | solution.py:235
  77.2 4.0 %collective-permute-start.4 = (bf16[64,128]{1,0:T(8,128)(2,1)S(1)}, bf16[64,128]{1,0:T(8,128)(2,1)S(1)}, u32[]{:S(2)}, u32[]{:S(2)}) collective-permute-start(bf16[64,128]{1,0:T(8,128)(2,1)S(1)} %get-tuple-element.23), channel_id=1, source_target_pairs={{0,6},{2,0},{4,2},{6,4},{1,7},{3,1},{5,3},{7,5},{8,14},{10,8},{12,... | collective-permute-start | bytes 49160 | tf_op jit(solution)/shard_map/ppermute | solution.py:235
  81.2 12.9 %collective-permute-done.4.refs_3_ = bf16[64,128]{1,0:T(8,128)(2,1)S(1)} collective-permute-done((bf16[64,128]{1,0:T(8,128)(2,1)S(1)}, bf16[64,128]{1,0:T(8,128)(2,1)S(1)}, u32[]{:S(2)}, u32[]{:S(2)}) %collective-permute-start.4) | collective-permute-done | bytes 16416 | tf_op jit(solution)/shard_map/ppermute | solution.py:235
  94.0 1.9 %collective-permute-start.2 = (bf16[64,128]{1,0:T(8,128)(2,1)S(1)}, bf16[64,128]{1,0:T(8,128)(2,1)S(1)}, u32[]{:S(2)}, u32[]{:S(2)}) collective-permute-start(bf16[64,128]{1,0:T(8,128)(2,1)S(1)} %get-tuple-element.25), channel_id=1, source_target_pairs={{0,2},{2,4},{4,6},{6,0},{1,3},{3,5},{5,7},{7,1},{8,10},{10,12},{12... | collective-permute-start | bytes 49160 | tf_op jit(solution)/shard_map/ppermute | solution.py:235
  96.0 5.0 %collective-permute-done.2.refs_1_ = bf16[64,128]{1,0:T(8,128)(2,1)S(1)} collective-permute-done((bf16[64,128]{1,0:T(8,128)(2,1)S(1)}, bf16[64,128]{1,0:T(8,128)(2,1)S(1)}, u32[]{:S(2)}, u32[]{:S(2)}) %collective-permute-start.2) | collective-permute-done | bytes 16416 | tf_op jit(solution)/shard_map/ppermute | solution.py:235
  100.9 2.5 %collective-permute-start.3 = (bf16[64,128]{1,0:T(8,128)(2,1)S(1)}, bf16[64,128]{1,0:T(8,128)(2,1)S(1)}, u32[]{:S(2)}, u32[]{:S(2)}) collective-permute-start(bf16[64,128]{1,0:T(8,128)(2,1)S(1)} %get-tuple-element.26), channel_id=1, source_target_pairs={{0,4},{2,6},{4,0},{6,2},{1,5},{3,7},{5,1},{7,3},{8,12},{10,14},{12... | collective-permute-start | bytes 49160 | tf_op jit(solution)/shard_map/ppermute | solution.py:235
  103.5 3.4 %collective-permute-done.3.refs_2_ = bf16[64,128]{1,0:T(8,128)(2,1)S(1)} collective-permute-done((bf16[64,128]{1,0:T(8,128)(2,1)S(1)}, bf16[64,128]{1,0:T(8,128)(2,1)S(1)}, u32[]{:S(2)}, u32[]{:S(2)}) %collective-permute-start.3) | collective-permute-done | bytes 16416 | tf_op jit(solution)/shard_map/ppermute | solution.py:235
  106.9 1.7 %attend_own.1 = (f32[256,128]{1,0:T(8,128)S(1)}, f32[256,128]{1,0:T(8,128)S(1)}, f32[256,128]{1,0:T(8,128)S(1)}) custom-call(s32[4]{0:T(128)S(1)} %pad_add_fusion.1.at_ref, bf16[32,136,128]{2,1,0:T(8,128)(2,1)S(1)} %all_to_all.15.kv_ref, bf16[64,128]{1,0:T(8,128)(2,1)S(1)} %get-tuple-element.24.refs_0_, bf16[64,128]{1,0:T(8,128)(2,1)S(1)} %collective-permute-done.2.refs_1_, ...), custom_call_target="tpu_custom_call" | custom-call | tf_op jit(solution)/shard_map/attend_own/pallas_call | solution.py:289
  108.6 2.6 %attend.1 = bf16[8,32,128]{2,1,0:T(8,128)(2,1)} custom-call(s32[4]{0:T(128)S(1)} %pad_add_fusion.1.at_ref, bf16[32,136,128]{2,1,0:T(8,128)(2,1)S(1)} %collective-permute-done.kv_ref, bf16[64,128]{1,0:T(8,128)(2,1)S(1)} %get-tuple-element.24.refs_0_, bf16[64,128]{1,0:T(8,128)(2,1)S(1)} %collective-permute-done.2.refs_1_, ...), custom_call_target="tpu_custom_call" | custom-call | tf_op jit(solution)/shard_map/attend/pallas_call | solution.py:298
  111.2 3.5 %all-to-all-start.1 = ((bf16[8,32,128]{2,1,0:T(8,128)(2,1)}), bf16[8,32,128]{2,1,0:T(8,128)(2,1)S(1)}, u32[]{:S(2)}, u32[]{:S(2)}) async-start(bf16[8,32,128]{2,1,0:T(8,128)(2,1)} %attend.1), calls=%async_computation.1 | async-start | bytes 131072 | tf_op jit(solution)/shard_map/all_to_all | solution.py:307
  114.7 0.8 copy-done.3
  115.5 1.0 copy-done.2
  116.6 1.0 copy-done.4
  117.6 1.3 join.1.refs_0_
  118.9 6.2 %collective-permute-start.8 = (bf16[64,128,128]{2,1,0:T(8,128)(2,1)S(1)}, bf16[64,128,128]{2,1,0:T(8,128)(2,1)}, u32[]{:S(2)}, u32[]{:S(2)}) collective-permute-start(bf16[64,128,128]{2,1,0:T(8,128)(2,1)S(1)} %join.1.refs_0_), channel_id=1, source_target_pairs={{0,8},{8,0},{1,9},{9,1},{2,10},{10,2},{3,11},{11,3},{4,12},{12,4},... | collective-permute-start | bytes 6291464 | tf_op jit(solution)/shard_map/ppermute | solution.py:235
  125.1 1.8 %compact.1 = bf16[32,128,128]{2,1,0:T(8,128)(2,1)S(1)} custom-call(bf16[128,256]{1,0:T(8,128)(2,1)S(1)} %copy-done.5, bf16[8,32,128]{2,1,0:T(8,128)(2,1)S(1)} %all-to-all-done.1.got_ref), custom_call_target="tpu_custom_call" | custom-call | tf_op jit(solution)/shard_map/compact/pallas_call | solution.py:308
  126.9 0.9 copy-done
  127.9 4.7 %all-to-all-start.2 = ((bf16[32,128,128]{2,1,0:T(8,128)(2,1)}), bf16[32,128,128]{2,1,0:T(8,128)(2,1)}, u32[]{:S(2)}, u32[]{:S(2)}) async-start(bf16[32,128,128]{2,1,0:T(8,128)(2,1)} %copy-done), calls=%async_computation.2 | async-start | bytes 2097152 | tf_op jit(solution)/shard_map/all_to_all | solution.py:317
  132.6 28.2 %all-to-all-done.2.rows_ref = bf16[32,128,128]{2,1,0:T(8,128)(2,1)} async-done(((bf16[32,128,128]{2,1,0:T(8,128)(2,1)}), bf16[32,128,128]{2,1,0:T(8,128)(2,1)}, u32[]{:S(2)}, u32[]{:S(2)}) %all-to-all-start.2) | async-done | bytes 1048608 | tf_op jit(solution)/shard_map/all_to_all | solution.py:317
  160.9 4.5 %project.1 = (bf16[256,128]{1,0:T(8,128)(2,1)S(1)}, bf16[256,128]{1,0:T(8,128)(2,1)S(1)}) custom-call(s32[3]{0:T(128)S(1)} %pad_add_fusion.at_ref, bf16[32,128,128]{2,1,0:T(8,128)(2,1)} %all-to-all-done.2.rows_ref, bf16[32,136,128]{2,1,0:T(8,128)(2,1)S(1)} %all_to_all.15.kv_ref, bf16[64,128,128]{2,1,0:T(8,128)(2,1)S(1)} %join.1.refs_0_, ...), custom_call_target="tpu_custom_call" | custom-call | tf_op jit(solution)/shard_map/project/pallas_call | solution.py:318
  165.4 3.9 %collective-permute-start.9 = (bf16[256,128]{1,0:T(8,128)(2,1)S(1)}, bf16[256,128]{1,0:T(8,128)(2,1)S(1)}, u32[]{:S(2)}, u32[]{:S(2)}) collective-permute-start(bf16[256,128]{1,0:T(8,128)(2,1)S(1)} %get-tuple-element.22), channel_id=1, source_target_pairs={{0,8},{8,0},{1,9},{9,1},{2,10},{10,2},{3,11},{11,3},{4,12},{12,4},... | collective-permute-start | bytes 196616 | tf_op jit(solution)/shard_map/ppermute | solution.py:235
  169.3 0.1 iota.11
  169.4 0.1 iota.12
  169.5 0.7 collective-permute-done.9
  170.2 0.8 bitcast_select_fusion
  (27 shorter events, 0.3 us)
Async XLA Ops:
  3.5 53.8 %copy-start.8 = (bf16[1152,128]{1,0:T(8,128)(2,1)S(1)}, bf16[1152,128]{1,0:T(8,128)(2,1)}, u32[]{:S(2)}) copy-start(bf16[1152,128]{1,0:T(8,128)(2,1)} %get-tuple-element.17) | copy-start | bytes 884740
  3.5 64.2 %copy-start.6 = (bf16[8,128,128]{2,1,0:T(8,128)(2,1)S(1)}, bf16[8,128,128]{2,1,0:T(8,128)(2,1)}, u32[]{:S(2)}) copy-start(bf16[8,128,128]{2,1,0:T(8,128)(2,1)} %w_ref.1) | copy-start | bytes 786436
  53.1 24.0 %copy-start.7 = (bf16[4,32,128]{2,1,0:T(8,128)(2,1)S(1)}, bf16[4,32,128]{2,1,0:T(8,128)(2,1)}, u32[]{:S(2)}) copy-start(bf16[4,32,128]{2,1,0:T(8,128)(2,1)} %get-tuple-element.16) | copy-start | bytes 98308
  53.1 55.5 %collective-permute-start = (bf16[32,136,128]{2,1,0:T(8,128)(2,1)S(1)}, bf16[32,136,128]{2,1,0:T(8,128)(2,1)S(1)}, u32[]{:S(2)}, u32[]{:S(2)}) collective-permute-start(bf16[32,136,128]{2,1,0:T(8,128)(2,1)S(1)} %all_to_all.15.kv_ref), channel_id=1, source_target_pairs={{0,8},{8,0},{1,9},{9,1},{2,10},{10,2},{3,11},{11,3},{4,12},{12,4},... | collective-permute-start | bytes 3342344 | tf_op jit(solution)/shard_map/ppermute | solution.py:235
  57.2 10.4 %collective-permute-start.1 = (bf16[1152,128]{1,0:T(8,128)(2,1)S(1)}, bf16[1152,128]{1,0:T(8,128)(2,1)S(1)}, u32[]{:S(2)}, u32[]{:S(2)}) collective-permute-start(bf16[1152,128]{1,0:T(8,128)(2,1)S(1)} %copy-done.8), channel_id=1, source_target_pairs={{0,1},{1,0},{2,3},{3,2},{4,5},{5,4},{6,7},{7,6},{8,9},{9,8},{10,11... | collective-permute-start | bytes 884744 | tf_op jit(solution)/shard_map/ppermute | solution.py:235
  67.8 43.4 %copy-start.1 = (bf16[16,128,128]{2,1,0:T(8,128)(2,1)}, bf16[16,128,128]{2,1,0:T(8,128)(2,1)S(1)}, u32[]{:S(2)}) copy-start(bf16[16,128,128]{2,1,0:T(8,128)(2,1)S(1)} %pad_maximum_fusion.refs_0_) | copy-start | bytes 1572868
  67.8 46.9 %collective-permute-start.7 = (bf16[16,128,128]{2,1,0:T(8,128)(2,1)S(1)}, bf16[16,128,128]{2,1,0:T(8,128)(2,1)S(1)}, u32[]{:S(2)}, u32[]{:S(2)}) collective-permute-start(bf16[16,128,128]{2,1,0:T(8,128)(2,1)S(1)} %pad_maximum_fusion.refs_0_), channel_id=1, source_target_pairs={{0,6},{2,0},{4,2},{6,4},{1,7},{3,1},{5,3},{7,5},{8,14},{10,8},{12,... | collective-permute-start | bytes 1572872 | tf_op jit(solution)/shard_map/ppermute | solution.py:235
  72.2 43.3 %collective-permute-start.6 = (bf16[16,128,128]{2,1,0:T(8,128)(2,1)S(1)}, bf16[16,128,128]{2,1,0:T(8,128)(2,1)}, u32[]{:S(2)}, u32[]{:S(2)}) collective-permute-start(bf16[16,128,128]{2,1,0:T(8,128)(2,1)S(1)} %pad_maximum_fusion.refs_0_), channel_id=1, source_target_pairs={{0,4},{2,6},{4,0},{6,2},{1,5},{3,7},{5,1},{7,3},{8,12},{10,14},{12... | collective-permute-start | bytes 1572872 | tf_op jit(solution)/shard_map/ppermute | solution.py:235
  74.6 40.9 %collective-permute-start.5 = (bf16[16,128,128]{2,1,0:T(8,128)(2,1)S(1)}, bf16[16,128,128]{2,1,0:T(8,128)(2,1)}, u32[]{:S(2)}, u32[]{:S(2)}) collective-permute-start(bf16[16,128,128]{2,1,0:T(8,128)(2,1)S(1)} %pad_maximum_fusion.refs_0_), channel_id=1, source_target_pairs={{0,2},{2,4},{4,6},{6,0},{1,3},{3,5},{5,7},{7,1},{8,10},{10,12},{12... | collective-permute-start | bytes 1572872 | tf_op jit(solution)/shard_map/ppermute | solution.py:235
  77.2 16.8 %collective-permute-start.4 = (bf16[64,128]{1,0:T(8,128)(2,1)S(1)}, bf16[64,128]{1,0:T(8,128)(2,1)S(1)}, u32[]{:S(2)}, u32[]{:S(2)}) collective-permute-start(bf16[64,128]{1,0:T(8,128)(2,1)S(1)} %get-tuple-element.23), channel_id=1, source_target_pairs={{0,6},{2,0},{4,2},{6,4},{1,7},{3,1},{5,3},{7,5},{8,14},{10,8},{12,... | collective-permute-start | bytes 49160 | tf_op jit(solution)/shard_map/ppermute | solution.py:235
  94.0 6.9 %collective-permute-start.2 = (bf16[64,128]{1,0:T(8,128)(2,1)S(1)}, bf16[64,128]{1,0:T(8,128)(2,1)S(1)}, u32[]{:S(2)}, u32[]{:S(2)}) collective-permute-start(bf16[64,128]{1,0:T(8,128)(2,1)S(1)} %get-tuple-element.25), channel_id=1, source_target_pairs={{0,2},{2,4},{4,6},{6,0},{1,3},{3,5},{5,7},{7,1},{8,10},{10,12},{12... | collective-permute-start | bytes 49160 | tf_op jit(solution)/shard_map/ppermute | solution.py:235
  100.9 6.0 %collective-permute-start.3 = (bf16[64,128]{1,0:T(8,128)(2,1)S(1)}, bf16[64,128]{1,0:T(8,128)(2,1)S(1)}, u32[]{:S(2)}, u32[]{:S(2)}) collective-permute-start(bf16[64,128]{1,0:T(8,128)(2,1)S(1)} %get-tuple-element.26), channel_id=1, source_target_pairs={{0,4},{2,6},{4,0},{6,2},{1,5},{3,7},{5,1},{7,3},{8,12},{10,14},{12... | collective-permute-start | bytes 49160 | tf_op jit(solution)/shard_map/ppermute | solution.py:235
  111.2 13.8 %copy-start.5 = (bf16[128,256]{1,0:T(8,128)(2,1)S(1)}, bf16[128,256]{1,0:T(8,128)(2,1)}, u32[]{:S(2)}) copy-start(bf16[128,256]{1,0:T(8,128)(2,1)} %get-tuple-element.14.back_ref) | copy-start | bytes 196612
  111.2 13.8 %all-to-all-start.1 = ((bf16[8,32,128]{2,1,0:T(8,128)(2,1)}), bf16[8,32,128]{2,1,0:T(8,128)(2,1)S(1)}, u32[]{:S(2)}, u32[]{:S(2)}) async-start(bf16[8,32,128]{2,1,0:T(8,128)(2,1)} %attend.1), calls=%async_computation.1 | async-start | bytes 131072 | tf_op jit(solution)/shard_map/all_to_all | solution.py:307
  114.7 0.8 copy-start.3
  115.5 1.0 copy-start.2
  116.6 1.0 copy-start.4
  118.9 13.8 %collective-permute-start.8 = (bf16[64,128,128]{2,1,0:T(8,128)(2,1)S(1)}, bf16[64,128,128]{2,1,0:T(8,128)(2,1)}, u32[]{:S(2)}, u32[]{:S(2)}) collective-permute-start(bf16[64,128,128]{2,1,0:T(8,128)(2,1)S(1)} %join.1.refs_0_), channel_id=1, source_target_pairs={{0,8},{8,0},{1,9},{9,1},{2,10},{10,2},{3,11},{11,3},{4,12},{12,4},... | collective-permute-start | bytes 6291464 | tf_op jit(solution)/shard_map/ppermute | solution.py:235
  126.9 1.0 copy-start
  127.9 33.0 %all-to-all-start.2 = ((bf16[32,128,128]{2,1,0:T(8,128)(2,1)}), bf16[32,128,128]{2,1,0:T(8,128)(2,1)}, u32[]{:S(2)}, u32[]{:S(2)}) async-start(bf16[32,128,128]{2,1,0:T(8,128)(2,1)} %copy-done), calls=%async_computation.2 | async-start | bytes 2097152 | tf_op jit(solution)/shard_map/all_to_all | solution.py:317
  165.4 4.8 %collective-permute-start.9 = (bf16[256,128]{1,0:T(8,128)(2,1)S(1)}, bf16[256,128]{1,0:T(8,128)(2,1)S(1)}, u32[]{:S(2)}, u32[]{:S(2)}) collective-permute-start(bf16[256,128]{1,0:T(8,128)(2,1)S(1)} %get-tuple-element.22), channel_id=1, source_target_pairs={{0,8},{8,0},{1,9},{9,1},{2,10},{10,2},{3,11},{11,3},{4,12},{12,4},... | collective-permute-start | bytes 196616 | tf_op jit(solution)/shard_map/ppermute | solution.py:235
